TPU v7x, 512 devices: a whole 4x4x16 slice. The times are simulated.
512 devices in a mesh: edp: 32 (over z_hi, y, core), etp: 16 (over z_lo, x).
Axes of the slice: x: 4, y: 4, z: 16 (z_hi: 4, z_lo: 4; z = z_hi * 4 + z_lo), core: 2. Of those that a mesh axis runs over, the one named last changes fastest.
Arguments:
- tokens: bfloat16 [16384, 3072], P('edp'), may hold values from -6 to 6
- expert_ids: int32 [16384, 2], P('edp'), may hold values from 0 to 7, as said below
- route_weight: float32 [16384, 2], P('edp'), may hold values from 0.2 to 1
- index_list: int32 [32, 256], P('edp'), may hold values from 0 to 512, as said below
- gate_weight: bfloat16 [3072, 8192], P('edp', 'etp'), may hold values from -0.109375 to 0.109375
- up_weight: bfloat16 [3072, 8192], P('edp', 'etp'), may hold values from -0.109375 to 0.109375
- down_weight: bfloat16 [8192, 3072], P('etp', 'edp'), may hold values from -0.0625 to 0.0625
Outputs:
- expert_out: bfloat16 [16384, 3072], P(('edp', 'etp'))
Inputs may be any that keep to these rules, and one draw needn't show every extreme that they name: `index_list`: row b lists, increasing, the positions within block b of the tokens that name expert 0, then 512 in the remaining slots; in every draw some block is full. `expert_ids`: each token names two different experts; a token names expert 0 exactly when its position stands in its block's row of index_list.
All inputs are finite; a program needn't handle non-finite values.
Results may differ from a plain program's by a relative error of at most 0.018.
Values may be sent and summed in bfloat16 or wider, within the bound.
No kernel may reach another device: no remote copies, remote signals or barrier semaphores. Data moves between devices by JAX's collectives and lax.ppermute only.
A program may use at most 64 MiB of HBM per device.

v0:
```python
import jax
import jax.numpy as jnp
from jax import lax
from jax.experimental import pallas as pl
from jax.experimental.pallas import tpu as pltpu
from jax.sharding import Mesh, PartitionSpec as P


BF = jnp.bfloat16
F32 = jnp.float32
STREAMS = 2


def vm():
    return pl.BlockSpec(memory_space=pltpu.VMEM)


def sm():
    return pl.BlockSpec(memory_space=pltpu.SMEM)


def call(body, out, ins, scratch=(), flops=0, byts=0):
    return pl.pallas_call(
        body,
        out_shape=out,
        in_specs=ins,
        out_specs=vm(),
        scratch_shapes=scratch,
        cost_estimate=pl.CostEstimate(flops=flops, transcendentals=0, bytes_accessed=byts),
        compiler_params=pltpu.CompilerParams(vmem_limit_bytes=40 * 1024 * 1024),
    )


def dot_nn(a, b):
    return lax.dot_general(a, b, (((1,), (0,)), ((), ())), preferred_element_type=F32)


def dot_nt(a, b):
    return lax.dot_general(a, b, (((1,), (1,)), ((), ())), preferred_element_type=F32)


def pick_body(idx_ref, tok_ref, out_ref):
    caps, rows = idx_ref.shape[0], tok_ref.shape[0]
    hot = (lax.broadcasted_iota(jnp.int32, (caps, rows), 1) == idx_ref[...]).astype(BF)
    width = tok_ref.shape[1] // out_ref.shape[0]
    pad = jnp.zeros((caps, out_ref.shape[2] - width), BF)
    for m in range(out_ref.shape[0]):
        out_ref[m, :, :width] = dot_nn(hot, tok_ref[:, m * width : (m + 1) * width]).astype(BF)
        out_ref[m, :, width:] = pad


def hidden_body(ord_ref, own_ref, mate_ref, first_ref, second_ref, out_ref):
    caps, width = own_ref.shape[1], 192
    half = first_ref.shape[0] // width
    core = ord_ref[16]
    for src, place in ((own_ref, core), (mate_ref, 1 - core)):
        acc = None
        for k in range(2 * half):
            wref = first_ref if k < half else second_ref
            lo = (k % half) * width
            part = dot_nn(src[ord_ref[k], :, :width], wref[lo : lo + width, :])
            acc = part if acc is None else acc + part
        cols = []
        for s in range(acc.shape[1] // 256):
            gate = acc[:, 256 * s : 256 * s + 128]
            up = acc[:, 256 * s + 128 : 256 * s + 256]
            cols.append((gate / (1.0 + jnp.exp(-gate)) * up).astype(BF))
        res = cols[0] if len(cols) == 1 else jnp.concatenate(cols, axis=1)
        out_ref[pl.ds(pl.multiple_of(place * caps, caps), caps), :] = res


def down_body(ord_ref, idx_ref, first_ref, second_ref, *rest):
    hid_refs, out_ref, scr = rest[:-2], rest[-2], rest[-1]
    caps = idx_ref.shape[1]
    rows = 512
    unit = 24
    groups = hid_refs[0].shape[0]
    for n, wref in enumerate((first_ref, second_ref)):
        acc = None
        for g in range(groups):
            core, x = g // 4, g % 4
            hid = [h[g] for h in hid_refs]
            hid = hid[0] if len(hid) == 1 else jnp.concatenate(hid, axis=1)
            lo = 512 * x + 256 * core
            part = dot_nt(wref[:, lo : lo + 256], hid)
            acc = part if acc is None else acc + part
        half = wref.shape[0] // unit
        for k in range(half):
            m = ord_ref[n * half + k]
            scr[pl.ds(pl.multiple_of(m * unit, 8), unit), :] = acc[k * unit : (k + 1) * unit, :]
    for b in range(2):
        hot = (lax.broadcasted_iota(jnp.int32, (rows, caps), 0) == idx_ref[b : b + 1, :]).astype(BF)
        dense = dot_nt(scr[:, b * caps : (b + 1) * caps].astype(BF), hot).astype(BF)
        for q in range(4):
            out_ref[q, :, b * 128 : (b + 1) * 128] = dense[:, q * 128 : (q + 1) * 128]


def quarter_body(in_ref, out_ref):
    for x in range(4):
        out_ref[:, 512 * x : 512 * (x + 1)] = in_ref[24 * x : 24 * (x + 1), :]


def total_body(in_ref, out_ref):
    acc = in_ref[0].astype(F32)
    for q in range(1, 4):
        acc = acc + in_ref[q].astype(F32)
    out_ref[...] = acc.T.astype(BF)


def place_body(in_ref, scale_ref, out_ref, scr):
    unit = 24
    for g in range(8):
        turned = in_ref[g].astype(F32).T
        core, x = g // 4, g % 4
        for m in range(16):
            lo = 192 * m + 96 * core + unit * x
            scr[lo : lo + unit, :] = turned[m * unit : (m + 1) * unit, :]
    for n in range(6):
        out_ref[:, n * 512 : (n + 1) * 512] = (scr[n * 512 : (n + 1) * 512, :].T * scale_ref[...]).astype(BF)


def pairs(step):
    flips = ((1, 3), (3, 1))
    return [(2 * i + c, 2 * (i ^ flips[c][step]) + c) for i in range(4) for c in range(2)]


def join_body(a_ref, b_ref, out_ref):
    rows = a_ref.shape[0]
    out_ref[:rows, :] = a_ref[...]
    out_ref[rows:, :] = b_ref[...]


def join(a, b):
    out = jax.ShapeDtypeStruct((a.shape[0] + b.shape[0], a.shape[1]), BF)
    return call(join_body, out, [vm(), vm()])(a, b)


def meet(value, axis, step):
    return lax.ppermute(value, (axis, "c"), pairs(step))


def gather16(value):
    near = meet(value, "zh", 0)
    both = join(value, near)
    far = meet(both, "zh", 1)
    four = join(both, far)
    near = meet(four, "y", 0)
    both = join(four, near)
    return both, meet(both, "y", 1)


def shards(tokens, expert_ids, route_weight, index_list, gate_weight, up_weight, down_weight):
    zh, y, c, zl, x = (lax.axis_index(n) for n in ("zh", "y", "c", "zl", "x"))
    caps = index_list.shape[1]

    cut = lambda w, n: w[:, 128 * n : 128 * n + 128]
    mine = [
        jnp.concatenate([cut(w, 2 * h + s) for s in range(2) for w in (gate_weight, up_weight)], axis=1)
        for h in range(2)
    ]
    both_rows = lax.all_to_all(jnp.concatenate(mine, axis=0), "c", 0, 0, tiled=True)

    turned = down_weight.T
    quarter = lax.all_to_all(turned, "x", 0, 0, tiled=True)
    quarter = call(quarter_body, jax.ShapeDtypeStruct((24, 2048), BF), [vm()])(quarter)

    flip = jnp.where(c == 0, jnp.array([0, 1, 3, 2]), jnp.array([0, 3, 1, 2])).astype(jnp.int32)
    order = ((zh ^ flip)[None, :] * 4 + (y ^ flip)[:, None]).reshape(16)
    order = jnp.concatenate([order, c.reshape(1)]).astype(jnp.int32)

    rows = call(
        pick_body, jax.ShapeDtypeStruct((16, caps, 256), BF), [vm(), vm()], flops=2 * 256 * 512 * 3072
    )(index_list.reshape(caps, 1), tokens)
    swap = [(0, 1), (1, 0)]
    rows_mate = lax.ppermute(rows, "c", swap)
    index_mate = lax.ppermute(index_list, "c", swap)
    index_both = jnp.where(
        c == 0,
        jnp.concatenate([index_list, index_mate], axis=0),
        jnp.concatenate([index_mate, index_list], axis=0),
    )

    width = 512 // STREAMS
    ups = [gather16(both_rows[:, n * width : (n + 1) * width]) for n in range(STREAMS)]
    down_first, down_second = gather16(quarter)

    hids = []
    for first, second in ups:
      h = call(
          hidden_body,
          jax.ShapeDtypeStruct((2 * caps, width // 2), BF),
          [sm(), vm(), vm(), vm(), vm()],
          flops=2 * 512 * 3072 * width,
      )(order, rows, rows_mate, first, second)
      wide = jnp.broadcast_to(h[None], (8,) + h.shape)
      hids.append(lax.all_to_all(wide, ("c", "x"), 0, 0, tiled=True))

    parts = call(
        down_body,
        jax.ShapeDtypeStruct((4, 384, 256), BF),
        [sm(), vm(), vm(), vm()] + [vm()] * len(hids),
        scratch=[pltpu.VMEM((384, 512), F32)],
        flops=2 * 512 * 384 * 2048,
    )(order, index_both, down_first, down_second, *hids)
    parts = lax.all_to_all(parts, "zl", 0, 0, tiled=True)
    total = call(total_body, jax.ShapeDtypeStruct((256, 384), BF), [vm()])(parts)
    owned = lax.all_to_all(total.reshape(8, 32, 384), ("c", "x"), 0, 0, tiled=True)

    start = (zl * 4 + x) * 32
    ids = lax.dynamic_slice_in_dim(expert_ids, start, 32, 0)
    weights = lax.dynamic_slice_in_dim(route_weight, start, 32, 0)
    scale = jnp.sum(jnp.where(ids == 0, weights, jnp.zeros_like(weights)), axis=1, keepdims=True)
    return call(
        place_body, jax.ShapeDtypeStruct((32, 3072), BF), [vm(), vm()], scratch=[pltpu.VMEM((3072, 32), F32)]
    )(owned, scale)


def solution(mesh):
    fine = Mesh(mesh.devices.reshape(4, 4, 2, 4, 4), ("zh", "y", "c", "zl", "x"))
    edp, etp = ("zh", "y", "c"), ("zl", "x")
    in_specs = (P(edp, None), P(edp, None), P(edp, None), P(edp, None), P(edp, etp), P(edp, etp), P(etp, edp))

    return jax.shard_map(shards, mesh=fine, in_specs=in_specs, out_specs=P(edp + etp, None), check_vma=False)
```

profile of v0, /device:TPU:1, one launch (start us, length us, event | category | flops | bytes accessed | tf_op | source)
XLA Modules:
  0.0 205.1 jit_solution(17237115746169253015)
XLA Ops:
  4.1 8.7 %collective-permute-start.5 = (bf16[16,256,256]{2,1,0:T(8,128)(2,1)S(1)}, bf16[16,256,256]{2,1,0:T(8,128)(2,1)}, u32[]{:S(2)}, u32[]{:S(2)}) collective-permute-start(bf16[16,256,256]{2,1,0:T(8,128)(2,1)S(1)} %shard_map.95.own_ref), channel_id=1, source_target_pairs={{0,16},{16,0},{1,17},{17,1},{2,18},{18,2},{3,19},{19,3},{4,20},{20... | collective-permute-start | bytes 6291464 | tf_op jit(solution)/shard_map/ppermute | solution.py:175
  12.9 3.8 %all_to_all.43 = bf16[2,96,512]{2,1,0:T(8,128)(2,1)S(1)} all-to-all(bf16[2,96,512]{2,1,0:T(8,128)(2,1)S(1)} %bitcast.10), channel_id=1, replica_groups=mesh['zh'=4,'y'=4,'c'=2,'zl'=4,'x'=4] {'c'}, dimensions={0} | all-to-all | bytes 393216 | tf_op jit(solution)/shard_map/all_to_all | solution.py:161
  16.7 7.1 %collective-permute-start.10 = (bf16[192,256]{1,0:T(8,128)(2,1)S(1)}, bf16[192,256]{1,0:T(8,128)(2,1)S(1)}, u32[]{:S(2)}, u32[]{:S(2)}) collective-permute-start(bf16[192,256]{1,0:T(8,128)(2,1)S(1)} %get-tuple-element.5.a_ref), channel_id=1, source_target_pairs={{0,128},{16,400},{128,0},{144,272},{256,384},{272,144},{384,256},{... | collective-permute-start | bytes 294920 | tf_op jit(solution)/shard_map/ppermute | solution.py:139
  23.8 3.2 %collective-permute-done.10.b_ref = bf16[192,256]{1,0:T(8,128)(2,1)S(1)} collective-permute-done((bf16[192,256]{1,0:T(8,128)(2,1)S(1)}, bf16[192,256]{1,0:T(8,128)(2,1)S(1)}, u32[]{:S(2)}, u32[]{:S(2)}) %collective-permute-start.10) | collective-permute-done | bytes 98336 | tf_op jit(solution)/shard_map/ppermute | solution.py:139
  27.0 7.2 %collective-permute-start.11 = (bf16[384,256]{1,0:T(8,128)(2,1)S(1)}, bf16[384,256]{1,0:T(8,128)(2,1)S(1)}, u32[]{:S(2)}, u32[]{:S(2)}) collective-permute-start(bf16[384,256]{1,0:T(8,128)(2,1)S(1)} %shard_map.100.a_ref), channel_id=1, source_target_pairs={{0,384},{16,144},{128,256},{144,16},{256,128},{272,400},{384,0},{4... | collective-permute-start | bytes 589832 | tf_op jit(solution)/shard_map/ppermute | solution.py:139
  34.2 7.2 %collective-permute-done.11.b_ref = bf16[384,256]{1,0:T(8,128)(2,1)S(1)} collective-permute-done((bf16[384,256]{1,0:T(8,128)(2,1)S(1)}, bf16[384,256]{1,0:T(8,128)(2,1)S(1)}, u32[]{:S(2)}, u32[]{:S(2)}) %collective-permute-start.11) | collective-permute-done | bytes 196640 | tf_op jit(solution)/shard_map/ppermute | solution.py:139
  41.5 8.2 %collective-permute-start.12 = (bf16[768,256]{1,0:T(8,128)(2,1)S(1)}, bf16[768,256]{1,0:T(8,128)(2,1)S(1)}, u32[]{:S(2)}, u32[]{:S(2)}) collective-permute-start(bf16[768,256]{1,0:T(8,128)(2,1)S(1)} %shard_map.101.a_ref), channel_id=1, source_target_pairs={{0,32},{16,112},{32,0},{48,80},{64,96},{80,48},{96,64},{112,16},{1... | collective-permute-start | bytes 1179656 | tf_op jit(solution)/shard_map/ppermute | solution.py:139
  49.6 5.2 %collective-permute-done.12.b_ref = bf16[768,256]{1,0:T(8,128)(2,1)S(1)} collective-permute-done((bf16[768,256]{1,0:T(8,128)(2,1)S(1)}, bf16[768,256]{1,0:T(8,128)(2,1)S(1)}, u32[]{:S(2)}, u32[]{:S(2)}) %collective-permute-start.12) | collective-permute-done | bytes 393248 | tf_op jit(solution)/shard_map/ppermute | solution.py:139
  54.8 2.2 %collective-permute-start.13 = (bf16[1536,256]{1,0:T(8,128)(2,1)S(1)}, bf16[1536,256]{1,0:T(8,128)(2,1)}, u32[]{:S(2)}, u32[]{:S(2)}) collective-permute-start(bf16[1536,256]{1,0:T(8,128)(2,1)S(1)} %shard_map.102.first_ref), channel_id=1, source_target_pairs={{0,96},{16,48},{32,64},{48,16},{64,32},{80,112},{96,0},{112,80},{1... | collective-permute-start | bytes 2359304 | tf_op jit(solution)/shard_map/ppermute | solution.py:139
  57.1 6.4 %collective-permute-start.6 = (bf16[192,256]{1,0:T(8,128)(2,1)S(1)}, bf16[192,256]{1,0:T(8,128)(2,1)S(1)}, u32[]{:S(2)}, u32[]{:S(2)}) collective-permute-start(bf16[192,256]{1,0:T(8,128)(2,1)S(1)} %get-tuple-element.6.a_ref), channel_id=1, source_target_pairs={{0,128},{16,400},{128,0},{144,272},{256,384},{272,144},{384,256},{... | collective-permute-start | bytes 294920 | tf_op jit(solution)/shard_map/ppermute | solution.py:139
  63.5 4.0 %all-to-all-start = ((bf16[4,24,512]{2,1,0:T(8,128)(2,1)}), bf16[4,24,512]{2,1,0:T(8,128)(2,1)}, u32[]{:S(2)}, u32[]{:S(2)}) async-start(bf16[4,24,512]{2,1,0:T(8,128)(2,1)} %bitcast.2), calls=%async_computation | async-start | bytes 196608 | tf_op jit(solution)/shard_map/all_to_all | solution.py:164
  67.6 3.2 %collective-permute-start.7 = (bf16[384,256]{1,0:T(8,128)(2,1)S(1)}, bf16[384,256]{1,0:T(8,128)(2,1)S(1)}, u32[]{:S(2)}, u32[]{:S(2)}) collective-permute-start(bf16[384,256]{1,0:T(8,128)(2,1)S(1)} %shard_map.96.a_ref), channel_id=1, source_target_pairs={{0,384},{16,144},{128,256},{144,16},{256,128},{272,400},{384,0},{4... | collective-permute-start | bytes 589832 | tf_op jit(solution)/shard_map/ppermute | solution.py:139
  70.8 12.9 %collective-permute-done.7.b_ref = bf16[384,256]{1,0:T(8,128)(2,1)S(1)} collective-permute-done((bf16[384,256]{1,0:T(8,128)(2,1)S(1)}, bf16[384,256]{1,0:T(8,128)(2,1)S(1)}, u32[]{:S(2)}, u32[]{:S(2)}) %collective-permute-start.7) | collective-permute-done | bytes 196640 | tf_op jit(solution)/shard_map/ppermute | solution.py:139
  83.8 3.9 %collective-permute-start.8 = (bf16[768,256]{1,0:T(8,128)(2,1)S(1)}, bf16[768,256]{1,0:T(8,128)(2,1)}, u32[]{:S(2)}, u32[]{:S(2)}) collective-permute-start(bf16[768,256]{1,0:T(8,128)(2,1)S(1)} %shard_map.97.a_ref), channel_id=1, source_target_pairs={{0,32},{16,112},{32,0},{48,80},{64,96},{80,48},{96,64},{112,16},{1... | collective-permute-start | bytes 1179656 | tf_op jit(solution)/shard_map/ppermute | solution.py:139
  87.9 3.0 %shard_map.103 = bf16[512,128]{1,0:T(8,128)(2,1)S(1)} custom-call(s32[17]{0:T(128)S(1)} %pad_add_fusion.ord_ref, bf16[16,256,256]{2,1,0:T(8,128)(2,1)S(1)} %shard_map.95.own_ref, bf16[16,256,256]{2,1,0:T(8,128)(2,1)} %collective-permute-done.5.mate_ref, bf16[1536,256]{1,0:T(8,128)(2,1)S(1)} %shard_map.102.first_ref, ...), custom_call_target="tpu_custom_call" | custom-call | flops 805306368 | tf_op jit(solution)/shard_map/pallas_call | solution.py:189
  92.1 7.8 %all-to-all-start.3 = ((bf16[8,512,128]{2,1,0:T(8,128)(2,1)}), bf16[8,512,128]{2,1,0:T(8,128)(2,1)S(1)}, u32[]{:S(2)}, u32[]{:S(2)}) async-start(bf16[8,512,128]{2,1,0:T(8,128)(2,1)} %broadcast_in_dim.9), calls=%async_computation.3 | async-start | bytes 2097152 | tf_op jit(solution)/shard_map/all_to_all | solution.py:196
  101.0 3.6 %collective-permute-start.9 = (bf16[1536,256]{1,0:T(8,128)(2,1)S(1)}, bf16[1536,256]{1,0:T(8,128)(2,1)S(1)}, u32[]{:S(2)}, u32[]{:S(2)}) collective-permute-start(bf16[1536,256]{1,0:T(8,128)(2,1)S(1)} %shard_map.98.first_ref), channel_id=1, source_target_pairs={{0,96},{16,48},{32,64},{48,16},{64,32},{80,112},{96,0},{112,80},{1... | collective-permute-start | bytes 2359304 | tf_op jit(solution)/shard_map/ppermute | solution.py:139
  105.5 1.9 collective-permute-start.1
  107.4 7.6 %collective-permute-done.1.b_ref = bf16[24,2048]{1,0:T(8,128)(2,1)S(1)} collective-permute-done((bf16[24,2048]{1,0:T(8,128)(2,1)S(1)}, bf16[24,2048]{1,0:T(8,128)(2,1)S(1)}, u32[]{:S(2)}, u32[]{:S(2)}) %collective-permute-start.1) | collective-permute-done | bytes 98336 | tf_op jit(solution)/shard_map/ppermute | solution.py:139
  115.1 8.0 %collective-permute-start.2 = (bf16[48,2048]{1,0:T(8,128)(2,1)S(1)}, bf16[48,2048]{1,0:T(8,128)(2,1)S(1)}, u32[]{:S(2)}, u32[]{:S(2)}) collective-permute-start(bf16[48,2048]{1,0:T(8,128)(2,1)S(1)} %shard_map.92.a_ref), channel_id=1, source_target_pairs={{0,384},{16,144},{128,256},{144,16},{256,128},{272,400},{384,0},{4... | collective-permute-start | bytes 589832 | tf_op jit(solution)/shard_map/ppermute | solution.py:139
  123.1 7.8 %collective-permute-done.2.b_ref = bf16[48,2048]{1,0:T(8,128)(2,1)S(1)} collective-permute-done((bf16[48,2048]{1,0:T(8,128)(2,1)S(1)}, bf16[48,2048]{1,0:T(8,128)(2,1)S(1)}, u32[]{:S(2)}, u32[]{:S(2)}) %collective-permute-start.2) | collective-permute-done | bytes 196640 | tf_op jit(solution)/shard_map/ppermute | solution.py:139
  131.0 4.0 %collective-permute-start.3 = (bf16[96,2048]{1,0:T(8,128)(2,1)S(1)}, bf16[96,2048]{1,0:T(8,128)(2,1)}, u32[]{:S(2)}, u32[]{:S(2)}) collective-permute-start(bf16[96,2048]{1,0:T(8,128)(2,1)S(1)} %shard_map.93.a_ref), channel_id=1, source_target_pairs={{0,32},{16,112},{32,0},{48,80},{64,96},{80,48},{96,64},{112,16},{1... | collective-permute-start | bytes 1179656 | tf_op jit(solution)/shard_map/ppermute | solution.py:139
  135.0 2.9 %shard_map.99 = bf16[512,128]{1,0:T(8,128)(2,1)S(1)} custom-call(s32[17]{0:T(128)S(1)} %pad_add_fusion.ord_ref, bf16[16,256,256]{2,1,0:T(8,128)(2,1)S(1)} %shard_map.95.own_ref, bf16[16,256,256]{2,1,0:T(8,128)(2,1)} %collective-permute-done.5.mate_ref, bf16[1536,256]{1,0:T(8,128)(2,1)S(1)} %shard_map.98.first_ref, ...), custom_call_target="tpu_custom_call" | custom-call | flops 805306368 | tf_op jit(solution)/shard_map/pallas_call | solution.py:189
  138.5 2.0 broadcast_in_dim.8
  140.5 6.2 %all-to-all-start.2 = ((bf16[8,512,128]{2,1,0:T(8,128)(2,1)}), bf16[8,512,128]{2,1,0:T(8,128)(2,1)S(1)}, u32[]{:S(2)}, u32[]{:S(2)}) async-start(bf16[8,512,128]{2,1,0:T(8,128)(2,1)} %broadcast_in_dim.8), calls=%async_computation.2 | async-start | bytes 2097152 | tf_op jit(solution)/shard_map/all_to_all | solution.py:196
  147.8 3.6 %collective-permute-start.4 = (bf16[192,2048]{1,0:T(8,128)(2,1)S(1)}, bf16[192,2048]{1,0:T(8,128)(2,1)S(1)}, u32[]{:S(2)}, u32[]{:S(2)}) collective-permute-start(bf16[192,2048]{1,0:T(8,128)(2,1)S(1)} %shard_map.94.first_ref), channel_id=1, source_target_pairs={{0,96},{16,48},{32,64},{48,16},{64,32},{80,112},{96,0},{112,80},{1... | collective-permute-start | bytes 2359304 | tf_op jit(solution)/shard_map/ppermute | solution.py:139
  151.4 3.1 %collective-permute-start = (s32[1,256]{1,0:T(1,128)S(1)}, s32[1,256]{1,0:T(1,128)S(1)}, u32[]{:S(2)}, u32[]{:S(2)}) collective-permute-start(s32[1,256]{1,0:T(1,128)S(1)} %copy-done.6), channel_id=1, source_target_pairs={{0,16},{16,0},{1,17},{17,1},{2,18},{18,2},{3,19},{19,3},{4,20},{20... | collective-permute-start | bytes 3080 | tf_op jit(solution)/shard_map/ppermute | solution.py:176
  155.4 5.7 %collective-permute-done.4.second_ref = bf16[192,2048]{1,0:T(8,128)(2,1)S(1)} collective-permute-done((bf16[192,2048]{1,0:T(8,128)(2,1)S(1)}, bf16[192,2048]{1,0:T(8,128)(2,1)S(1)}, u32[]{:S(2)}, u32[]{:S(2)}) %collective-permute-start.4) | collective-permute-done | bytes 786464 | tf_op jit(solution)/shard_map/ppermute | solution.py:139
  163.1 2.4 %shard_map.104 = bf16[4,384,256]{2,1,0:T(8,128)(2,1)S(1)} custom-call(s32[17]{0:T(128)S(1)} %pad_add_fusion.ord_ref, s32[2,256]{1,0:T(2,128)S(1)} %add_select_fusion.idx_ref, bf16[192,2048]{1,0:T(8,128)(2,1)S(1)} %shard_map.94.first_ref, bf16[192,2048]{1,0:T(8,128)(2,1)S(1)} %copy-done.2, bf16[8,512,128]{2,1,0:T(8,128)(2,1)S(1)} %all-to-all-done.2.rest_0_, ...), custom_call_target="tpu_custom_call" | custom-call | flops 805306368 | tf_op jit(solution)/shard_map/pallas_call | solution.py:198
  165.5 25.2 %all_to_all.44.in_ref = bf16[4,384,256]{2,1,0:T(8,128)(2,1)S(1)} all-to-all(bf16[4,384,256]{2,1,0:T(8,128)(2,1)S(1)} %shard_map.104), channel_id=1, replica_groups=mesh['zh'=4,'y'=4,'c'=2,'zl'=4,'x'=4] {'zl'}, dimensions={0} | all-to-all | bytes 1572864 | tf_op jit(solution)/shard_map/all_to_all | solution.py:205
  191.6 6.3 %all-to-all-start.5 = ((bf16[8,32,384]{2,1,0:T(8,128)(2,1)}), bf16[8,32,384]{2,1,0:T(8,128)(2,1)S(1)}, u32[]{:S(2)}, u32[]{:S(2)}) async-start(bf16[8,32,384]{2,1,0:T(8,128)(2,1)} %bitcast.7), calls=%async_computation.5 | async-start | bytes 393216 | tf_op jit(solution)/shard_map/all_to_all | solution.py:207
  198.8 5.0 %all-to-all-done.5.in_ref = bf16[8,32,384]{2,1,0:T(8,128)(2,1)S(1)} async-done(((bf16[8,32,384]{2,1,0:T(8,128)(2,1)}), bf16[8,32,384]{2,1,0:T(8,128)(2,1)S(1)}, u32[]{:S(2)}, u32[]{:S(2)}) %all-to-all-start.5) | async-done | bytes 196640 | tf_op jit(solution)/shard_map/all_to_all | solution.py:207
  (53 shorter events, 15.3 us)
Async XLA Ops:
  0.8 1.9 copy-start
  2.7 10.1 %copy-start.4 = (bf16[96,512]{1,0:T(8,128)(2,1)S(1)}, bf16[96,512]{1,0:T(8,128)(2,1)}, u32[]{:S(2)}) copy-start(bf16[96,512]{1,0:T(8,128)(2,1)} %param.13) | copy-start | bytes 294916
  2.7 10.1 %copy-start.5 = (bf16[96,512]{1,0:T(8,128)(2,1)S(1)}, bf16[96,512]{1,0:T(8,128)(2,1)}, u32[]{:S(2)}) copy-start(bf16[96,512]{1,0:T(8,128)(2,1)} %param.14) | copy-start | bytes 294916
  4.1 83.8 %collective-permute-start.5 = (bf16[16,256,256]{2,1,0:T(8,128)(2,1)S(1)}, bf16[16,256,256]{2,1,0:T(8,128)(2,1)}, u32[]{:S(2)}, u32[]{:S(2)}) collective-permute-start(bf16[16,256,256]{2,1,0:T(8,128)(2,1)S(1)} %shard_map.95.own_ref), channel_id=1, source_target_pairs={{0,16},{16,0},{1,17},{17,1},{2,18},{18,2},{3,19},{19,3},{4,20},{20... | collective-permute-start | bytes 6291464 | tf_op jit(solution)/shard_map/ppermute | solution.py:175
  12.9 57.9 %copy-start.7 = (s32[4]{0:T(128)S(1)}, s32[4]{0:T(128)}, u32[]{:S(2)}) copy-start(s32[4]{0:T(128)} %constant.38.clone) | copy-start | bytes 52
  12.9 57.9 %copy-start.8 = (s32[4]{0:T(128)S(1)}, s32[4]{0:T(128)}, u32[]{:S(2)}) copy-start(s32[4]{0:T(128)} %constant.39.clone) | copy-start | bytes 52
  16.7 10.3 %collective-permute-start.10 = (bf16[192,256]{1,0:T(8,128)(2,1)S(1)}, bf16[192,256]{1,0:T(8,128)(2,1)S(1)}, u32[]{:S(2)}, u32[]{:S(2)}) collective-permute-start(bf16[192,256]{1,0:T(8,128)(2,1)S(1)} %get-tuple-element.5.a_ref), channel_id=1, source_target_pairs={{0,128},{16,400},{128,0},{144,272},{256,384},{272,144},{384,256},{... | collective-permute-start | bytes 294920 | tf_op jit(solution)/shard_map/ppermute | solution.py:139
  27.0 14.4 %collective-permute-start.11 = (bf16[384,256]{1,0:T(8,128)(2,1)S(1)}, bf16[384,256]{1,0:T(8,128)(2,1)S(1)}, u32[]{:S(2)}, u32[]{:S(2)}) collective-permute-start(bf16[384,256]{1,0:T(8,128)(2,1)S(1)} %shard_map.100.a_ref), channel_id=1, source_target_pairs={{0,384},{16,144},{128,256},{144,16},{256,128},{272,400},{384,0},{4... | collective-permute-start | bytes 589832 | tf_op jit(solution)/shard_map/ppermute | solution.py:139
  41.5 13.3 %collective-permute-start.12 = (bf16[768,256]{1,0:T(8,128)(2,1)S(1)}, bf16[768,256]{1,0:T(8,128)(2,1)S(1)}, u32[]{:S(2)}, u32[]{:S(2)}) collective-permute-start(bf16[768,256]{1,0:T(8,128)(2,1)S(1)} %shard_map.101.a_ref), channel_id=1, source_target_pairs={{0,32},{16,112},{32,0},{48,80},{64,96},{80,48},{96,64},{112,16},{1... | collective-permute-start | bytes 1179656 | tf_op jit(solution)/shard_map/ppermute | solution.py:139
  54.8 33.1 %collective-permute-start.13 = (bf16[1536,256]{1,0:T(8,128)(2,1)S(1)}, bf16[1536,256]{1,0:T(8,128)(2,1)}, u32[]{:S(2)}, u32[]{:S(2)}) collective-permute-start(bf16[1536,256]{1,0:T(8,128)(2,1)S(1)} %shard_map.102.first_ref), channel_id=1, source_target_pairs={{0,96},{16,48},{32,64},{48,16},{64,32},{80,112},{96,0},{112,80},{1... | collective-permute-start | bytes 2359304 | tf_op jit(solution)/shard_map/ppermute | solution.py:139
  57.1 10.5 %collective-permute-start.6 = (bf16[192,256]{1,0:T(8,128)(2,1)S(1)}, bf16[192,256]{1,0:T(8,128)(2,1)S(1)}, u32[]{:S(2)}, u32[]{:S(2)}) collective-permute-start(bf16[192,256]{1,0:T(8,128)(2,1)S(1)} %get-tuple-element.6.a_ref), channel_id=1, source_target_pairs={{0,128},{16,400},{128,0},{144,272},{256,384},{272,144},{384,256},{... | collective-permute-start | bytes 294920 | tf_op jit(solution)/shard_map/ppermute | solution.py:139
  63.5 27.5 %all-to-all-start = ((bf16[4,24,512]{2,1,0:T(8,128)(2,1)}), bf16[4,24,512]{2,1,0:T(8,128)(2,1)}, u32[]{:S(2)}, u32[]{:S(2)}) async-start(bf16[4,24,512]{2,1,0:T(8,128)(2,1)} %bitcast.2), calls=%async_computation | async-start | bytes 196608 | tf_op jit(solution)/shard_map/all_to_all | solution.py:164
  67.6 16.2 %collective-permute-start.7 = (bf16[384,256]{1,0:T(8,128)(2,1)S(1)}, bf16[384,256]{1,0:T(8,128)(2,1)S(1)}, u32[]{:S(2)}, u32[]{:S(2)}) collective-permute-start(bf16[384,256]{1,0:T(8,128)(2,1)S(1)} %shard_map.96.a_ref), channel_id=1, source_target_pairs={{0,384},{16,144},{128,256},{144,16},{256,128},{272,400},{384,0},{4... | collective-permute-start | bytes 589832 | tf_op jit(solution)/shard_map/ppermute | solution.py:139
  83.8 16.1 %collective-permute-start.8 = (bf16[768,256]{1,0:T(8,128)(2,1)S(1)}, bf16[768,256]{1,0:T(8,128)(2,1)}, u32[]{:S(2)}, u32[]{:S(2)}) collective-permute-start(bf16[768,256]{1,0:T(8,128)(2,1)S(1)} %shard_map.97.a_ref), channel_id=1, source_target_pairs={{0,32},{16,112},{32,0},{48,80},{64,96},{80,48},{96,64},{112,16},{1... | collective-permute-start | bytes 1179656 | tf_op jit(solution)/shard_map/ppermute | solution.py:139
  92.1 46.4 %all-to-all-start.3 = ((bf16[8,512,128]{2,1,0:T(8,128)(2,1)}), bf16[8,512,128]{2,1,0:T(8,128)(2,1)S(1)}, u32[]{:S(2)}, u32[]{:S(2)}) async-start(bf16[8,512,128]{2,1,0:T(8,128)(2,1)} %broadcast_in_dim.9), calls=%async_computation.3 | async-start | bytes 2097152 | tf_op jit(solution)/shard_map/all_to_all | solution.py:196
  101.0 34.0 %collective-permute-start.9 = (bf16[1536,256]{1,0:T(8,128)(2,1)S(1)}, bf16[1536,256]{1,0:T(8,128)(2,1)S(1)}, u32[]{:S(2)}, u32[]{:S(2)}) collective-permute-start(bf16[1536,256]{1,0:T(8,128)(2,1)S(1)} %shard_map.98.first_ref), channel_id=1, source_target_pairs={{0,96},{16,48},{32,64},{48,16},{64,32},{80,112},{96,0},{112,80},{1... | collective-permute-start | bytes 2359304 | tf_op jit(solution)/shard_map/ppermute | solution.py:139
  105.5 9.6 %collective-permute-start.1 = (bf16[24,2048]{1,0:T(8,128)(2,1)S(1)}, bf16[24,2048]{1,0:T(8,128)(2,1)S(1)}, u32[]{:S(2)}, u32[]{:S(2)}) collective-permute-start(bf16[24,2048]{1,0:T(8,128)(2,1)S(1)} %shard_map.91.a_ref), channel_id=1, source_target_pairs={{0,128},{16,400},{128,0},{144,272},{256,384},{272,144},{384,256},{... | collective-permute-start | bytes 294920 | tf_op jit(solution)/shard_map/ppermute | solution.py:139
  115.1 15.8 %collective-permute-start.2 = (bf16[48,2048]{1,0:T(8,128)(2,1)S(1)}, bf16[48,2048]{1,0:T(8,128)(2,1)S(1)}, u32[]{:S(2)}, u32[]{:S(2)}) collective-permute-start(bf16[48,2048]{1,0:T(8,128)(2,1)S(1)} %shard_map.92.a_ref), channel_id=1, source_target_pairs={{0,384},{16,144},{128,256},{144,16},{256,128},{272,400},{384,0},{4... | collective-permute-start | bytes 589832 | tf_op jit(solution)/shard_map/ppermute | solution.py:139
  131.0 15.8 %collective-permute-start.3 = (bf16[96,2048]{1,0:T(8,128)(2,1)S(1)}, bf16[96,2048]{1,0:T(8,128)(2,1)}, u32[]{:S(2)}, u32[]{:S(2)}) collective-permute-start(bf16[96,2048]{1,0:T(8,128)(2,1)S(1)} %shard_map.93.a_ref), channel_id=1, source_target_pairs={{0,32},{16,112},{32,0},{48,80},{64,96},{80,48},{96,64},{112,16},{1... | collective-permute-start | bytes 1179656 | tf_op jit(solution)/shard_map/ppermute | solution.py:139
  137.8 0.7 copy-start.3
  140.5 10.9 %copy-start.6 = (s32[1,256]{1,0:T(1,128)S(1)}, s32[1,256]{1,0:T(1,128)}, u32[]{:S(2)}) copy-start(s32[1,256]{1,0:T(1,128)} %param.12) | copy-start | bytes 3076
  140.5 21.4 %all-to-all-start.2 = ((bf16[8,512,128]{2,1,0:T(8,128)(2,1)}), bf16[8,512,128]{2,1,0:T(8,128)(2,1)S(1)}, u32[]{:S(2)}, u32[]{:S(2)}) async-start(bf16[8,512,128]{2,1,0:T(8,128)(2,1)} %broadcast_in_dim.8), calls=%async_computation.2 | async-start | bytes 2097152 | tf_op jit(solution)/shard_map/all_to_all | solution.py:196
  147.8 13.3 %collective-permute-start.4 = (bf16[192,2048]{1,0:T(8,128)(2,1)S(1)}, bf16[192,2048]{1,0:T(8,128)(2,1)S(1)}, u32[]{:S(2)}, u32[]{:S(2)}) collective-permute-start(bf16[192,2048]{1,0:T(8,128)(2,1)S(1)} %shard_map.94.first_ref), channel_id=1, source_target_pairs={{0,96},{16,48},{32,64},{48,16},{64,32},{80,112},{96,0},{112,80},{1... | collective-permute-start | bytes 2359304 | tf_op jit(solution)/shard_map/ppermute | solution.py:139
  151.4 4.0 %collective-permute-start = (s32[1,256]{1,0:T(1,128)S(1)}, s32[1,256]{1,0:T(1,128)S(1)}, u32[]{:S(2)}, u32[]{:S(2)}) collective-permute-start(s32[1,256]{1,0:T(1,128)S(1)} %copy-done.6), channel_id=1, source_target_pairs={{0,16},{16,0},{1,17},{17,1},{2,18},{18,2},{3,19},{19,3},{4,20},{20... | collective-permute-start | bytes 3080 | tf_op jit(solution)/shard_map/ppermute | solution.py:176
  161.1 0.9 copy-start.1
  162.0 1.1 copy-start.2
  191.6 12.1 %all-to-all-start.5 = ((bf16[8,32,384]{2,1,0:T(8,128)(2,1)}), bf16[8,32,384]{2,1,0:T(8,128)(2,1)S(1)}, u32[]{:S(2)}, u32[]{:S(2)}) async-start(bf16[8,32,384]{2,1,0:T(8,128)(2,1)} %bitcast.7), calls=%async_computation.5 | async-start | bytes 393216 | tf_op jit(solution)/shard_map/all_to_all | solution.py:207
where the time goes:
time: 206 us; the launch traced here: 205 us
  starting transfers between devices  95.6 us (46%)
  waiting for transfers between devices  55.4 us (27%)
  blocking collectives  29 us (14%)
  Pallas kernels  15.1 us (7%)
  local copies, waits for them, and re-layouts  8.77 us (4%)
    ppermute x12, starting transfers between devices, meet(): return lax.ppermute(value, (axis, 'c'), pairs(step))  59.4 us
    ppermute x12, waiting for transfers between devices, meet(): return lax.ppermute(value, (axis, 'c'), pairs(step))  49.6 us
    all_to_all x1, blocking collectives, shards(): parts = lax.all_to_all(parts, 'zl', 0, 0, tiled=True)  25.2 us
    all_to_all x2, starting transfers between devices, shards(): hids.append(lax.all_to_all(wide, ('c', 'x'), 0, 0, tiled=True))  14 us
    ppermute x1, starting transfers between devices, shards(): rows_mate = lax.ppermute(rows, 'c', swap)  8.75 us
    all_to_all x1, starting transfers between devices, shards(): lax.all_to_all(total.reshape(8, 32, 384), ('c', 'x'), 0, 0, tiled=True)  6.28 us
    pallas_call x2, Pallas kernels, shards(): call(hidden_body, jax.ShapeDtypeStruct((2 * caps, width // 2), BF), [sm()...  5.89 us
    all_to_all x1, waiting for transfers between devices, shards(): lax.all_to_all(total.reshape(8, 32, 384), ('c', 'x'), 0, 0, tiled=True)  4.95 us
  transfers between devices with their start and end apart: 18, of which 9 were waited for; matrix products, arithmetic and copies ran while one was open for 2% of the time, Pallas kernels for 4%

commit v1 on v0

v1 whole, which is shorter than its diff:
```python
import jax
import jax.numpy as jnp
from jax import lax
from jax.experimental import pallas as pl
from jax.experimental.pallas import tpu as pltpu
from jax.sharding import Mesh, PartitionSpec as P


BF = jnp.bfloat16
F32 = jnp.float32


def vm():
    return pl.BlockSpec(memory_space=pltpu.VMEM)


def sm():
    return pl.BlockSpec(memory_space=pltpu.SMEM)


def hb():
    return pl.BlockSpec(memory_space=pltpu.HBM)


def call(body, out, ins, scratch=(), flops=0, mib=16, to=vm):
    return pl.pallas_call(
        body,
        out_shape=out,
        in_specs=ins,
        out_specs=to(),
        scratch_shapes=scratch,
        cost_estimate=pl.CostEstimate(flops=flops, transcendentals=0, bytes_accessed=0),
        compiler_params=pltpu.CompilerParams(vmem_limit_bytes=mib * 1024 * 1024),
    )


def dot_nn(a, b):
    return lax.dot_general(a, b, (((1,), (0,)), ((), ())), preferred_element_type=F32)


def dot_nt(a, b):
    return lax.dot_general(a, b, (((1,), (1,)), ((), ())), preferred_element_type=F32)


def pick_body(idx_ref, tok_ref, out_ref):
    caps, rows = idx_ref.shape[0], tok_ref.shape[0]
    hot = (lax.broadcasted_iota(jnp.int32, (caps, rows), 1) == idx_ref[...]).astype(BF)
    width = tok_ref.shape[1] // out_ref.shape[0]
    pad = jnp.zeros((caps, out_ref.shape[2] - width), BF)
    for m in range(out_ref.shape[0]):
        out_ref[m, :, :width] = dot_nn(hot, tok_ref[:, m * width : (m + 1) * width]).astype(BF)
        out_ref[m, :, width:] = pad


def mix(ord_ref, src, wrefs, spots):
    width, acc = 192, None
    for wref, places in zip(wrefs, spots):
        pieces = len(places) // 4
        for n, k in enumerate(places):
            lo = (n % pieces) * width
            part = dot_nn(src[ord_ref[k], :, :width], wref[n // pieces, lo : lo + width, :])
            acc = part if acc is None else acc + part
    return acc


def early_body(ord_ref, own_ref, mate_ref, a_ref, b_ref, out_ref):
    caps = own_ref.shape[1]
    spots = ([4 * q for q in range(4)], [4 * q + 1 for q in range(4)])
    for n, src in enumerate((own_ref, mate_ref)):
        out_ref[n * caps : (n + 1) * caps, :] = mix(ord_ref, src, (a_ref, b_ref), spots)


def hidden_body(ord_ref, own_ref, mate_ref, early_ref, c_ref, out_ref, res_ref, sems):
    caps = own_ref.shape[1]
    core = ord_ref[32]
    spots = ([4 * q + n for q in range(4) for n in (2, 3)],)
    for n, src in enumerate((own_ref, mate_ref)):
        acc = early_ref[n * caps : (n + 1) * caps, :] + mix(ord_ref, src, (c_ref,), spots)
        cols = []
        for s in range(2):
            gate = acc[:, 256 * s : 256 * s + 128]
            up = acc[:, 256 * s + 128 : 256 * s + 256]
            cols.append((gate / (1.0 + jnp.exp(-gate)) * up).astype(BF))
        at = pl.multiple_of((core if n == 0 else 1 - core) * caps, caps)
        res_ref[pl.ds(at, caps), :] = jnp.concatenate(cols, axis=1)
    copies = [pltpu.make_async_copy(res_ref, out_ref.at[g], sems.at[g]) for g in range(8)]
    for copy in copies:
        copy.start()
    for copy in copies:
        copy.wait()


def down_body(ord_ref, idx_ref, first_ref, second_ref, hid_ref, out_ref, scr, second_vmem, sem):
    caps = idx_ref.shape[1]
    rows, unit = 512, 24
    fetch = pltpu.make_async_copy(second_ref, second_vmem, sem)
    fetch.start()
    for n, w_ref in enumerate((first_ref, second_vmem)):
        if n == 1:
            fetch.wait()
        acc = None
        for g in range(8):
            lo = 512 * (g % 4) + 256 * (g // 4)
            part = dot_nt(w_ref[:, lo : lo + 256], hid_ref[g])
            acc = part if acc is None else acc + part
        for k in range(8):
            at = pl.multiple_of(ord_ref[16 + 8 * n + k] * unit, 8)
            scr[pl.ds(at, unit), :] = acc[k * unit : (k + 1) * unit, :]
    for b in range(2):
        hot = (lax.broadcasted_iota(jnp.int32, (rows, caps), 0) == idx_ref[b : b + 1, :]).astype(BF)
        dense = dot_nt(scr[:, b * caps : (b + 1) * caps].astype(BF), hot).astype(BF)
        for q in range(4):
            out_ref[q, :, b * 128 : (b + 1) * 128] = dense[:, q * 128 : (q + 1) * 128]


def spread_body(*refs):
    out_ref, sems = refs[-2], refs[-1]
    lo, copies = 0, []
    for n, r in enumerate(refs[:-2]):
        for q in range(out_ref.shape[0]):
            copies.append(pltpu.make_async_copy(r, out_ref.at[q, pl.ds(lo, r.shape[0])], sems.at[n, q]))
        lo += r.shape[0]
    for copy in copies:
        copy.start()
    for copy in copies:
        copy.wait()


def quarter_body(in_ref, out_ref):
    for x in range(4):
        out_ref[:, 512 * x : 512 * (x + 1)] = in_ref[24 * x : 24 * (x + 1), :]


def total_body(in_ref, out_ref):
    acc = in_ref[0].astype(F32)
    for q in range(1, 4):
        acc = acc + in_ref[q].astype(F32)
    out_ref[...] = acc.T.astype(BF)


def place_body(in_ref, scale_ref, out_ref, scr):
    unit = 24
    for g in range(8):
        turned = in_ref[g].astype(F32).T
        core, x = g // 4, g % 4
        for m in range(16):
            lo = 192 * m + 96 * core + unit * x
            scr[lo : lo + unit, :] = turned[m * unit : (m + 1) * unit, :]
    for n in range(6):
        out_ref[:, n * 512 : (n + 1) * 512] = (scr[n * 512 : (n + 1) * 512, :].T * scale_ref[...]).astype(BF)


def pairs(step):
    flips = ((1, 3), (3, 1))
    return [(2 * i + c, 2 * (i ^ flips[c][step]) + c) for i in range(4) for c in range(2)]


def join_body(a_ref, b_ref, out_ref):
    rows = a_ref.shape[0]
    out_ref[:rows, :] = a_ref[...]
    out_ref[rows:, :] = b_ref[...]


def join(a, b):
    out = jax.ShapeDtypeStruct((a.shape[0] + b.shape[0], a.shape[1]), BF)
    return call(join_body, out, [vm(), vm()], mib=4)(a, b)


def meet(value, axis, step):
    return lax.ppermute(value, (axis, "c"), pairs(step))


def over_y(parts):
    rows, cols = sum(p.shape[0] for p in parts), parts[0].shape[1]
    wide = call(
        spread_body,
        jax.ShapeDtypeStruct((4, rows, cols), BF),
        [vm()] * len(parts),
        scratch=[pltpu.SemaphoreType.DMA((len(parts), 4))],
        mib=4,
        to=hb,
    )(*parts)
    return lax.all_to_all(wide, "y", 0, 0, tiled=True)


def shards(tokens, expert_ids, route_weight, index_list, gate_weight, up_weight, down_weight):
    zh, y, c, zl, x = (lax.axis_index(n) for n in ("zh", "y", "c", "zl", "x"))
    caps = index_list.shape[1]

    cut = lambda w, n: w[:, 128 * n : 128 * n + 128]
    mine = [
        jnp.concatenate([cut(w, 2 * h + s) for s in range(2) for w in (gate_weight, up_weight)], axis=1)
        for h in range(2)
    ]
    both_rows = lax.all_to_all(jnp.concatenate(mine, axis=0), "c", 0, 0, tiled=True)

    turned = down_weight.T
    quarter = lax.all_to_all(turned, "x", 0, 0, tiled=True)
    quarter = call(quarter_body, jax.ShapeDtypeStruct((24, 2048), BF), [vm()], mib=4)(quarter)

    flip = jnp.where(c == 0, jnp.array([0, 1, 3, 2]), jnp.array([0, 3, 1, 2])).astype(jnp.int32)
    order = ((zh ^ flip)[None, :] * 4 + jnp.arange(4, dtype=jnp.int32)[:, None]).reshape(16)
    order_down = ((zh ^ flip)[None, :] * 4 + (y ^ flip)[:, None]).reshape(16)
    order = jnp.concatenate([order, order_down, c.reshape(1)]).astype(jnp.int32)

    rows = call(
        pick_body, jax.ShapeDtypeStruct((16, caps, 256), BF), [vm(), vm()], flops=2 * 256 * 512 * 3072
    )(index_list.reshape(caps, 1), tokens)
    swap = [(0, 1), (1, 0)]
    rows_mate = lax.ppermute(rows, "c", swap)
    index_mate = lax.ppermute(index_list, "c", swap)
    index_both = jnp.where(
        c == 0,
        jnp.concatenate([index_list, index_mate], axis=0),
        jnp.concatenate([index_mate, index_list], axis=0),
    )

    near = meet(both_rows, "zh", 0)
    far = meet(join(both_rows, near), "zh", 1)
    ya = over_y((both_rows,))
    yb = over_y((near,))
    yc = over_y((far,))

    near = meet(quarter, "zh", 0)
    two = join(quarter, near)
    far = meet(two, "zh", 1)
    four = join(two, far)
    near = meet(four, "y", 0)
    down_first = join(four, near)
    down_second = meet(down_first, "y", 1)

    early = call(
        early_body, jax.ShapeDtypeStruct((512, 512), F32), [sm()] + [vm()] * 4, flops=512 * 3072 * 512
    )(order, rows, rows_mate, ya, yb)
    wide = call(
        hidden_body, jax.ShapeDtypeStruct((8, 512, 256), BF), [sm()] + [vm()] * 4, flops=512 * 3072 * 512,
        scratch=[pltpu.VMEM((512, 256), BF), pltpu.SemaphoreType.DMA((8,))], to=hb,
    )(order, rows, rows_mate, early, yc)
    hid = lax.all_to_all(wide, ("c", "x"), 0, 0, tiled=True)

    parts = call(
        down_body,
        jax.ShapeDtypeStruct((4, 384, 256), BF),
        [sm(), vm(), vm(), hb(), vm()],
        scratch=[pltpu.VMEM((384, 512), F32), pltpu.VMEM((192, 2048), BF), pltpu.SemaphoreType.DMA],
        flops=2 * 512 * 384 * 2048,
    )(order, index_both, down_first, down_second, hid)
    parts = lax.all_to_all(parts, "zl", 0, 0, tiled=True)
    total = call(total_body, jax.ShapeDtypeStruct((256, 384), BF), [vm()], mib=8)(parts)
    owned = lax.all_to_all(total.reshape(8, 32, 384), ("c", "x"), 0, 0, tiled=True)

    start = (zl * 4 + x) * 32
    ids = lax.dynamic_slice_in_dim(expert_ids, start, 32, 0)
    weights = lax.dynamic_slice_in_dim(route_weight, start, 32, 0)
    scale = jnp.sum(jnp.where(ids == 0, weights, jnp.zeros_like(weights)), axis=1, keepdims=True)
    return call(
        place_body, jax.ShapeDtypeStruct((32, 3072), BF), [vm(), vm()], mib=8, scratch=[pltpu.VMEM((3072, 32), F32)]
    )(owned, scale)


def solution(mesh):
    fine = Mesh(mesh.devices.reshape(4, 4, 2, 4, 4), ("zh", "y", "c", "zl", "x"))
    edp, etp = ("zh", "y", "c"), ("zl", "x")
    in_specs = (P(edp, None), P(edp, None), P(edp, None), P(edp, None), P(edp, etp), P(edp, etp), P(etp, edp))

    return jax.shard_map(shards, mesh=fine, in_specs=in_specs, out_specs=P(edp + etp, None), check_vma=False)
```

time: 206 us -> 201 us (0.976)
  starting transfers between devices: 95.6 us -> 70.4 us
  waiting for transfers between devices: 55.4 us -> 72.3 us
  blocking collectives: 29 us -> 31.2 us
    ppermute x12 -> x6, starting transfers between devices: 59.4 us -> 32.2 us  [meet(): return lax.ppermute(value, (axis, 'c'), pairs(step))]
    all_to_all x2 -> x4, waiting for transfers between devices: 0.01 us -> 13.7 us  [the longest x3 13.7 us: over_y(): return lax.all_to_all(wide, 'y', 0, 0, tiled=True)]
    all_to_all x2 -> x4, starting transfers between devices: 14 us -> 21.1 us  [the longest x3 12.8 us: over_y(): return lax.all_to_all(wide, 'y', 0, 0, tiled=True)]
    all_to_all x1, blocking collectives: 3.78 us -> 10.4 us  [shards(): lax.all_to_all(jnp.concatenate(mine, axis=0), 'c', 0, 0, tiled=True)]
    ppermute x1, starting transfers between devices: 8.75 us -> 2.27 us  [shards(): rows_mate = lax.ppermute(rows, 'c', swap)]
    all_to_all x1, blocking collectives: 25.2 us -> 20.8 us  [shards(): parts = lax.all_to_all(parts, 'zl', 0, 0, tiled=True)]
    broadcast_in_dim x2 -> x0, local copies, waits for them, and re-layouts: 3.15 us -> none  [shards(): wide = jnp.broadcast_to(h[None], (8,) + h.shape)]
    unnamed x18 -> x20, local copies, waits for them, and re-layouts: 4.59 us -> 7.57 us
  transfers between devices with their start and end apart: 18 -> 14, of which waited for: 9 -> 9; matrix products, arithmetic and copies ran while one was open for 2% -> 1% of each run, Pallas kernels for 4% -> 5%
where the time goes in v1:
time: 201 us; the launch traced here: 199 us
  waiting for transfers between devices  72.3 us (36%)
  starting transfers between devices  70.4 us (35%)
  blocking collectives  31.2 us (16%)
  Pallas kernels  15.5 us (8%)
  local copies, waits for them, and re-layouts  8.85 us (4%)
    ppermute x6, waiting for transfers between devices, meet(): return lax.ppermute(value, (axis, 'c'), pairs(step))  52.5 us
    ppermute x6, starting transfers between devices, meet(): return lax.ppermute(value, (axis, 'c'), pairs(step))  32.2 us
    all_to_all x1, blocking collectives, shards(): parts = lax.all_to_all(parts, 'zl', 0, 0, tiled=True)  20.8 us
    all_to_all x3, waiting for transfers between devices, over_y(): return lax.all_to_all(wide, 'y', 0, 0, tiled=True)  13.7 us
    all_to_all x3, starting transfers between devices, over_y(): return lax.all_to_all(wide, 'y', 0, 0, tiled=True)  12.8 us
    all_to_all x1, blocking collectives, shards(): lax.all_to_all(jnp.concatenate(mine, axis=0), 'c', 0, 0, tiled=True)  10.4 us
    all_to_all x1, starting transfers between devices, shards(): hid = lax.all_to_all(wide, ('c', 'x'), 0, 0, tiled=True)  8.37 us
    unnamed x20, local copies, waits for them, and re-layouts  7.57 us
  transfers between devices with their start and end apart: 14, of which 9 were waited for; matrix products, arithmetic and copies ran while one was open for 1% of the time, Pallas kernels for 5%

profile of v1, /device:TPU:1, one launch (start us, length us, event | category | flops | bytes accessed | tf_op | source)
XLA Modules:
  0.0 199.5 jit_solution(11302656807790686773)
XLA Ops:
  0.9 10.4 %all_to_all.52 = bf16[2,96,512]{2,1,0:T(8,128)(2,1)S(1)} all-to-all(bf16[2,96,512]{2,1,0:T(8,128)(2,1)S(1)} %bitcast.14), channel_id=1, replica_groups=mesh['zh'=4,'y'=4,'c'=2,'zl'=4,'x'=4] {'c'}, dimensions={0} | all-to-all | bytes 393216 | tf_op jit(solution)/shard_map/all_to_all | solution.py:195
  12.2 3.5 %all-to-all-start.2 = ((bf16[4,192,512]{2,1,0:T(8,128)(2,1)}), bf16[4,192,512]{2,1,0:T(8,128)(2,1)S(1)}, u32[]{:S(2)}, u32[]{:S(2)}) async-start(bf16[4,192,512]{2,1,0:T(8,128)(2,1)} %shard_map.96), calls=%async_computation.2 | async-start | bytes 1572864 | tf_op jit(solution)/shard_map/all_to_all | solution.py:183
  15.9 1.9 copy-done.2
  17.8 1.3 shard_map.95.own_ref
  19.1 2.3 %collective-permute-start.5 = (bf16[16,256,256]{2,1,0:T(8,128)(2,1)S(1)}, bf16[16,256,256]{2,1,0:T(8,128)(2,1)}, u32[]{:S(2)}, u32[]{:S(2)}) collective-permute-start(bf16[16,256,256]{2,1,0:T(8,128)(2,1)S(1)} %shard_map.95.own_ref), channel_id=1, source_target_pairs={{0,16},{16,0},{1,17},{17,1},{2,18},{18,2},{3,19},{19,3},{4,20},{20... | collective-permute-start | bytes 6291464 | tf_op jit(solution)/shard_map/ppermute | solution.py:210
  21.4 8.1 %collective-permute-start.6 = (bf16[192,512]{1,0:T(8,128)(2,1)S(1)}, bf16[192,512]{1,0:T(8,128)(2,1)S(1)}, u32[]{:S(2)}, u32[]{:S(2)}) collective-permute-start(bf16[192,512]{1,0:T(8,128)(2,1)S(1)} %bitcast.11), channel_id=1, source_target_pairs={{0,128},{16,400},{128,0},{144,272},{256,384},{272,144},{384,256},{... | collective-permute-start | bytes 589832 | tf_op jit(solution)/shard_map/ppermute | solution.py:170
  29.5 6.5 %collective-permute-done.6.refs_0_.b_ref = bf16[192,512]{1,0:T(8,128)(2,1)S(1)} collective-permute-done((bf16[192,512]{1,0:T(8,128)(2,1)S(1)}, bf16[192,512]{1,0:T(8,128)(2,1)S(1)}, u32[]{:S(2)}, u32[]{:S(2)}) %collective-permute-start.6) | collective-permute-done | bytes 196640 | tf_op jit(solution)/shard_map/ppermute | solution.py:170
  36.9 4.5 %all-to-all-start.3 = ((bf16[4,192,512]{2,1,0:T(8,128)(2,1)}), bf16[4,192,512]{2,1,0:T(8,128)(2,1)}, u32[]{:S(2)}, u32[]{:S(2)}) async-start(bf16[4,192,512]{2,1,0:T(8,128)(2,1)} %shard_map.97), calls=%async_computation.3 | async-start | bytes 1572864 | tf_op jit(solution)/shard_map/all_to_all | solution.py:183
  41.5 8.1 %collective-permute-start.7 = (bf16[384,512]{1,0:T(8,128)(2,1)S(1)}, bf16[384,512]{1,0:T(8,128)(2,1)S(1)}, u32[]{:S(2)}, u32[]{:S(2)}) collective-permute-start(bf16[384,512]{1,0:T(8,128)(2,1)S(1)} %shard_map.99), channel_id=1, source_target_pairs={{0,384},{16,144},{128,256},{144,16},{256,128},{272,400},{384,0},{4... | collective-permute-start | bytes 1179656 | tf_op jit(solution)/shard_map/ppermute | solution.py:170
  49.6 17.4 %collective-permute-done.7.refs_0_ = bf16[384,512]{1,0:T(8,128)(2,1)S(1)} collective-permute-done((bf16[384,512]{1,0:T(8,128)(2,1)S(1)}, bf16[384,512]{1,0:T(8,128)(2,1)S(1)}, u32[]{:S(2)}, u32[]{:S(2)}) %collective-permute-start.7) | collective-permute-done | bytes 393248 | tf_op jit(solution)/shard_map/ppermute | solution.py:170
  67.8 1.2 copy-done.1
  68.9 4.7 %all-to-all-start.4 = ((bf16[4,384,512]{2,1,0:T(8,128)(2,1)}), bf16[4,384,512]{2,1,0:T(8,128)(2,1)}, u32[]{:S(2)}, u32[]{:S(2)}) async-start(bf16[4,384,512]{2,1,0:T(8,128)(2,1)} %copy-done.1), calls=%async_computation.4 | async-start | bytes 3145728 | tf_op jit(solution)/shard_map/all_to_all | solution.py:183
  75.1 3.0 %shard_map.98.early_ref = f32[512,512]{1,0:T(8,128)S(1)} custom-call(s32[33]{0:T(128)S(1)} %pad_add_fusion.ord_ref, bf16[16,256,256]{2,1,0:T(8,128)(2,1)S(1)} %shard_map.95.own_ref, bf16[16,256,256]{2,1,0:T(8,128)(2,1)} %collective-permute-done.5.mate_ref, bf16[4,192,512]{2,1,0:T(8,128)(2,1)S(1)} %copy-done.4, bf16[4,192,512]{2,1,0:T(8,128)(2,1)} %all-to-all-done.3.b_ref), custom_call_target="tpu_custom_call" | custom-call | flops 805306368 | tf_op jit(solution)/shard_map/pallas_call | solution.py:232
  78.1 13.7 %all-to-all-done.4.c_ref = bf16[4,384,512]{2,1,0:T(8,128)(2,1)} async-done(((bf16[4,384,512]{2,1,0:T(8,128)(2,1)}), bf16[4,384,512]{2,1,0:T(8,128)(2,1)}, u32[]{:S(2)}, u32[]{:S(2)}) %all-to-all-start.4) | async-done | bytes 1572896 | tf_op jit(solution)/shard_map/all_to_all | solution.py:183
  91.8 5.4 %all-to-all-start = ((bf16[4,24,512]{2,1,0:T(8,128)(2,1)}), bf16[4,24,512]{2,1,0:T(8,128)(2,1)S(1)}, u32[]{:S(2)}, u32[]{:S(2)}) async-start(bf16[4,24,512]{2,1,0:T(8,128)(2,1)} %bitcast.2), calls=%async_computation | async-start | bytes 196608 | tf_op jit(solution)/shard_map/all_to_all | solution.py:198
  97.2 3.5 %shard_map.101 = bf16[8,512,256]{2,1,0:T(8,128)(2,1)S(1)} custom-call(s32[33]{0:T(128)S(1)} %pad_add_fusion.ord_ref, bf16[16,256,256]{2,1,0:T(8,128)(2,1)S(1)} %shard_map.95.own_ref, bf16[16,256,256]{2,1,0:T(8,128)(2,1)} %collective-permute-done.5.mate_ref, f32[512,512]{1,0:T(8,128)S(1)} %shard_map.98.early_ref, bf16[4,384,512]{2,1,0:T(8,128)(2,1)} %all-to-all-done.4.c_ref), custom_call_target="tpu_custom_call" | custom-call | flops 805306368 | tf_op jit(solution)/shard_map/pallas_call | solution.py:235
  100.8 1.3 copy-done
  102.2 8.4 %all-to-all-start.5 = ((bf16[8,512,256]{2,1,0:T(8,128)(2,1)}), bf16[8,512,256]{2,1,0:T(8,128)(2,1)S(1)}, u32[]{:S(2)}, u32[]{:S(2)}) async-start(bf16[8,512,256]{2,1,0:T(8,128)(2,1)} %copy-done), calls=%async_computation.5 | async-start | bytes 4194304 | tf_op jit(solution)/shard_map/all_to_all | solution.py:239
  110.5 6.2 %collective-permute-start.1 = (bf16[24,2048]{1,0:T(8,128)(2,1)S(1)}, bf16[24,2048]{1,0:T(8,128)(2,1)S(1)}, u32[]{:S(2)}, u32[]{:S(2)}) collective-permute-start(bf16[24,2048]{1,0:T(8,128)(2,1)S(1)} %shard_map.91.a_ref), channel_id=1, source_target_pairs={{0,128},{16,400},{128,0},{144,272},{256,384},{272,144},{384,256},{... | collective-permute-start | bytes 294920 | tf_op jit(solution)/shard_map/ppermute | solution.py:170
  116.8 4.7 %collective-permute-done.1.b_ref = bf16[24,2048]{1,0:T(8,128)(2,1)S(1)} collective-permute-done((bf16[24,2048]{1,0:T(8,128)(2,1)S(1)}, bf16[24,2048]{1,0:T(8,128)(2,1)S(1)}, u32[]{:S(2)}, u32[]{:S(2)}) %collective-permute-start.1) | collective-permute-done | bytes 98336 | tf_op jit(solution)/shard_map/ppermute | solution.py:170
  121.5 5.2 %collective-permute-start.2 = (bf16[48,2048]{1,0:T(8,128)(2,1)S(1)}, bf16[48,2048]{1,0:T(8,128)(2,1)S(1)}, u32[]{:S(2)}, u32[]{:S(2)}) collective-permute-start(bf16[48,2048]{1,0:T(8,128)(2,1)S(1)} %shard_map.92.a_ref), channel_id=1, source_target_pairs={{0,384},{16,144},{128,256},{144,16},{256,128},{272,400},{384,0},{4... | collective-permute-start | bytes 589832 | tf_op jit(solution)/shard_map/ppermute | solution.py:170
  126.6 9.0 %collective-permute-done.2.b_ref = bf16[48,2048]{1,0:T(8,128)(2,1)S(1)} collective-permute-done((bf16[48,2048]{1,0:T(8,128)(2,1)S(1)}, bf16[48,2048]{1,0:T(8,128)(2,1)S(1)}, u32[]{:S(2)}, u32[]{:S(2)}) %collective-permute-start.2) | collective-permute-done | bytes 196640 | tf_op jit(solution)/shard_map/ppermute | solution.py:170
  135.7 2.8 %collective-permute-start.3 = (bf16[96,2048]{1,0:T(8,128)(2,1)S(1)}, bf16[96,2048]{1,0:T(8,128)(2,1)S(1)}, u32[]{:S(2)}, u32[]{:S(2)}) collective-permute-start(bf16[96,2048]{1,0:T(8,128)(2,1)S(1)} %shard_map.93.a_ref), channel_id=1, source_target_pairs={{0,32},{16,112},{32,0},{48,80},{64,96},{80,48},{96,64},{112,16},{1... | collective-permute-start | bytes 1179656 | tf_op jit(solution)/shard_map/ppermute | solution.py:170
  138.5 6.9 %collective-permute-done.3.b_ref = bf16[96,2048]{1,0:T(8,128)(2,1)S(1)} collective-permute-done((bf16[96,2048]{1,0:T(8,128)(2,1)S(1)}, bf16[96,2048]{1,0:T(8,128)(2,1)S(1)}, u32[]{:S(2)}, u32[]{:S(2)}) %collective-permute-start.3) | collective-permute-done | bytes 393248 | tf_op jit(solution)/shard_map/ppermute | solution.py:170
  145.5 1.9 collective-permute-start.4
  147.4 1.9 collective-permute-start
  150.5 8.0 %collective-permute-done.4.second_ref = bf16[192,2048]{1,0:T(8,128)(2,1)S(1)} collective-permute-done((bf16[192,2048]{1,0:T(8,128)(2,1)S(1)}, bf16[192,2048]{1,0:T(8,128)(2,1)S(1)}, u32[]{:S(2)}, u32[]{:S(2)}) %collective-permute-start.4) | collective-permute-done | bytes 786464 | tf_op jit(solution)/shard_map/ppermute | solution.py:170
  160.5 2.6 %shard_map.102 = bf16[4,384,256]{2,1,0:T(8,128)(2,1)S(1)} custom-call(s32[33]{0:T(128)S(1)} %pad_add_fusion.ord_ref, s32[2,256]{1,0:T(2,128)S(1)} %add_select_fusion.idx_ref, bf16[192,2048]{1,0:T(8,128)(2,1)S(1)} %shard_map.94.first_ref, bf16[192,2048]{1,0:T(8,128)(2,1)S(1)} %copy-done.6, bf16[8,512,256]{2,1,0:T(8,128)(2,1)S(1)} %all-to-all-done.5.hid_ref), custom_call_target="tpu_custom_call" | custom-call | flops 805306368 | tf_op jit(solution)/shard_map/pallas_call | solution.py:241
  163.1 20.8 %all_to_all.53.in_ref = bf16[4,384,256]{2,1,0:T(8,128)(2,1)S(1)} all-to-all(bf16[4,384,256]{2,1,0:T(8,128)(2,1)S(1)} %shard_map.102), channel_id=1, replica_groups=mesh['zh'=4,'y'=4,'c'=2,'zl'=4,'x'=4] {'zl'}, dimensions={0} | all-to-all | bytes 1572864 | tf_op jit(solution)/shard_map/all_to_all | solution.py:248
  184.8 7.4 %all-to-all-start.7 = ((bf16[8,32,384]{2,1,0:T(8,128)(2,1)}), bf16[8,32,384]{2,1,0:T(8,128)(2,1)S(1)}, u32[]{:S(2)}, u32[]{:S(2)}) async-start(bf16[8,32,384]{2,1,0:T(8,128)(2,1)} %bitcast.7), calls=%async_computation.7 | async-start | bytes 393216 | tf_op jit(solution)/shard_map/all_to_all | solution.py:250
  193.1 5.0 %all-to-all-done.7.in_ref = bf16[8,32,384]{2,1,0:T(8,128)(2,1)S(1)} async-done(((bf16[8,32,384]{2,1,0:T(8,128)(2,1)}), bf16[8,32,384]{2,1,0:T(8,128)(2,1)S(1)}, u32[]{:S(2)}, u32[]{:S(2)}) %all-to-all-start.7) | async-done | bytes 196640 | tf_op jit(solution)/shard_map/all_to_all | solution.py:250
  198.1 1.4 shard_map.104
  (43 shorter events, 10.2 us)
Async XLA Ops:
  0.0 15.8 %copy-start.7 = (s32[1,256]{1,0:T(1,128)S(1)}, s32[1,256]{1,0:T(1,128)}, u32[]{:S(2)}) copy-start(s32[1,256]{1,0:T(1,128)} %param.12) | copy-start | bytes 3076
  12.2 24.7 %all-to-all-start.2 = ((bf16[4,192,512]{2,1,0:T(8,128)(2,1)}), bf16[4,192,512]{2,1,0:T(8,128)(2,1)S(1)}, u32[]{:S(2)}, u32[]{:S(2)}) async-start(bf16[4,192,512]{2,1,0:T(8,128)(2,1)} %shard_map.96), calls=%async_computation.2 | async-start | bytes 1572864 | tf_op jit(solution)/shard_map/all_to_all | solution.py:183
  15.9 1.9 copy-start.2
  19.1 54.9 %collective-permute-start.5 = (bf16[16,256,256]{2,1,0:T(8,128)(2,1)S(1)}, bf16[16,256,256]{2,1,0:T(8,128)(2,1)}, u32[]{:S(2)}, u32[]{:S(2)}) collective-permute-start(bf16[16,256,256]{2,1,0:T(8,128)(2,1)S(1)} %shard_map.95.own_ref), channel_id=1, source_target_pairs={{0,16},{16,0},{1,17},{17,1},{2,18},{18,2},{3,19},{19,3},{4,20},{20... | collective-permute-start | bytes 6291464 | tf_op jit(solution)/shard_map/ppermute | solution.py:210
  21.4 14.6 %collective-permute-start.6 = (bf16[192,512]{1,0:T(8,128)(2,1)S(1)}, bf16[192,512]{1,0:T(8,128)(2,1)S(1)}, u32[]{:S(2)}, u32[]{:S(2)}) collective-permute-start(bf16[192,512]{1,0:T(8,128)(2,1)S(1)} %bitcast.11), channel_id=1, source_target_pairs={{0,128},{16,400},{128,0},{144,272},{256,384},{272,144},{384,256},{... | collective-permute-start | bytes 589832 | tf_op jit(solution)/shard_map/ppermute | solution.py:170
  36.9 30.8 %copy-start.3 = (bf16[4,192,512]{2,1,0:T(8,128)(2,1)}, bf16[4,192,512]{2,1,0:T(8,128)(2,1)S(1)}, u32[]{:S(2)}) copy-start(bf16[4,192,512]{2,1,0:T(8,128)(2,1)S(1)} %all-to-all-done.2.a_ref) | copy-start | bytes 2359300
  36.9 32.0 %all-to-all-start.3 = ((bf16[4,192,512]{2,1,0:T(8,128)(2,1)}), bf16[4,192,512]{2,1,0:T(8,128)(2,1)}, u32[]{:S(2)}, u32[]{:S(2)}) async-start(bf16[4,192,512]{2,1,0:T(8,128)(2,1)} %shard_map.97), calls=%async_computation.3 | async-start | bytes 1572864 | tf_op jit(solution)/shard_map/all_to_all | solution.py:183
  41.5 32.2 %copy-start.8 = (s32[4]{0:T(128)S(1)}, s32[4]{0:T(128)}, u32[]{:S(2)}) copy-start(s32[4]{0:T(128)} %constant.38.clone) | copy-start | bytes 52
  41.5 32.2 %copy-start.9 = (s32[4]{0:T(128)S(1)}, s32[4]{0:T(128)}, u32[]{:S(2)}) copy-start(s32[4]{0:T(128)} %constant.39.clone) | copy-start | bytes 52
  41.5 25.5 %collective-permute-start.7 = (bf16[384,512]{1,0:T(8,128)(2,1)S(1)}, bf16[384,512]{1,0:T(8,128)(2,1)S(1)}, u32[]{:S(2)}, u32[]{:S(2)}) collective-permute-start(bf16[384,512]{1,0:T(8,128)(2,1)S(1)} %shard_map.99), channel_id=1, source_target_pairs={{0,384},{16,144},{128,256},{144,16},{256,128},{272,400},{384,0},{4... | collective-permute-start | bytes 1179656 | tf_op jit(solution)/shard_map/ppermute | solution.py:170
  67.8 1.2 copy-start.1
  68.9 22.9 %all-to-all-start.4 = ((bf16[4,384,512]{2,1,0:T(8,128)(2,1)}), bf16[4,384,512]{2,1,0:T(8,128)(2,1)}, u32[]{:S(2)}, u32[]{:S(2)}) async-start(bf16[4,384,512]{2,1,0:T(8,128)(2,1)} %copy-done.1), calls=%async_computation.4 | async-start | bytes 3145728 | tf_op jit(solution)/shard_map/all_to_all | solution.py:183
  74.0 1.1 copy-start.4
  91.8 10.3 %all-to-all-start = ((bf16[4,24,512]{2,1,0:T(8,128)(2,1)}), bf16[4,24,512]{2,1,0:T(8,128)(2,1)S(1)}, u32[]{:S(2)}, u32[]{:S(2)}) async-start(bf16[4,24,512]{2,1,0:T(8,128)(2,1)} %bitcast.2), calls=%async_computation | async-start | bytes 196608 | tf_op jit(solution)/shard_map/all_to_all | solution.py:198
  100.8 1.4 copy-start
  102.2 57.2 %all-to-all-start.5 = ((bf16[8,512,256]{2,1,0:T(8,128)(2,1)}), bf16[8,512,256]{2,1,0:T(8,128)(2,1)S(1)}, u32[]{:S(2)}, u32[]{:S(2)}) async-start(bf16[8,512,256]{2,1,0:T(8,128)(2,1)} %copy-done), calls=%async_computation.5 | async-start | bytes 4194304 | tf_op jit(solution)/shard_map/all_to_all | solution.py:239
  110.5 10.9 %collective-permute-start.1 = (bf16[24,2048]{1,0:T(8,128)(2,1)S(1)}, bf16[24,2048]{1,0:T(8,128)(2,1)S(1)}, u32[]{:S(2)}, u32[]{:S(2)}) collective-permute-start(bf16[24,2048]{1,0:T(8,128)(2,1)S(1)} %shard_map.91.a_ref), channel_id=1, source_target_pairs={{0,128},{16,400},{128,0},{144,272},{256,384},{272,144},{384,256},{... | collective-permute-start | bytes 294920 | tf_op jit(solution)/shard_map/ppermute | solution.py:170
  121.5 14.2 %collective-permute-start.2 = (bf16[48,2048]{1,0:T(8,128)(2,1)S(1)}, bf16[48,2048]{1,0:T(8,128)(2,1)S(1)}, u32[]{:S(2)}, u32[]{:S(2)}) collective-permute-start(bf16[48,2048]{1,0:T(8,128)(2,1)S(1)} %shard_map.92.a_ref), channel_id=1, source_target_pairs={{0,384},{16,144},{128,256},{144,16},{256,128},{272,400},{384,0},{4... | collective-permute-start | bytes 589832 | tf_op jit(solution)/shard_map/ppermute | solution.py:170
  135.7 9.7 %collective-permute-start.3 = (bf16[96,2048]{1,0:T(8,128)(2,1)S(1)}, bf16[96,2048]{1,0:T(8,128)(2,1)S(1)}, u32[]{:S(2)}, u32[]{:S(2)}) collective-permute-start(bf16[96,2048]{1,0:T(8,128)(2,1)S(1)} %shard_map.93.a_ref), channel_id=1, source_target_pairs={{0,32},{16,112},{32,0},{48,80},{64,96},{80,48},{96,64},{112,16},{1... | collective-permute-start | bytes 1179656 | tf_op jit(solution)/shard_map/ppermute | solution.py:170
  145.5 13.0 %collective-permute-start.4 = (bf16[192,2048]{1,0:T(8,128)(2,1)S(1)}, bf16[192,2048]{1,0:T(8,128)(2,1)S(1)}, u32[]{:S(2)}, u32[]{:S(2)}) collective-permute-start(bf16[192,2048]{1,0:T(8,128)(2,1)S(1)} %shard_map.94.first_ref), channel_id=1, source_target_pairs={{0,96},{16,48},{32,64},{48,16},{64,32},{80,112},{96,0},{112,80},{1... | collective-permute-start | bytes 2359304 | tf_op jit(solution)/shard_map/ppermute | solution.py:170
  147.4 3.1 %collective-permute-start = (s32[1,256]{1,0:T(1,128)S(1)}, s32[1,256]{1,0:T(1,128)S(1)}, u32[]{:S(2)}, u32[]{:S(2)}) collective-permute-start(s32[1,256]{1,0:T(1,128)S(1)} %copy-done.7), channel_id=1, source_target_pairs={{0,16},{16,0},{1,17},{17,1},{2,18},{18,2},{3,19},{19,3},{4,20},{20... | collective-permute-start | bytes 3080 | tf_op jit(solution)/shard_map/ppermute | solution.py:211
  158.5 0.9 copy-start.5
  159.4 1.1 copy-start.6
  184.8 13.2 %all-to-all-start.7 = ((bf16[8,32,384]{2,1,0:T(8,128)(2,1)}), bf16[8,32,384]{2,1,0:T(8,128)(2,1)S(1)}, u32[]{:S(2)}, u32[]{:S(2)}) async-start(bf16[8,32,384]{2,1,0:T(8,128)(2,1)} %bitcast.7), calls=%async_computation.7 | async-start | bytes 393216 | tf_op jit(solution)/shard_map/all_to_all | solution.py:250

commit v2 on v1

--- a/solution.py
+++ b/solution.py
@@ -63,11 +63,11 @@
     return acc
 
 
-def early_body(ord_ref, own_ref, mate_ref, a_ref, b_ref, out_ref):
+def early_body(ord_ref, own_ref, mate_ref, ab_ref, out_ref):
     caps = own_ref.shape[1]
-    spots = ([4 * q for q in range(4)], [4 * q + 1 for q in range(4)])
+    spots = ([4 * q + n for q in range(4) for n in (0, 1)],)
     for n, src in enumerate((own_ref, mate_ref)):
-        out_ref[n * caps : (n + 1) * caps, :] = mix(ord_ref, src, (a_ref, b_ref), spots)
+        out_ref[n * caps : (n + 1) * caps, :] = mix(ord_ref, src, (ab_ref,), spots)
 
 
 def hidden_body(ord_ref, own_ref, mate_ref, early_ref, c_ref, out_ref, res_ref, sems):
@@ -108,9 +108,9 @@
             scr[pl.ds(at, unit), :] = acc[k * unit : (k + 1) * unit, :]
     for b in range(2):
         hot = (lax.broadcasted_iota(jnp.int32, (rows, caps), 0) == idx_ref[b : b + 1, :]).astype(BF)
-        dense = dot_nt(scr[:, b * caps : (b + 1) * caps].astype(BF), hot).astype(BF)
-        for q in range(4):
-            out_ref[q, :, b * 128 : (b + 1) * 128] = dense[:, q * 128 : (q + 1) * 128]
+        dense = dot_nt(hot, scr[:, b * caps : (b + 1) * caps].astype(BF)).astype(BF)
+        for n in range(16):
+            out_ref[16 * b + n] = dense[32 * n : 32 * n + 32, :]
 
 
 def spread_body(*refs):
@@ -131,18 +131,14 @@
         out_ref[:, 512 * x : 512 * (x + 1)] = in_ref[24 * x : 24 * (x + 1), :]
 
 
-def total_body(in_ref, out_ref):
-    acc = in_ref[0].astype(F32)
-    for q in range(1, 4):
-        acc = acc + in_ref[q].astype(F32)
-    out_ref[...] = acc.T.astype(BF)
-
-
 def place_body(in_ref, scale_ref, out_ref, scr):
     unit = 24
     for g in range(8):
-        turned = in_ref[g].astype(F32).T
         core, x = g // 4, g % 4
+        acc = in_ref[16 * core + x].astype(F32)
+        for q in range(1, 4):
+            acc = acc + in_ref[16 * core + 4 * q + x].astype(F32)
+        turned = acc.T
         for m in range(16):
             lo = 192 * m + 96 * core + unit * x
             scr[lo : lo + unit, :] = turned[m * unit : (m + 1) * unit, :]
@@ -216,9 +212,9 @@
     )
 
     near = meet(both_rows, "zh", 0)
-    far = meet(join(both_rows, near), "zh", 1)
-    ya = over_y((both_rows,))
-    yb = over_y((near,))
+    both = join(both_rows, near)
+    far = meet(both, "zh", 1)
+    yab = over_y((both,))
     yc = over_y((far,))
 
     near = meet(quarter, "zh", 0)
@@ -230,8 +226,8 @@
     down_second = meet(down_first, "y", 1)
 
     early = call(
-        early_body, jax.ShapeDtypeStruct((512, 512), F32), [sm()] + [vm()] * 4, flops=512 * 3072 * 512
-    )(order, rows, rows_mate, ya, yb)
+        early_body, jax.ShapeDtypeStruct((512, 512), F32), [sm()] + [vm()] * 3, flops=512 * 3072 * 512
+    )(order, rows, rows_mate, yab)
     wide = call(
         hidden_body, jax.ShapeDtypeStruct((8, 512, 256), BF), [sm()] + [vm()] * 4, flops=512 * 3072 * 512,
         scratch=[pltpu.VMEM((512, 256), BF), pltpu.SemaphoreType.DMA((8,))], to=hb,
@@ -240,14 +236,12 @@
 
     parts = call(
         down_body,
-        jax.ShapeDtypeStruct((4, 384, 256), BF),
+        jax.ShapeDtypeStruct((32, 32, 384), BF),
         [sm(), vm(), vm(), hb(), vm()],
         scratch=[pltpu.VMEM((384, 512), F32), pltpu.VMEM((192, 2048), BF), pltpu.SemaphoreType.DMA],
         flops=2 * 512 * 384 * 2048,
     )(order, index_both, down_first, down_second, hid)
-    parts = lax.all_to_all(parts, "zl", 0, 0, tiled=True)
-    total = call(total_body, jax.ShapeDtypeStruct((256, 384), BF), [vm()], mib=8)(parts)
-    owned = lax.all_to_all(total.reshape(8, 32, 384), ("c", "x"), 0, 0, tiled=True)
+    owned = lax.all_to_all(parts, ("c", "zl", "x"), 0, 0, tiled=True)
 
     start = (zl * 4 + x) * 32
     ids = lax.dynamic_slice_in_dim(expert_ids, start, 32, 0)

time: 201 us -> 191 us (0.950)
  blocking collectives: 31.2 us -> 10.4 us
  waiting for transfers between devices: 72.3 us -> 91 us
  starting transfers between devices: 70.4 us -> 64.6 us
    all_to_all x1 -> x0, blocking collectives: 20.8 us -> none  [shards(): parts = lax.all_to_all(parts, 'zl', 0, 0, tiled=True)]
    all_to_all x1, waiting for transfers between devices: 4.95 us -> 20.9 us  [shards(): owned = lax.all_to_all(parts, ('c', 'zl', 'x'), 0, 0, tiled=True)]
    ppermute x6, starting transfers between devices: 32.2 us -> 26.8 us  [meet(): return lax.ppermute(value, (axis, 'c'), pairs(step))]
    all_to_all x1, starting transfers between devices: 7.41 us -> 11.2 us  [shards(): owned = lax.all_to_all(parts, ('c', 'zl', 'x'), 0, 0, tiled=True)]
    all_to_all x1, starting transfers between devices: 8.37 us -> 5.47 us  [shards(): hid = lax.all_to_all(wide, ('c', 'x'), 0, 0, tiled=True)]
    all_to_all x3 -> x2, waiting for transfers between devices: 13.7 us -> 16.5 us  [over_y(): return lax.all_to_all(wide, 'y', 0, 0, tiled=True)]
    ppermute x1, starting transfers between devices: 1.94 us -> 4.42 us  [shards(): index_mate = lax.ppermute(index_list, 'c', swap)]
    all_to_all x3 -> x2, starting transfers between devices: 12.8 us -> 10.7 us  [over_y(): return lax.all_to_all(wide, 'y', 0, 0, tiled=True)]
  transfers between devices with their start and end apart: 14 -> 13, of which waited for: 9 -> 9; matrix products, arithmetic and copies ran while one was open for 1% -> 1% of each run, Pallas kernels for 5% -> 5%
where the time goes in v2:
time: 191 us; the launch traced here: 190 us
  waiting for transfers between devices  91 us (48%)
  starting transfers between devices  64.6 us (34%)
  Pallas kernels  15.5 us (8%)
  blocking collectives  10.4 us (5%)
  local copies, waits for them, and re-layouts  7.67 us (4%)
    ppermute x6, waiting for transfers between devices, meet(): return lax.ppermute(value, (axis, 'c'), pairs(step))  52.8 us
    ppermute x6, starting transfers between devices, meet(): return lax.ppermute(value, (axis, 'c'), pairs(step))  26.8 us
    all_to_all x1, waiting for transfers between devices, shards(): owned = lax.all_to_all(parts, ('c', 'zl', 'x'), 0, 0, tiled=True)  20.9 us
    all_to_all x2, waiting for transfers between devices, over_y(): return lax.all_to_all(wide, 'y', 0, 0, tiled=True)  16.5 us
    all_to_all x1, starting transfers between devices, shards(): owned = lax.all_to_all(parts, ('c', 'zl', 'x'), 0, 0, tiled=True)  11.2 us
    all_to_all x2, starting transfers between devices, over_y(): return lax.all_to_all(wide, 'y', 0, 0, tiled=True)  10.7 us
    all_to_all x1, blocking collectives, shards(): lax.all_to_all(jnp.concatenate(mine, axis=0), 'c', 0, 0, tiled=True)  10.4 us
    unnamed x16, local copies, waits for them, and re-layouts  6.41 us
  transfers between devices with their start and end apart: 13, of which 9 were waited for; matrix products, arithmetic and copies ran while one was open for 1% of the time, Pallas kernels for 5%

profile of v2, /device:TPU:1, one launch (start us, length us, event | category | flops | bytes accessed | tf_op | source)
XLA Modules:
  0.0 190.5 jit_solution(982490292045293083)
XLA Ops:
  0.9 10.4 %all_to_all.42 = bf16[2,96,512]{2,1,0:T(8,128)(2,1)S(1)} all-to-all(bf16[2,96,512]{2,1,0:T(8,128)(2,1)S(1)} %bitcast.12), channel_id=1, replica_groups=mesh['zh'=4,'y'=4,'c'=2,'zl'=4,'x'=4] {'c'}, dimensions={0} | all-to-all | bytes 393216 | tf_op jit(solution)/shard_map/all_to_all | solution.py:191
  11.3 7.1 %collective-permute-start.6 = (bf16[192,512]{1,0:T(8,128)(2,1)S(1)}, bf16[192,512]{1,0:T(8,128)(2,1)S(1)}, u32[]{:S(2)}, u32[]{:S(2)}) collective-permute-start(bf16[192,512]{1,0:T(8,128)(2,1)S(1)} %bitcast.9), channel_id=1, source_target_pairs={{0,128},{16,400},{128,0},{144,272},{256,384},{272,144},{384,256},{... | collective-permute-start | bytes 589832 | tf_op jit(solution)/shard_map/ppermute | solution.py:166
  18.4 6.7 %collective-permute-done.6.b_ref = bf16[192,512]{1,0:T(8,128)(2,1)S(1)} collective-permute-done((bf16[192,512]{1,0:T(8,128)(2,1)S(1)}, bf16[192,512]{1,0:T(8,128)(2,1)S(1)}, u32[]{:S(2)}, u32[]{:S(2)}) %collective-permute-start.6) | collective-permute-done | bytes 196640 | tf_op jit(solution)/shard_map/ppermute | solution.py:166
  25.2 1.2 shard_map.97
  26.4 6.4 %all-to-all-start.2 = ((bf16[4,384,512]{2,1,0:T(8,128)(2,1)}), bf16[4,384,512]{2,1,0:T(8,128)(2,1)}, u32[]{:S(2)}, u32[]{:S(2)}) async-start(bf16[4,384,512]{2,1,0:T(8,128)(2,1)} %shard_map.97), calls=%async_computation.2 | async-start | bytes 3145728 | tf_op jit(solution)/shard_map/all_to_all | solution.py:179
  32.9 1.9 copy-done.2
  34.8 1.3 shard_map.95.own_ref
  36.2 1.9 %collective-permute-start.5 = (bf16[16,256,256]{2,1,0:T(8,128)(2,1)S(1)}, bf16[16,256,256]{2,1,0:T(8,128)(2,1)}, u32[]{:S(2)}, u32[]{:S(2)}) collective-permute-start(bf16[16,256,256]{2,1,0:T(8,128)(2,1)S(1)} %shard_map.95.own_ref), channel_id=1, source_target_pairs={{0,16},{16,0},{1,17},{17,1},{2,18},{18,2},{3,19},{19,3},{4,20},{20... | collective-permute-start | bytes 6291464 | tf_op jit(solution)/shard_map/ppermute | solution.py:206
  38.1 5.8 %collective-permute-start.7 = (bf16[384,512]{1,0:T(8,128)(2,1)S(1)}, bf16[384,512]{1,0:T(8,128)(2,1)S(1)}, u32[]{:S(2)}, u32[]{:S(2)}) collective-permute-start(bf16[384,512]{1,0:T(8,128)(2,1)S(1)} %shard_map.96.refs_0_), channel_id=1, source_target_pairs={{0,384},{16,144},{128,256},{144,16},{256,128},{272,400},{384,0},{4... | collective-permute-start | bytes 1179656 | tf_op jit(solution)/shard_map/ppermute | solution.py:166
  43.9 19.3 %collective-permute-done.7.refs_0_ = bf16[384,512]{1,0:T(8,128)(2,1)S(1)} collective-permute-done((bf16[384,512]{1,0:T(8,128)(2,1)S(1)}, bf16[384,512]{1,0:T(8,128)(2,1)S(1)}, u32[]{:S(2)}, u32[]{:S(2)}) %collective-permute-start.7) | collective-permute-done | bytes 393248 | tf_op jit(solution)/shard_map/ppermute | solution.py:166
  64.0 1.2 copy-done.1
  65.1 4.3 %all-to-all-start.3 = ((bf16[4,384,512]{2,1,0:T(8,128)(2,1)}), bf16[4,384,512]{2,1,0:T(8,128)(2,1)}, u32[]{:S(2)}, u32[]{:S(2)}) async-start(bf16[4,384,512]{2,1,0:T(8,128)(2,1)} %copy-done.1), calls=%async_computation.3 | async-start | bytes 3145728 | tf_op jit(solution)/shard_map/all_to_all | solution.py:179
  69.8 3.3 %shard_map.98.early_ref = f32[512,512]{1,0:T(8,128)S(1)} custom-call(s32[33]{0:T(128)S(1)} %pad_add_fusion.ord_ref, bf16[16,256,256]{2,1,0:T(8,128)(2,1)S(1)} %shard_map.95.own_ref, bf16[16,256,256]{2,1,0:T(8,128)(2,1)} %collective-permute-done.5.mate_ref, bf16[4,384,512]{2,1,0:T(8,128)(2,1)} %all-to-all-done.2.ab_ref), custom_call_target="tpu_custom_call" | custom-call | flops 805306368 | tf_op jit(solution)/shard_map/pallas_call | solution.py:228
  73.1 16.5 %all-to-all-done.3.c_ref = bf16[4,384,512]{2,1,0:T(8,128)(2,1)} async-done(((bf16[4,384,512]{2,1,0:T(8,128)(2,1)}), bf16[4,384,512]{2,1,0:T(8,128)(2,1)}, u32[]{:S(2)}, u32[]{:S(2)}) %all-to-all-start.3) | async-done | bytes 1572896 | tf_op jit(solution)/shard_map/all_to_all | solution.py:179
  89.6 4.1 %all-to-all-start = ((bf16[4,24,512]{2,1,0:T(8,128)(2,1)}), bf16[4,24,512]{2,1,0:T(8,128)(2,1)S(1)}, u32[]{:S(2)}, u32[]{:S(2)}) async-start(bf16[4,24,512]{2,1,0:T(8,128)(2,1)} %bitcast.2), calls=%async_computation | async-start | bytes 196608 | tf_op jit(solution)/shard_map/all_to_all | solution.py:194
  93.7 3.5 %shard_map.100 = bf16[8,512,256]{2,1,0:T(8,128)(2,1)S(1)} custom-call(s32[33]{0:T(128)S(1)} %pad_add_fusion.ord_ref, bf16[16,256,256]{2,1,0:T(8,128)(2,1)S(1)} %shard_map.95.own_ref, bf16[16,256,256]{2,1,0:T(8,128)(2,1)} %collective-permute-done.5.mate_ref, f32[512,512]{1,0:T(8,128)S(1)} %shard_map.98.early_ref, bf16[4,384,512]{2,1,0:T(8,128)(2,1)} %all-to-all-done.3.c_ref), custom_call_target="tpu_custom_call" | custom-call | flops 805306368 | tf_op jit(solution)/shard_map/pallas_call | solution.py:231
  97.3 1.3 copy-done
  98.6 5.5 %all-to-all-start.4 = ((bf16[8,512,256]{2,1,0:T(8,128)(2,1)}), bf16[8,512,256]{2,1,0:T(8,128)(2,1)S(1)}, u32[]{:S(2)}, u32[]{:S(2)}) async-start(bf16[8,512,256]{2,1,0:T(8,128)(2,1)} %copy-done), calls=%async_computation.4 | async-start | bytes 4194304 | tf_op jit(solution)/shard_map/all_to_all | solution.py:235
  104.1 5.2 %collective-permute-start.1 = (bf16[24,2048]{1,0:T(8,128)(2,1)S(1)}, bf16[24,2048]{1,0:T(8,128)(2,1)S(1)}, u32[]{:S(2)}, u32[]{:S(2)}) collective-permute-start(bf16[24,2048]{1,0:T(8,128)(2,1)S(1)} %shard_map.91.a_ref), channel_id=1, source_target_pairs={{0,128},{16,400},{128,0},{144,272},{256,384},{272,144},{384,256},{... | collective-permute-start | bytes 294920 | tf_op jit(solution)/shard_map/ppermute | solution.py:166
  109.3 5.2 %collective-permute-done.1.b_ref = bf16[24,2048]{1,0:T(8,128)(2,1)S(1)} collective-permute-done((bf16[24,2048]{1,0:T(8,128)(2,1)S(1)}, bf16[24,2048]{1,0:T(8,128)(2,1)S(1)}, u32[]{:S(2)}, u32[]{:S(2)}) %collective-permute-start.1) | collective-permute-done | bytes 98336 | tf_op jit(solution)/shard_map/ppermute | solution.py:166
  114.5 4.8 %collective-permute-start.2 = (bf16[48,2048]{1,0:T(8,128)(2,1)S(1)}, bf16[48,2048]{1,0:T(8,128)(2,1)S(1)}, u32[]{:S(2)}, u32[]{:S(2)}) collective-permute-start(bf16[48,2048]{1,0:T(8,128)(2,1)S(1)} %shard_map.92.a_ref), channel_id=1, source_target_pairs={{0,384},{16,144},{128,256},{144,16},{256,128},{272,400},{384,0},{4... | collective-permute-start | bytes 589832 | tf_op jit(solution)/shard_map/ppermute | solution.py:166
  119.3 8.0 %collective-permute-done.2.b_ref = bf16[48,2048]{1,0:T(8,128)(2,1)S(1)} collective-permute-done((bf16[48,2048]{1,0:T(8,128)(2,1)S(1)}, bf16[48,2048]{1,0:T(8,128)(2,1)S(1)}, u32[]{:S(2)}, u32[]{:S(2)}) %collective-permute-start.2) | collective-permute-done | bytes 196640 | tf_op jit(solution)/shard_map/ppermute | solution.py:166
  127.3 1.9 %collective-permute-start.3 = (bf16[96,2048]{1,0:T(8,128)(2,1)S(1)}, bf16[96,2048]{1,0:T(8,128)(2,1)S(1)}, u32[]{:S(2)}, u32[]{:S(2)}) collective-permute-start(bf16[96,2048]{1,0:T(8,128)(2,1)S(1)} %shard_map.93.a_ref), channel_id=1, source_target_pairs={{0,32},{16,112},{32,0},{48,80},{64,96},{80,48},{96,64},{112,16},{1... | collective-permute-start | bytes 1179656 | tf_op jit(solution)/shard_map/ppermute | solution.py:166
  129.3 7.8 %collective-permute-done.3.b_ref = bf16[96,2048]{1,0:T(8,128)(2,1)S(1)} collective-permute-done((bf16[96,2048]{1,0:T(8,128)(2,1)S(1)}, bf16[96,2048]{1,0:T(8,128)(2,1)S(1)}, u32[]{:S(2)}, u32[]{:S(2)}) %collective-permute-start.3) | collective-permute-done | bytes 393248 | tf_op jit(solution)/shard_map/ppermute | solution.py:166
  137.1 1.9 %collective-permute-start.4 = (bf16[192,2048]{1,0:T(8,128)(2,1)S(1)}, bf16[192,2048]{1,0:T(8,128)(2,1)S(1)}, u32[]{:S(2)}, u32[]{:S(2)}) collective-permute-start(bf16[192,2048]{1,0:T(8,128)(2,1)S(1)} %shard_map.94.first_ref), channel_id=1, source_target_pairs={{0,96},{16,48},{32,64},{48,16},{64,32},{80,112},{96,0},{112,80},{1... | collective-permute-start | bytes 2359304 | tf_op jit(solution)/shard_map/ppermute | solution.py:166
  139.1 4.4 %collective-permute-start = (s32[1,256]{1,0:T(1,128)S(1)}, s32[1,256]{1,0:T(1,128)S(1)}, u32[]{:S(2)}, u32[]{:S(2)}) collective-permute-start(s32[1,256]{1,0:T(1,128)S(1)} %copy-done.5), channel_id=1, source_target_pairs={{0,16},{16,0},{1,17},{17,1},{2,18},{18,2},{3,19},{19,3},{4,20},{20... | collective-permute-start | bytes 3080 | tf_op jit(solution)/shard_map/ppermute | solution.py:207
  144.3 5.9 %collective-permute-done.4.second_ref = bf16[192,2048]{1,0:T(8,128)(2,1)S(1)} collective-permute-done((bf16[192,2048]{1,0:T(8,128)(2,1)S(1)}, bf16[192,2048]{1,0:T(8,128)(2,1)S(1)}, u32[]{:S(2)}, u32[]{:S(2)}) %collective-permute-start.4) | collective-permute-done | bytes 786464 | tf_op jit(solution)/shard_map/ppermute | solution.py:166
  151.1 1.1 copy-done.4
  152.2 3.6 %shard_map.101 = bf16[32,32,384]{2,1,0:T(8,128)(2,1)} custom-call(s32[33]{0:T(128)S(1)} %pad_add_fusion.ord_ref, s32[2,256]{1,0:T(2,128)S(1)} %add_select_fusion.idx_ref, bf16[192,2048]{1,0:T(8,128)(2,1)S(1)} %shard_map.94.first_ref, bf16[192,2048]{1,0:T(8,128)(2,1)S(1)} %copy-done.4, bf16[8,512,256]{2,1,0:T(8,128)(2,1)S(1)} %all-to-all-done.4.hid_ref), custom_call_target="tpu_custom_call" | custom-call | flops 805306368 | tf_op jit(solution)/shard_map/pallas_call | solution.py:237
  155.8 11.2 %all-to-all-start.5 = ((bf16[32,32,384]{2,1,0:T(8,128)(2,1)}), bf16[32,32,384]{2,1,0:T(8,128)(2,1)S(1)}, u32[]{:S(2)}, u32[]{:S(2)}) async-start(bf16[32,32,384]{2,1,0:T(8,128)(2,1)} %shard_map.101), calls=%async_computation.5 | async-start | bytes 1572864 | tf_op jit(solution)/shard_map/all_to_all | solution.py:244
  167.9 20.9 %all-to-all-done.5.in_ref = bf16[32,32,384]{2,1,0:T(8,128)(2,1)S(1)} async-done(((bf16[32,32,384]{2,1,0:T(8,128)(2,1)}), bf16[32,32,384]{2,1,0:T(8,128)(2,1)S(1)}, u32[]{:S(2)}, u32[]{:S(2)}) %all-to-all-start.5) | async-done | bytes 786464 | tf_op jit(solution)/shard_map/all_to_all | solution.py:244
  188.8 1.6 shard_map.102
  (34 shorter events, 4.9 us)
Async XLA Ops:
  11.3 13.8 %collective-permute-start.6 = (bf16[192,512]{1,0:T(8,128)(2,1)S(1)}, bf16[192,512]{1,0:T(8,128)(2,1)S(1)}, u32[]{:S(2)}, u32[]{:S(2)}) collective-permute-start(bf16[192,512]{1,0:T(8,128)(2,1)S(1)} %bitcast.9), channel_id=1, source_target_pairs={{0,128},{16,400},{128,0},{144,272},{256,384},{272,144},{384,256},{... | collective-permute-start | bytes 589832 | tf_op jit(solution)/shard_map/ppermute | solution.py:166
  25.1 7.6 %copy-start.5 = (s32[1,256]{1,0:T(1,128)S(1)}, s32[1,256]{1,0:T(1,128)}, u32[]{:S(2)}) copy-start(s32[1,256]{1,0:T(1,128)} %param.12) | copy-start | bytes 3076
  26.4 38.8 %all-to-all-start.2 = ((bf16[4,384,512]{2,1,0:T(8,128)(2,1)}), bf16[4,384,512]{2,1,0:T(8,128)(2,1)}, u32[]{:S(2)}, u32[]{:S(2)}) async-start(bf16[4,384,512]{2,1,0:T(8,128)(2,1)} %shard_map.97), calls=%async_computation.2 | async-start | bytes 3145728 | tf_op jit(solution)/shard_map/all_to_all | solution.py:179
  32.9 1.9 copy-start.2
  36.1 33.3 %copy-start.6 = (s32[4]{0:T(128)S(1)}, s32[4]{0:T(128)}, u32[]{:S(2)}) copy-start(s32[4]{0:T(128)} %constant.38.clone) | copy-start | bytes 52
  36.1 33.3 %copy-start.7 = (s32[4]{0:T(128)S(1)}, s32[4]{0:T(128)}, u32[]{:S(2)}) copy-start(s32[4]{0:T(128)} %constant.39.clone) | copy-start | bytes 52
  36.2 33.7 %collective-permute-start.5 = (bf16[16,256,256]{2,1,0:T(8,128)(2,1)S(1)}, bf16[16,256,256]{2,1,0:T(8,128)(2,1)}, u32[]{:S(2)}, u32[]{:S(2)}) collective-permute-start(bf16[16,256,256]{2,1,0:T(8,128)(2,1)S(1)} %shard_map.95.own_ref), channel_id=1, source_target_pairs={{0,16},{16,0},{1,17},{17,1},{2,18},{18,2},{3,19},{19,3},{4,20},{20... | collective-permute-start | bytes 6291464 | tf_op jit(solution)/shard_map/ppermute | solution.py:206
  38.1 25.1 %collective-permute-start.7 = (bf16[384,512]{1,0:T(8,128)(2,1)S(1)}, bf16[384,512]{1,0:T(8,128)(2,1)S(1)}, u32[]{:S(2)}, u32[]{:S(2)}) collective-permute-start(bf16[384,512]{1,0:T(8,128)(2,1)S(1)} %shard_map.96.refs_0_), channel_id=1, source_target_pairs={{0,384},{16,144},{128,256},{144,16},{256,128},{272,400},{384,0},{4... | collective-permute-start | bytes 1179656 | tf_op jit(solution)/shard_map/ppermute | solution.py:166
  64.0 1.2 copy-start.1
  65.1 24.5 %all-to-all-start.3 = ((bf16[4,384,512]{2,1,0:T(8,128)(2,1)}), bf16[4,384,512]{2,1,0:T(8,128)(2,1)}, u32[]{:S(2)}, u32[]{:S(2)}) async-start(bf16[4,384,512]{2,1,0:T(8,128)(2,1)} %copy-done.1), calls=%async_computation.3 | async-start | bytes 3145728 | tf_op jit(solution)/shard_map/all_to_all | solution.py:179
  89.6 9.0 %all-to-all-start = ((bf16[4,24,512]{2,1,0:T(8,128)(2,1)}), bf16[4,24,512]{2,1,0:T(8,128)(2,1)S(1)}, u32[]{:S(2)}, u32[]{:S(2)}) async-start(bf16[4,24,512]{2,1,0:T(8,128)(2,1)} %bitcast.2), calls=%async_computation | async-start | bytes 196608 | tf_op jit(solution)/shard_map/all_to_all | solution.py:194
  97.2 1.3 copy-start
  98.6 52.5 %all-to-all-start.4 = ((bf16[8,512,256]{2,1,0:T(8,128)(2,1)}), bf16[8,512,256]{2,1,0:T(8,128)(2,1)S(1)}, u32[]{:S(2)}, u32[]{:S(2)}) async-start(bf16[8,512,256]{2,1,0:T(8,128)(2,1)} %copy-done), calls=%async_computation.4 | async-start | bytes 4194304 | tf_op jit(solution)/shard_map/all_to_all | solution.py:235
  104.1 10.4 %collective-permute-start.1 = (bf16[24,2048]{1,0:T(8,128)(2,1)S(1)}, bf16[24,2048]{1,0:T(8,128)(2,1)S(1)}, u32[]{:S(2)}, u32[]{:S(2)}) collective-permute-start(bf16[24,2048]{1,0:T(8,128)(2,1)S(1)} %shard_map.91.a_ref), channel_id=1, source_target_pairs={{0,128},{16,400},{128,0},{144,272},{256,384},{272,144},{384,256},{... | collective-permute-start | bytes 294920 | tf_op jit(solution)/shard_map/ppermute | solution.py:166
  114.5 12.8 %collective-permute-start.2 = (bf16[48,2048]{1,0:T(8,128)(2,1)S(1)}, bf16[48,2048]{1,0:T(8,128)(2,1)S(1)}, u32[]{:S(2)}, u32[]{:S(2)}) collective-permute-start(bf16[48,2048]{1,0:T(8,128)(2,1)S(1)} %shard_map.92.a_ref), channel_id=1, source_target_pairs={{0,384},{16,144},{128,256},{144,16},{256,128},{272,400},{384,0},{4... | collective-permute-start | bytes 589832 | tf_op jit(solution)/shard_map/ppermute | solution.py:166
  127.3 9.7 %collective-permute-start.3 = (bf16[96,2048]{1,0:T(8,128)(2,1)S(1)}, bf16[96,2048]{1,0:T(8,128)(2,1)S(1)}, u32[]{:S(2)}, u32[]{:S(2)}) collective-permute-start(bf16[96,2048]{1,0:T(8,128)(2,1)S(1)} %shard_map.93.a_ref), channel_id=1, source_target_pairs={{0,32},{16,112},{32,0},{48,80},{64,96},{80,48},{96,64},{112,16},{1... | collective-permute-start | bytes 1179656 | tf_op jit(solution)/shard_map/ppermute | solution.py:166
  137.1 13.0 %collective-permute-start.4 = (bf16[192,2048]{1,0:T(8,128)(2,1)S(1)}, bf16[192,2048]{1,0:T(8,128)(2,1)S(1)}, u32[]{:S(2)}, u32[]{:S(2)}) collective-permute-start(bf16[192,2048]{1,0:T(8,128)(2,1)S(1)} %shard_map.94.first_ref), channel_id=1, source_target_pairs={{0,96},{16,48},{32,64},{48,16},{64,32},{80,112},{96,0},{112,80},{1... | collective-permute-start | bytes 2359304 | tf_op jit(solution)/shard_map/ppermute | solution.py:166
  139.1 5.2 %collective-permute-start = (s32[1,256]{1,0:T(1,128)S(1)}, s32[1,256]{1,0:T(1,128)S(1)}, u32[]{:S(2)}, u32[]{:S(2)}) collective-permute-start(s32[1,256]{1,0:T(1,128)S(1)} %copy-done.5), channel_id=1, source_target_pairs={{0,16},{16,0},{1,17},{17,1},{2,18},{18,2},{3,19},{19,3},{4,20},{20... | collective-permute-start | bytes 3080 | tf_op jit(solution)/shard_map/ppermute | solution.py:207
  150.2 0.9 copy-start.3
  151.1 1.1 copy-start.4
  155.8 33.0 %all-to-all-start.5 = ((bf16[32,32,384]{2,1,0:T(8,128)(2,1)}), bf16[32,32,384]{2,1,0:T(8,128)(2,1)S(1)}, u32[]{:S(2)}, u32[]{:S(2)}) async-start(bf16[32,32,384]{2,1,0:T(8,128)(2,1)} %shard_map.101), calls=%async_computation.5 | async-start | bytes 1572864 | tf_op jit(solution)/shard_map/all_to_all | solution.py:244

commit v3 on v2

--- a/solution.py
+++ b/solution.py
@@ -83,14 +83,14 @@
             cols.append((gate / (1.0 + jnp.exp(-gate)) * up).astype(BF))
         at = pl.multiple_of((core if n == 0 else 1 - core) * caps, caps)
         res_ref[pl.ds(at, caps), :] = jnp.concatenate(cols, axis=1)
-    copies = [pltpu.make_async_copy(res_ref, out_ref.at[g], sems.at[g]) for g in range(8)]
+    copies = [pltpu.make_async_copy(res_ref, out_ref.at[g], sems.at[g]) for g in range(4)]
     for copy in copies:
         copy.start()
     for copy in copies:
         copy.wait()
 
 
-def down_body(ord_ref, idx_ref, first_ref, second_ref, hid_ref, out_ref, scr, second_vmem, sem):
+def down_body(ord_ref, idx_ref, first_ref, second_ref, hid_ref, mate_ref, out_ref, scr, second_vmem, sem):
     caps = idx_ref.shape[1]
     rows, unit = 512, 24
     fetch = pltpu.make_async_copy(second_ref, second_vmem, sem)
@@ -99,10 +99,11 @@
         if n == 1:
             fetch.wait()
         acc = None
-        for g in range(8):
-            lo = 512 * (g % 4) + 256 * (g // 4)
-            part = dot_nt(w_ref[:, lo : lo + 256], hid_ref[g])
-            acc = part if acc is None else acc + part
+        for core, h_ref in ((ord_ref[32], hid_ref), (1 - ord_ref[32], mate_ref)):
+            for x in range(4):
+                lo = pl.multiple_of(512 * x + 256 * core, 256)
+                part = dot_nt(w_ref[:, pl.ds(lo, 256)], h_ref[x])
+                acc = part if acc is None else acc + part
         for k in range(8):
             at = pl.multiple_of(ord_ref[16 + 8 * n + k] * unit, 8)
             scr[pl.ds(at, unit), :] = acc[k * unit : (k + 1) * unit, :]
@@ -170,7 +171,7 @@
     rows, cols = sum(p.shape[0] for p in parts), parts[0].shape[1]
     wide = call(
         spread_body,
-        jax.ShapeDtypeStruct((4, rows, cols), BF),
+        pltpu.HBM((4, rows, cols), BF),
         [vm()] * len(parts),
         scratch=[pltpu.SemaphoreType.DMA((len(parts), 4))],
         mib=4,
@@ -229,18 +230,19 @@
         early_body, jax.ShapeDtypeStruct((512, 512), F32), [sm()] + [vm()] * 3, flops=512 * 3072 * 512
     )(order, rows, rows_mate, yab)
     wide = call(
-        hidden_body, jax.ShapeDtypeStruct((8, 512, 256), BF), [sm()] + [vm()] * 4, flops=512 * 3072 * 512,
-        scratch=[pltpu.VMEM((512, 256), BF), pltpu.SemaphoreType.DMA((8,))], to=hb,
+        hidden_body, pltpu.HBM((4, 512, 256), BF), [sm()] + [vm()] * 4, flops=512 * 3072 * 512,
+        scratch=[pltpu.VMEM((512, 256), BF), pltpu.SemaphoreType.DMA((4,))], to=hb,
     )(order, rows, rows_mate, early, yc)
-    hid = lax.all_to_all(wide, ("c", "x"), 0, 0, tiled=True)
+    hid = lax.all_to_all(wide, "x", 0, 0, tiled=True)
+    hid_mate = lax.ppermute(hid, "c", swap)
 
     parts = call(
         down_body,
         jax.ShapeDtypeStruct((32, 32, 384), BF),
-        [sm(), vm(), vm(), hb(), vm()],
+        [sm(), vm(), vm(), hb(), vm(), vm()],
         scratch=[pltpu.VMEM((384, 512), F32), pltpu.VMEM((192, 2048), BF), pltpu.SemaphoreType.DMA],
         flops=2 * 512 * 384 * 2048,
-    )(order, index_both, down_first, down_second, hid)
+    )(order, index_both, down_first, down_second, hid, hid_mate)
     owned = lax.all_to_all(parts, ("c", "zl", "x"), 0, 0, tiled=True)
 
     start = (zl * 4 + x) * 32

time: 191 us -> 191 us (level)
  starting transfers between devices: 64.6 us -> 78.3 us
  waiting for transfers between devices: 91 us -> 80.3 us
  local copies, waits for them, and re-layouts: 7.67 us -> 3.17 us
    ppermute x6, waiting for transfers between devices: 52.8 us -> 41.8 us  [meet(): return lax.ppermute(value, (axis, 'c'), pairs(step))]
    ppermute x0 -> x1, starting transfers between devices: none -> 8.5 us  [shards(): hid_mate = lax.ppermute(hid, 'c', swap)]
    all_to_all x1, starting transfers between devices: 11.2 us -> 16.5 us  [shards(): owned = lax.all_to_all(parts, ('c', 'zl', 'x'), 0, 0, tiled=True)]
    unnamed x16 -> x8, local copies, waits for them, and re-layouts: 6.41 us -> 1.91 us
    ppermute x1, starting transfers between devices: 4.42 us -> 6.45 us  [shards(): index_mate = lax.ppermute(index_list, 'c', swap)]
  transfers between devices with their start and end apart: 13 -> 14, of which waited for: 9 -> 9; matrix products, arithmetic and copies ran while one was open for 1% -> 1% of each run, Pallas kernels for 5% -> 5%
where the time goes in v3:
time: 191 us; the launch traced here: 190 us
  waiting for transfers between devices  80.3 us (42%)
  starting transfers between devices  78.3 us (41%)
  Pallas kernels  16.7 us (9%)
  blocking collectives  10.4 us (5%)
  local copies, waits for them, and re-layouts  3.17 us (2%)
    ppermute x6, waiting for transfers between devices, meet(): return lax.ppermute(value, (axis, 'c'), pairs(step))  41.8 us
    ppermute x6, starting transfers between devices, meet(): return lax.ppermute(value, (axis, 'c'), pairs(step))  26.2 us
    all_to_all x1, waiting for transfers between devices, shards(): owned = lax.all_to_all(parts, ('c', 'zl', 'x'), 0, 0, tiled=True)  20.9 us
    all_to_all x1, starting transfers between devices, shards(): owned = lax.all_to_all(parts, ('c', 'zl', 'x'), 0, 0, tiled=True)  16.5 us
    all_to_all x2, waiting for transfers between devices, over_y(): return lax.all_to_all(wide, 'y', 0, 0, tiled=True)  16.5 us
    all_to_all x2, starting transfers between devices, over_y(): return lax.all_to_all(wide, 'y', 0, 0, tiled=True)  10.7 us
    all_to_all x1, blocking collectives, shards(): lax.all_to_all(jnp.concatenate(mine, axis=0), 'c', 0, 0, tiled=True)  10.4 us
    ppermute x1, starting transfers between devices, shards(): hid_mate = lax.ppermute(hid, 'c', swap)  8.5 us
  transfers between devices with their start and end apart: 14, of which 9 were waited for; matrix products, arithmetic and copies ran while one was open for 1% of the time, Pallas kernels for 5%

profile of v3, /device:TPU:1, one launch (start us, length us, event | category | flops | bytes accessed | tf_op | source)
XLA Modules:
  0.0 190.1 jit_solution(3410863025881049027)
XLA Ops:
  0.0 0.9 fusion.2
  0.9 10.4 %all_to_all.42 = bf16[2,96,512]{2,1,0:T(8,128)(2,1)S(1)} all-to-all(bf16[2,96,512]{2,1,0:T(8,128)(2,1)S(1)} %bitcast.12), channel_id=1, replica_groups=mesh['zh'=4,'y'=4,'c'=2,'zl'=4,'x'=4] {'c'}, dimensions={0} | all-to-all | bytes 393216 | tf_op jit(solution)/shard_map/all_to_all | solution.py:192
  11.3 7.1 %collective-permute-start.6 = (bf16[192,512]{1,0:T(8,128)(2,1)S(1)}, bf16[192,512]{1,0:T(8,128)(2,1)S(1)}, u32[]{:S(2)}, u32[]{:S(2)}) collective-permute-start(bf16[192,512]{1,0:T(8,128)(2,1)S(1)} %bitcast.9), channel_id=1, source_target_pairs={{0,128},{16,400},{128,0},{144,272},{256,384},{272,144},{384,256},{... | collective-permute-start | bytes 589832 | tf_op jit(solution)/shard_map/ppermute | solution.py:167
  18.4 6.7 %collective-permute-done.6.b_ref = bf16[192,512]{1,0:T(8,128)(2,1)S(1)} collective-permute-done((bf16[192,512]{1,0:T(8,128)(2,1)S(1)}, bf16[192,512]{1,0:T(8,128)(2,1)S(1)}, u32[]{:S(2)}, u32[]{:S(2)}) %collective-permute-start.6) | collective-permute-done | bytes 196640 | tf_op jit(solution)/shard_map/ppermute | solution.py:167
  25.1 1.2 shard_map.97
  26.4 6.4 %all-to-all-start.2 = ((bf16[4,384,512]{2,1,0:T(8,128)(2,1)}), bf16[4,384,512]{2,1,0:T(8,128)(2,1)}, u32[]{:S(2)}, u32[]{:S(2)}) async-start(bf16[4,384,512]{2,1,0:T(8,128)(2,1)} %shard_map.97), calls=%async_computation.2 | async-start | bytes 3145728 | tf_op jit(solution)/shard_map/all_to_all | solution.py:180
  32.9 1.9 copy-done
  34.8 1.3 shard_map.95.own_ref
  36.1 1.9 %collective-permute-start.5 = (bf16[16,256,256]{2,1,0:T(8,128)(2,1)S(1)}, bf16[16,256,256]{2,1,0:T(8,128)(2,1)}, u32[]{:S(2)}, u32[]{:S(2)}) collective-permute-start(bf16[16,256,256]{2,1,0:T(8,128)(2,1)S(1)} %shard_map.95.own_ref), channel_id=1, source_target_pairs={{0,16},{16,0},{1,17},{17,1},{2,18},{18,2},{3,19},{19,3},{4,20},{20... | collective-permute-start | bytes 6291464 | tf_op jit(solution)/shard_map/ppermute | solution.py:207
  38.1 5.8 %collective-permute-start.7 = (bf16[384,512]{1,0:T(8,128)(2,1)S(1)}, bf16[384,512]{1,0:T(8,128)(2,1)S(1)}, u32[]{:S(2)}, u32[]{:S(2)}) collective-permute-start(bf16[384,512]{1,0:T(8,128)(2,1)S(1)} %shard_map.96.refs_0_), channel_id=1, source_target_pairs={{0,384},{16,144},{128,256},{144,16},{256,128},{272,400},{384,0},{4... | collective-permute-start | bytes 1179656 | tf_op jit(solution)/shard_map/ppermute | solution.py:167
  43.9 19.3 %collective-permute-done.7.refs_0_ = bf16[384,512]{1,0:T(8,128)(2,1)S(1)} collective-permute-done((bf16[384,512]{1,0:T(8,128)(2,1)S(1)}, bf16[384,512]{1,0:T(8,128)(2,1)S(1)}, u32[]{:S(2)}, u32[]{:S(2)}) %collective-permute-start.7) | collective-permute-done | bytes 393248 | tf_op jit(solution)/shard_map/ppermute | solution.py:167
  63.1 1.2 shard_map.99
  64.4 4.3 %all-to-all-start.3 = ((bf16[4,384,512]{2,1,0:T(8,128)(2,1)}), bf16[4,384,512]{2,1,0:T(8,128)(2,1)}, u32[]{:S(2)}, u32[]{:S(2)}) async-start(bf16[4,384,512]{2,1,0:T(8,128)(2,1)} %shard_map.99), calls=%async_computation.3 | async-start | bytes 3145728 | tf_op jit(solution)/shard_map/all_to_all | solution.py:180
  69.1 3.3 %shard_map.98.early_ref = f32[512,512]{1,0:T(8,128)S(1)} custom-call(s32[33]{0:T(128)S(1)} %pad_add_fusion.ord_ref, bf16[16,256,256]{2,1,0:T(8,128)(2,1)S(1)} %shard_map.95.own_ref, bf16[16,256,256]{2,1,0:T(8,128)(2,1)} %collective-permute-done.5.mate_ref, bf16[4,384,512]{2,1,0:T(8,128)(2,1)} %all-to-all-done.2.ab_ref), custom_call_target="tpu_custom_call" | custom-call | flops 805306368 | tf_op jit(solution)/shard_map/pallas_call | solution.py:229
  72.4 16.5 %all-to-all-done.3.c_ref = bf16[4,384,512]{2,1,0:T(8,128)(2,1)} async-done(((bf16[4,384,512]{2,1,0:T(8,128)(2,1)}), bf16[4,384,512]{2,1,0:T(8,128)(2,1)}, u32[]{:S(2)}, u32[]{:S(2)}) %all-to-all-start.3) | async-done | bytes 1572896 | tf_op jit(solution)/shard_map/all_to_all | solution.py:180
  88.9 4.1 %all-to-all-start = ((bf16[4,24,512]{2,1,0:T(8,128)(2,1)}), bf16[4,24,512]{2,1,0:T(8,128)(2,1)S(1)}, u32[]{:S(2)}, u32[]{:S(2)}) async-start(bf16[4,24,512]{2,1,0:T(8,128)(2,1)} %bitcast.2), calls=%async_computation | async-start | bytes 196608 | tf_op jit(solution)/shard_map/all_to_all | solution.py:195
  92.9 4.3 %shard_map.100 = bf16[4,512,256]{2,1,0:T(8,128)(2,1)} custom-call(s32[33]{0:T(128)S(1)} %pad_add_fusion.ord_ref, bf16[16,256,256]{2,1,0:T(8,128)(2,1)S(1)} %shard_map.95.own_ref, bf16[16,256,256]{2,1,0:T(8,128)(2,1)} %collective-permute-done.5.mate_ref, f32[512,512]{1,0:T(8,128)S(1)} %shard_map.98.early_ref, bf16[4,384,512]{2,1,0:T(8,128)(2,1)} %all-to-all-done.3.c_ref), custom_call_target="tpu_custom_call" | custom-call | flops 805306368 | tf_op jit(solution)/shard_map/pallas_call | solution.py:232
  97.6 4.0 %all-to-all-start.4 = ((bf16[4,512,256]{2,1,0:T(8,128)(2,1)}), bf16[4,512,256]{2,1,0:T(8,128)(2,1)S(1)}, u32[]{:S(2)}, u32[]{:S(2)}) async-start(bf16[4,512,256]{2,1,0:T(8,128)(2,1)} %shard_map.100), calls=%async_computation.4 | async-start | bytes 2097152 | tf_op jit(solution)/shard_map/all_to_all | solution.py:236
  101.5 2.7 %collective-permute-start.1 = (bf16[24,2048]{1,0:T(8,128)(2,1)S(1)}, bf16[24,2048]{1,0:T(8,128)(2,1)S(1)}, u32[]{:S(2)}, u32[]{:S(2)}) collective-permute-start(bf16[24,2048]{1,0:T(8,128)(2,1)S(1)} %shard_map.91.a_ref), channel_id=1, source_target_pairs={{0,128},{16,400},{128,0},{144,272},{256,384},{272,144},{384,256},{... | collective-permute-start | bytes 294920 | tf_op jit(solution)/shard_map/ppermute | solution.py:167
  104.2 6.6 %collective-permute-done.1.b_ref = bf16[24,2048]{1,0:T(8,128)(2,1)S(1)} collective-permute-done((bf16[24,2048]{1,0:T(8,128)(2,1)S(1)}, bf16[24,2048]{1,0:T(8,128)(2,1)S(1)}, u32[]{:S(2)}, u32[]{:S(2)}) %collective-permute-start.1) | collective-permute-done | bytes 98336 | tf_op jit(solution)/shard_map/ppermute | solution.py:167
  110.8 4.2 %collective-permute-start.2 = (bf16[48,2048]{1,0:T(8,128)(2,1)S(1)}, bf16[48,2048]{1,0:T(8,128)(2,1)S(1)}, u32[]{:S(2)}, u32[]{:S(2)}) collective-permute-start(bf16[48,2048]{1,0:T(8,128)(2,1)S(1)} %shard_map.92.a_ref), channel_id=1, source_target_pairs={{0,384},{16,144},{128,256},{144,16},{256,128},{272,400},{384,0},{4... | collective-permute-start | bytes 589832 | tf_op jit(solution)/shard_map/ppermute | solution.py:167
  115.0 6.4 %collective-permute-done.2.b_ref = bf16[48,2048]{1,0:T(8,128)(2,1)S(1)} collective-permute-done((bf16[48,2048]{1,0:T(8,128)(2,1)S(1)}, bf16[48,2048]{1,0:T(8,128)(2,1)S(1)}, u32[]{:S(2)}, u32[]{:S(2)}) %collective-permute-start.2) | collective-permute-done | bytes 196640 | tf_op jit(solution)/shard_map/ppermute | solution.py:167
  121.4 2.8 %collective-permute-start.3 = (bf16[96,2048]{1,0:T(8,128)(2,1)S(1)}, bf16[96,2048]{1,0:T(8,128)(2,1)S(1)}, u32[]{:S(2)}, u32[]{:S(2)}) collective-permute-start(bf16[96,2048]{1,0:T(8,128)(2,1)S(1)} %shard_map.93.a_ref), channel_id=1, source_target_pairs={{0,32},{16,112},{32,0},{48,80},{64,96},{80,48},{96,64},{112,16},{1... | collective-permute-start | bytes 1179656 | tf_op jit(solution)/shard_map/ppermute | solution.py:167
  124.2 8.5 %collective-permute-start.8 = (bf16[4,512,256]{2,1,0:T(8,128)(2,1)S(1)}, bf16[4,512,256]{2,1,0:T(8,128)(2,1)S(1)}, u32[]{:S(2)}, u32[]{:S(2)}) collective-permute-start(bf16[4,512,256]{2,1,0:T(8,128)(2,1)S(1)} %all-to-all-done.4.hid_ref), channel_id=1, source_target_pairs={{0,16},{16,0},{1,17},{17,1},{2,18},{18,2},{3,19},{19,3},{4,20},{20... | collective-permute-start | bytes 3145736 | tf_op jit(solution)/shard_map/ppermute | solution.py:237
  132.8 3.6 %collective-permute-start.4 = (bf16[192,2048]{1,0:T(8,128)(2,1)S(1)}, bf16[192,2048]{1,0:T(8,128)(2,1)S(1)}, u32[]{:S(2)}, u32[]{:S(2)}) collective-permute-start(bf16[192,2048]{1,0:T(8,128)(2,1)S(1)} %shard_map.94.first_ref), channel_id=1, source_target_pairs={{0,96},{16,48},{32,64},{48,16},{64,32},{80,112},{96,0},{112,80},{1... | collective-permute-start | bytes 2359304 | tf_op jit(solution)/shard_map/ppermute | solution.py:167
  136.4 6.5 %collective-permute-start = (s32[1,256]{1,0:T(1,128)S(1)}, s32[1,256]{1,0:T(1,128)S(1)}, u32[]{:S(2)}, u32[]{:S(2)}) collective-permute-start(s32[1,256]{1,0:T(1,128)S(1)} %copy-done.1), channel_id=1, source_target_pairs={{0,16},{16,0},{1,17},{17,1},{2,18},{18,2},{3,19},{19,3},{4,20},{20... | collective-permute-start | bytes 3080 | tf_op jit(solution)/shard_map/ppermute | solution.py:208
  142.9 0.8 collective-permute-done
  143.7 2.9 %collective-permute-done.4.second_ref = bf16[192,2048]{1,0:T(8,128)(2,1)S(1)} collective-permute-done((bf16[192,2048]{1,0:T(8,128)(2,1)S(1)}, bf16[192,2048]{1,0:T(8,128)(2,1)S(1)}, u32[]{:S(2)}, u32[]{:S(2)}) %collective-permute-start.4) | collective-permute-done | bytes 786464 | tf_op jit(solution)/shard_map/ppermute | solution.py:167
  146.6 3.6 %shard_map.101 = bf16[32,32,384]{2,1,0:T(8,128)(2,1)} custom-call(s32[33]{0:T(128)S(1)} %pad_add_fusion.ord_ref, s32[2,256]{1,0:T(2,128)S(1)} %add_select_fusion.idx_ref, bf16[192,2048]{1,0:T(8,128)(2,1)S(1)} %shard_map.94.first_ref, bf16[192,2048]{1,0:T(8,128)(2,1)S(1)} %collective-permute-done.4.second_ref, ...), custom_call_target="tpu_custom_call" | custom-call | flops 805306368 | tf_op jit(solution)/shard_map/pallas_call | solution.py:239
  150.2 16.5 %all-to-all-start.5 = ((bf16[32,32,384]{2,1,0:T(8,128)(2,1)}), bf16[32,32,384]{2,1,0:T(8,128)(2,1)S(1)}, u32[]{:S(2)}, u32[]{:S(2)}) async-start(bf16[32,32,384]{2,1,0:T(8,128)(2,1)} %shard_map.101), calls=%async_computation.5 | async-start | bytes 1572864 | tf_op jit(solution)/shard_map/all_to_all | solution.py:246
  167.6 20.9 %all-to-all-done.5.in_ref = bf16[32,32,384]{2,1,0:T(8,128)(2,1)S(1)} async-done(((bf16[32,32,384]{2,1,0:T(8,128)(2,1)}), bf16[32,32,384]{2,1,0:T(8,128)(2,1)S(1)}, u32[]{:S(2)}, u32[]{:S(2)}) %all-to-all-start.5) | async-done | bytes 786464 | tf_op jit(solution)/shard_map/all_to_all | solution.py:246
  188.5 1.6 shard_map.102
  (28 shorter events, 1.8 us)
Async XLA Ops:
  11.3 13.8 %collective-permute-start.6 = (bf16[192,512]{1,0:T(8,128)(2,1)S(1)}, bf16[192,512]{1,0:T(8,128)(2,1)S(1)}, u32[]{:S(2)}, u32[]{:S(2)}) collective-permute-start(bf16[192,512]{1,0:T(8,128)(2,1)S(1)} %bitcast.9), channel_id=1, source_target_pairs={{0,128},{16,400},{128,0},{144,272},{256,384},{272,144},{384,256},{... | collective-permute-start | bytes 589832 | tf_op jit(solution)/shard_map/ppermute | solution.py:167
  26.3 6.4 %copy-start.1 = (s32[1,256]{1,0:T(1,128)S(1)}, s32[1,256]{1,0:T(1,128)}, u32[]{:S(2)}) copy-start(s32[1,256]{1,0:T(1,128)} %param.12) | copy-start | bytes 3076
  26.4 38.0 %all-to-all-start.2 = ((bf16[4,384,512]{2,1,0:T(8,128)(2,1)}), bf16[4,384,512]{2,1,0:T(8,128)(2,1)}, u32[]{:S(2)}, u32[]{:S(2)}) async-start(bf16[4,384,512]{2,1,0:T(8,128)(2,1)} %shard_map.97), calls=%async_computation.2 | async-start | bytes 3145728 | tf_op jit(solution)/shard_map/all_to_all | solution.py:180
  32.9 1.9 copy-start
  36.1 33.0 %collective-permute-start.5 = (bf16[16,256,256]{2,1,0:T(8,128)(2,1)S(1)}, bf16[16,256,256]{2,1,0:T(8,128)(2,1)}, u32[]{:S(2)}, u32[]{:S(2)}) collective-permute-start(bf16[16,256,256]{2,1,0:T(8,128)(2,1)S(1)} %shard_map.95.own_ref), channel_id=1, source_target_pairs={{0,16},{16,0},{1,17},{17,1},{2,18},{18,2},{3,19},{19,3},{4,20},{20... | collective-permute-start | bytes 6291464 | tf_op jit(solution)/shard_map/ppermute | solution.py:207
  38.1 25.1 %collective-permute-start.7 = (bf16[384,512]{1,0:T(8,128)(2,1)S(1)}, bf16[384,512]{1,0:T(8,128)(2,1)S(1)}, u32[]{:S(2)}, u32[]{:S(2)}) collective-permute-start(bf16[384,512]{1,0:T(8,128)(2,1)S(1)} %shard_map.96.refs_0_), channel_id=1, source_target_pairs={{0,384},{16,144},{128,256},{144,16},{256,128},{272,400},{384,0},{4... | collective-permute-start | bytes 1179656 | tf_op jit(solution)/shard_map/ppermute | solution.py:167
  64.3 4.4 %copy-start.2 = (s32[4]{0:T(128)S(1)}, s32[4]{0:T(128)}, u32[]{:S(2)}) copy-start(s32[4]{0:T(128)} %constant.38.clone) | copy-start | bytes 52
  64.3 4.4 %copy-start.3 = (s32[4]{0:T(128)S(1)}, s32[4]{0:T(128)}, u32[]{:S(2)}) copy-start(s32[4]{0:T(128)} %constant.39.clone) | copy-start | bytes 52
  64.4 24.5 %all-to-all-start.3 = ((bf16[4,384,512]{2,1,0:T(8,128)(2,1)}), bf16[4,384,512]{2,1,0:T(8,128)(2,1)}, u32[]{:S(2)}, u32[]{:S(2)}) async-start(bf16[4,384,512]{2,1,0:T(8,128)(2,1)} %shard_map.99), calls=%async_computation.3 | async-start | bytes 3145728 | tf_op jit(solution)/shard_map/all_to_all | solution.py:180
  88.9 8.7 %all-to-all-start = ((bf16[4,24,512]{2,1,0:T(8,128)(2,1)}), bf16[4,24,512]{2,1,0:T(8,128)(2,1)S(1)}, u32[]{:S(2)}, u32[]{:S(2)}) async-start(bf16[4,24,512]{2,1,0:T(8,128)(2,1)} %bitcast.2), calls=%async_computation | async-start | bytes 196608 | tf_op jit(solution)/shard_map/all_to_all | solution.py:195
  97.6 26.6 %all-to-all-start.4 = ((bf16[4,512,256]{2,1,0:T(8,128)(2,1)}), bf16[4,512,256]{2,1,0:T(8,128)(2,1)S(1)}, u32[]{:S(2)}, u32[]{:S(2)}) async-start(bf16[4,512,256]{2,1,0:T(8,128)(2,1)} %shard_map.100), calls=%async_computation.4 | async-start | bytes 2097152 | tf_op jit(solution)/shard_map/all_to_all | solution.py:236
  101.5 9.3 %collective-permute-start.1 = (bf16[24,2048]{1,0:T(8,128)(2,1)S(1)}, bf16[24,2048]{1,0:T(8,128)(2,1)S(1)}, u32[]{:S(2)}, u32[]{:S(2)}) collective-permute-start(bf16[24,2048]{1,0:T(8,128)(2,1)S(1)} %shard_map.91.a_ref), channel_id=1, source_target_pairs={{0,128},{16,400},{128,0},{144,272},{256,384},{272,144},{384,256},{... | collective-permute-start | bytes 294920 | tf_op jit(solution)/shard_map/ppermute | solution.py:167
  110.8 10.5 %collective-permute-start.2 = (bf16[48,2048]{1,0:T(8,128)(2,1)S(1)}, bf16[48,2048]{1,0:T(8,128)(2,1)S(1)}, u32[]{:S(2)}, u32[]{:S(2)}) collective-permute-start(bf16[48,2048]{1,0:T(8,128)(2,1)S(1)} %shard_map.92.a_ref), channel_id=1, source_target_pairs={{0,384},{16,144},{128,256},{144,16},{256,128},{272,400},{384,0},{4... | collective-permute-start | bytes 589832 | tf_op jit(solution)/shard_map/ppermute | solution.py:167
  121.4 11.3 %collective-permute-start.3 = (bf16[96,2048]{1,0:T(8,128)(2,1)S(1)}, bf16[96,2048]{1,0:T(8,128)(2,1)S(1)}, u32[]{:S(2)}, u32[]{:S(2)}) collective-permute-start(bf16[96,2048]{1,0:T(8,128)(2,1)S(1)} %shard_map.93.a_ref), channel_id=1, source_target_pairs={{0,32},{16,112},{32,0},{48,80},{64,96},{80,48},{96,64},{112,16},{1... | collective-permute-start | bytes 1179656 | tf_op jit(solution)/shard_map/ppermute | solution.py:167
  124.2 22.4 %collective-permute-start.8 = (bf16[4,512,256]{2,1,0:T(8,128)(2,1)S(1)}, bf16[4,512,256]{2,1,0:T(8,128)(2,1)S(1)}, u32[]{:S(2)}, u32[]{:S(2)}) collective-permute-start(bf16[4,512,256]{2,1,0:T(8,128)(2,1)S(1)} %all-to-all-done.4.hid_ref), channel_id=1, source_target_pairs={{0,16},{16,0},{1,17},{17,1},{2,18},{18,2},{3,19},{19,3},{4,20},{20... | collective-permute-start | bytes 3145736 | tf_op jit(solution)/shard_map/ppermute | solution.py:237
  132.8 13.8 %collective-permute-start.4 = (bf16[192,2048]{1,0:T(8,128)(2,1)S(1)}, bf16[192,2048]{1,0:T(8,128)(2,1)S(1)}, u32[]{:S(2)}, u32[]{:S(2)}) collective-permute-start(bf16[192,2048]{1,0:T(8,128)(2,1)S(1)} %shard_map.94.first_ref), channel_id=1, source_target_pairs={{0,96},{16,48},{32,64},{48,16},{64,32},{80,112},{96,0},{112,80},{1... | collective-permute-start | bytes 2359304 | tf_op jit(solution)/shard_map/ppermute | solution.py:167
  136.4 7.3 %collective-permute-start = (s32[1,256]{1,0:T(1,128)S(1)}, s32[1,256]{1,0:T(1,128)S(1)}, u32[]{:S(2)}, u32[]{:S(2)}) collective-permute-start(s32[1,256]{1,0:T(1,128)S(1)} %copy-done.1), channel_id=1, source_target_pairs={{0,16},{16,0},{1,17},{17,1},{2,18},{18,2},{3,19},{19,3},{4,20},{20... | collective-permute-start | bytes 3080 | tf_op jit(solution)/shard_map/ppermute | solution.py:208
  150.2 38.3 %all-to-all-start.5 = ((bf16[32,32,384]{2,1,0:T(8,128)(2,1)}), bf16[32,32,384]{2,1,0:T(8,128)(2,1)S(1)}, u32[]{:S(2)}, u32[]{:S(2)}) async-start(bf16[32,32,384]{2,1,0:T(8,128)(2,1)} %shard_map.101), calls=%async_computation.5 | async-start | bytes 1572864 | tf_op jit(solution)/shard_map/all_to_all | solution.py:246

commit v4 on v3

v4 whole, which is shorter than its diff:
```python
import jax
import jax.numpy as jnp
from jax import lax
from jax.experimental import pallas as pl
from jax.experimental.pallas import tpu as pltpu
from jax.sharding import Mesh, PartitionSpec as P


BF = jnp.bfloat16
F32 = jnp.float32


def vm():
    return pl.BlockSpec(memory_space=pltpu.VMEM)


def sm():
    return pl.BlockSpec(memory_space=pltpu.SMEM)


def hb():
    return pl.BlockSpec(memory_space=pltpu.HBM)


def call(body, out, ins, scratch=(), flops=0, mib=16, to=vm):
    return pl.pallas_call(
        body,
        out_shape=out,
        in_specs=ins,
        out_specs=[to(), to()] if isinstance(out, list) else to(),
        scratch_shapes=scratch,
        cost_estimate=pl.CostEstimate(flops=flops, transcendentals=0, bytes_accessed=0),
        compiler_params=pltpu.CompilerParams(vmem_limit_bytes=mib * 1024 * 1024),
    )


def dot_nn(a, b):
    return lax.dot_general(a, b, (((1,), (0,)), ((), ())), preferred_element_type=F32)


def dot_nt(a, b):
    return lax.dot_general(a, b, (((1,), (1,)), ((), ())), preferred_element_type=F32)


def pick_body(idx_ref, tok_ref, out_ref):
    caps, rows = idx_ref.shape[0], tok_ref.shape[0]
    hot = (lax.broadcasted_iota(jnp.int32, (caps, rows), 1) == idx_ref[...]).astype(BF)
    width = tok_ref.shape[1] // out_ref.shape[0]
    pad = jnp.zeros((caps, out_ref.shape[2] - width), BF)
    for m in range(out_ref.shape[0]):
        out_ref[m, :, :width] = dot_nn(hot, tok_ref[:, m * width : (m + 1) * width]).astype(BF)
        out_ref[m, :, width:] = pad


def lay(ord_ref, own_ref, mate_ref, out_ref, places):
    caps, width = own_ref.shape[1], 192
    for i, k in enumerate(places):
        out_ref[:caps, i * width : (i + 1) * width] = own_ref[ord_ref[k], :, :width]
        out_ref[caps:, i * width : (i + 1) * width] = mate_ref[ord_ref[k], :, :width]


def early_body(ord_ref, own_ref, mate_ref, a_ref, b_ref, out_ref, late_ref, now_ref, then_ref, sum_ref, sems):
    lay(ord_ref, own_ref, mate_ref, then_ref, [4 * q + n for q in range(4) for n in (2, 3)])
    copy = pltpu.make_async_copy(then_ref, late_ref, sems.at[0])
    copy.start()
    lay(ord_ref, own_ref, mate_ref, now_ref, [4 * q + n for n in (0, 1) for q in range(4)])
    half = a_ref.shape[0]
    sum_ref[...] = dot_nn(now_ref[:, :half], a_ref[...]) + dot_nn(now_ref[:, half:], b_ref[...])
    store = pltpu.make_async_copy(sum_ref, out_ref, sems.at[1])
    store.start()
    copy.wait()
    store.wait()


def hidden_body(ord_ref, rows_ref, early_ref, c_ref, out_ref, res_ref, rows_vmem, sum_ref, sems, out_sems):
    caps = rows_ref.shape[0] // 2
    half = rows_ref.shape[1] // 2
    core = ord_ref[32]
    copies = [
        pltpu.make_async_copy(rows_ref.at[:, pl.ds(n * half, half)], rows_vmem.at[:, pl.ds(n * half, half)], sems.at[n])
        for n in range(2)
    ] + [pltpu.make_async_copy(early_ref, sum_ref, sems.at[2])]
    for copy in copies:
        copy.start()
    acc = None
    for n in range(2):
        copies[n].wait()
        part = dot_nn(rows_vmem[:, n * half : (n + 1) * half], c_ref[n * half : (n + 1) * half, :])
        acc = part if acc is None else acc + part
    copies[2].wait()
    acc = acc + sum_ref[...]
    cols = []
    for s in range(2):
        gate = acc[:, 256 * s : 256 * s + 128]
        up = acc[:, 256 * s + 128 : 256 * s + 256]
        cols.append((gate / (1.0 + jnp.exp(-gate)) * up).astype(BF))
    res = jnp.concatenate(cols, axis=1)
    res_ref[pl.ds(pl.multiple_of(core * caps, caps), caps), :] = res[:caps]
    res_ref[pl.ds(pl.multiple_of((1 - core) * caps, caps), caps), :] = res[caps:]
    copies = [pltpu.make_async_copy(res_ref, out_ref.at[g], out_sems.at[g]) for g in range(4)]
    for copy in copies:
        copy.start()
    for copy in copies:
        copy.wait()


def down_body(ord_ref, idx_ref, first_ref, second_ref, hid_ref, mate_ref, out_ref, scr, w_ref, sems):
    caps = idx_ref.shape[1]
    rows, unit, acc = 512, 24, None
    copies = [
        pltpu.make_async_copy(r, w_ref.at[pl.ds(192 * n, 192)], sems.at[n]) for n, r in enumerate((first_ref, second_ref))
    ]
    for copy in copies:
        copy.start()
    for copy in copies:
        copy.wait()
    for core, h_ref in ((ord_ref[32], hid_ref), (1 - ord_ref[32], mate_ref)):
        for x in range(4):
            lo = pl.multiple_of(512 * x + 256 * core, 256)
            part = dot_nt(w_ref[:, pl.ds(lo, 256)], h_ref[x])
            acc = part if acc is None else acc + part
    for k in range(16):
        at = pl.multiple_of(ord_ref[16 + k] * unit, 8)
        scr[pl.ds(at, unit), :] = acc[k * unit : (k + 1) * unit, :]
    for b in range(2):
        hot = (lax.broadcasted_iota(jnp.int32, (rows, caps), 0) == idx_ref[b : b + 1, :]).astype(BF)
        dense = dot_nt(hot, scr[:, b * caps : (b + 1) * caps].astype(BF)).astype(BF)
        for n in range(16):
            out_ref[16 * b + n] = dense[32 * n : 32 * n + 32, :]


def spread_body(*refs):
    out_ref, sems = refs[-2], refs[-1]
    lo, copies = 0, []
    for n, r in enumerate(refs[:-2]):
        rows = min(r.shape[0], out_ref.shape[1] - lo)
        for q in range(out_ref.shape[0]):
            copies.append(
                pltpu.make_async_copy(r.at[pl.ds(0, rows)], out_ref.at[q, pl.ds(lo, rows)], sems.at[n, q])
            )
        lo += rows
    for copy in copies:
        copy.start()
    for copy in copies:
        copy.wait()


def quarter_body(own_ref, got_ref, out_ref):
    lo = got_ref.shape[0] - 96
    for x in range(4):
        out_ref[:24, 512 * x : 512 * (x + 1)] = own_ref[24 * x : 24 * (x + 1), :]
        out_ref[24:, 512 * x : 512 * (x + 1)] = got_ref[lo + 24 * x : lo + 24 * (x + 1), :]


def place_body(in_ref, scale_ref, out_ref, scr):
    unit = 24
    for g in range(8):
        core, x = g // 4, g % 4
        acc = in_ref[16 * core + x].astype(F32)
        for q in range(1, 4):
            acc = acc + in_ref[16 * core + 4 * q + x].astype(F32)
        turned = acc.T
        for m in range(16):
            lo = 192 * m + 96 * core + unit * x
            scr[lo : lo + unit, :] = turned[m * unit : (m + 1) * unit, :]
    for n in range(6):
        out_ref[:, n * 512 : (n + 1) * 512] = (scr[n * 512 : (n + 1) * 512, :].T * scale_ref[...]).astype(BF)


def pairs(step):
    flips = ((1, 3), (3, 1))
    return [(2 * i + c, 2 * (i ^ flips[c][step]) + c) for i in range(4) for c in range(2)]


def join_body(*refs):
    lo = 0
    for r in refs[:-1]:
        refs[-1][lo : lo + r.shape[0], :] = r[...]
        lo += r.shape[0]


def join(parts):
    out = jax.ShapeDtypeStruct((sum(p.shape[0] for p in parts), parts[0].shape[1]), BF)
    return call(join_body, out, [vm()] * len(parts), mib=4)(*parts)


def meet(value, axis, step):
    return lax.ppermute(value, (axis, "c"), pairs(step))


def over_y(parts, rows):
    cols = parts[0].shape[1]
    wide = call(
        spread_body,
        pltpu.HBM((4, rows, cols), BF),
        [vm()] * len(parts),
        scratch=[pltpu.SemaphoreType.DMA((len(parts), 4))],
        mib=4,
        to=hb,
    )(*parts)
    return lax.all_to_all(wide, "y", 0, 0, tiled=True)


def shards(tokens, expert_ids, route_weight, index_list, gate_weight, up_weight, down_weight):
    zh, y, c, zl, x = (lax.axis_index(n) for n in ("zh", "y", "c", "zl", "x"))
    caps = index_list.shape[1]

    cut = lambda w, n: w[:, 128 * n : 128 * n + 128]
    mine = [
        jnp.concatenate([cut(w, 2 * h + s) for s in range(2) for w in (gate_weight, up_weight)], axis=1)
        for h in range(2)
    ]
    both_rows = lax.all_to_all(jnp.concatenate(mine, axis=0), "c", 0, 0, tiled=True)

    turned = down_weight.T
    quarter = lax.all_to_all(turned, "x", 0, 0, tiled=True)
    flip = jnp.where(c == 0, jnp.array([0, 1, 3, 2]), jnp.array([0, 3, 1, 2])).astype(jnp.int32)
    order = ((zh ^ flip)[None, :] * 4 + jnp.arange(4, dtype=jnp.int32)[:, None]).reshape(16)
    turned_flip = jnp.where(c == 0, jnp.array([0, 3, 1, 2]), jnp.array([0, 1, 3, 2])).astype(jnp.int32)
    order_down = ((zh ^ turned_flip)[None, :] * 4 + (y ^ flip)[:, None]).reshape(16)
    order = jnp.concatenate([order, order_down, c.reshape(1)]).astype(jnp.int32)

    rows = call(
        pick_body, jax.ShapeDtypeStruct((16, caps, 256), BF), [vm(), vm()], flops=2 * 256 * 512 * 3072
    )(index_list.reshape(caps, 1), tokens)
    swap = [(0, 1), (1, 0)]
    rows_mate = lax.ppermute(rows, "c", swap)
    index_mate = lax.ppermute(index_list, "c", swap)
    index_both = jnp.where(
        c == 0,
        jnp.concatenate([index_list, index_mate], axis=0),
        jnp.concatenate([index_mate, index_list], axis=0),
    )

    near = meet(both_rows, "zh", 0)
    ya = over_y((both_rows,), 192)
    yb = over_y((near,), 192)
    far = meet(join((both_rows, near, quarter)), "zh", 1)
    yc = over_y((far,), 384)
    ya, yb, yc = ya.reshape(768, 512), yb.reshape(768, 512), yc.reshape(1536, 512)

    two = call(quarter_body, jax.ShapeDtypeStruct((48, 2048), BF), [vm()] * 2, mib=4)(quarter, far)
    far = pltpu.with_memory_space_constraint(meet(two, "zh", 0), pltpu.HBM)
    four = join((two, far))
    near = pltpu.with_memory_space_constraint(meet(four, "y", 0), pltpu.HBM)
    down_first = join((four, near))
    down_second = meet(down_first, "y", 1)

    early, rows_late = call(
        early_body,
        [pltpu.HBM((512, 512), F32), pltpu.HBM((512, 1536), BF)],
        [sm()] + [vm()] * 4,
        scratch=[pltpu.VMEM((512, 1536), BF)] * 2 + [pltpu.VMEM((512, 512), F32), pltpu.SemaphoreType.DMA((2,))],
        flops=512 * 3072 * 512,
        to=hb,
    )(order, rows, rows_mate, ya, yb)
    early, rows_late = (pltpu.with_memory_space_constraint(v, pltpu.HBM) for v in (early, rows_late))
    wide = call(
        hidden_body,
        pltpu.HBM((4, 512, 256), BF),
        [sm(), hb(), hb(), vm()],
        scratch=[
            pltpu.VMEM((512, 256), BF),
            pltpu.VMEM((512, 1536), BF),
            pltpu.VMEM((512, 512), F32),
            pltpu.SemaphoreType.DMA((3,)),
            pltpu.SemaphoreType.DMA((4,)),
        ],
        flops=512 * 3072 * 512,
        to=hb,
    )(order, rows_late, early, yc)
    hid = lax.all_to_all(wide, "x", 0, 0, tiled=True)
    hid_mate = lax.ppermute(hid, "c", swap)

    parts = call(
        down_body,
        jax.ShapeDtypeStruct((32, 32, 384), BF),
        [sm(), vm(), hb(), hb(), vm(), vm()],
        scratch=[pltpu.VMEM((384, 512), F32), pltpu.VMEM((384, 2048), BF), pltpu.SemaphoreType.DMA((2,))],
        flops=2 * 512 * 384 * 2048,
    )(order, index_both, down_first, down_second, hid, hid_mate)
    owned = lax.all_to_all(parts, ("c", "zl", "x"), 0, 0, tiled=True)

    start = (zl * 4 + x) * 32
    ids = lax.dynamic_slice_in_dim(expert_ids, start, 32, 0)
    weights = lax.dynamic_slice_in_dim(route_weight, start, 32, 0)
    scale = jnp.sum(jnp.where(ids == 0, weights, jnp.zeros_like(weights)), axis=1, keepdims=True)
    return call(
        place_body, jax.ShapeDtypeStruct((32, 3072), BF), [vm(), vm()], mib=8, scratch=[pltpu.VMEM((3072, 32), F32)]
    )(owned, scale)


def solution(mesh):
    fine = Mesh(mesh.devices.reshape(4, 4, 2, 4, 4), ("zh", "y", "c", "zl", "x"))
    edp, etp = ("zh", "y", "c"), ("zl", "x")
    in_specs = (P(edp, None), P(edp, None), P(edp, None), P(edp, None), P(edp, etp), P(edp, etp), P(etp, edp))

    return jax.shard_map(shards, mesh=fine, in_specs=in_specs, out_specs=P(edp + etp, None), check_vma=False)
```

time: 191 us -> 192 us (level)
  waiting for transfers between devices: 80.3 us -> 73.8 us
  Pallas kernels: 16.7 us -> 20.4 us
  starting transfers between devices: 78.3 us -> 81.5 us
    ppermute x6 -> x5, waiting for transfers between devices: 41.8 us -> 35.8 us  [meet(): return lax.ppermute(value, (axis, 'c'), pairs(step))]
    all_to_all x2 -> x3, waiting for transfers between devices: 16.5 us -> 12.6 us  [over_y(): return lax.all_to_all(wide, 'y', 0, 0, tiled=True)]
    all_to_all x1, waiting for transfers between devices: 0.3 us -> 3.68 us  [shards(): quarter = lax.all_to_all(turned, 'x', 0, 0, tiled=True)]
    ppermute x1, starting transfers between devices: 6.45 us -> 9.8 us  [shards(): index_mate = lax.ppermute(index_list, 'c', swap)]
    pallas_call x8 -> x7, Pallas kernels: 11.4 us -> 14.4 us  [the longest x1 4.98 us: shards(): call(hidden_body, pltpu.HBM((4, 512, 256), BF), [sm(), hb(), hb(), vm()],...]
    all_to_all x2 -> x3, starting transfers between devices: 10.7 us -> 12.7 us  [over_y(): return lax.all_to_all(wide, 'y', 0, 0, tiled=True)]
    ppermute x6 -> x5, starting transfers between devices: 26.2 us -> 25 us  [meet(): return lax.ppermute(value, (axis, 'c'), pairs(step))]
  transfers between devices with their start and end apart: 14 -> 14, of which waited for: 9 -> 7; matrix products, arithmetic and copies ran while one was open for 1% -> 1% of each run, Pallas kernels for 5% -> 6%
where the time goes in v4:
time: 192 us; the launch traced here: 191 us
  starting transfers between devices  81.5 us (42%)
  waiting for transfers between devices  73.8 us (38%)
  Pallas kernels  20.4 us (11%)
  blocking collectives  10.4 us (5%)
  local copies, waits for them, and re-layouts  3.86 us (2%)
    ppermute x5, waiting for transfers between devices, meet(): return lax.ppermute(value, (axis, 'c'), pairs(step))  35.8 us
    ppermute x5, starting transfers between devices, meet(): return lax.ppermute(value, (axis, 'c'), pairs(step))  25 us
    all_to_all x1, waiting for transfers between devices, shards(): owned = lax.all_to_all(parts, ('c', 'zl', 'x'), 0, 0, tiled=True)  20.9 us
    all_to_all x1, starting transfers between devices, shards(): owned = lax.all_to_all(parts, ('c', 'zl', 'x'), 0, 0, tiled=True)  16.4 us
    all_to_all x3, starting transfers between devices, over_y(): return lax.all_to_all(wide, 'y', 0, 0, tiled=True)  12.7 us
    all_to_all x3, waiting for transfers between devices, over_y(): return lax.all_to_all(wide, 'y', 0, 0, tiled=True)  12.6 us
    all_to_all x1, blocking collectives, shards(): lax.all_to_all(jnp.concatenate(mine, axis=0), 'c', 0, 0, tiled=True)  10.4 us
    ppermute x1, starting transfers between devices, shards(): index_mate = lax.ppermute(index_list, 'c', swap)  9.8 us
  transfers between devices with their start and end apart: 14, of which 7 were waited for; matrix products, arithmetic and copies ran while one was open for 1% of the time, Pallas kernels for 6%

profile of v4, /device:TPU:1, one launch (start us, length us, event | category | flops | bytes accessed | tf_op | source)
XLA Modules:
  0.0 191.2 jit_solution(7573465988177049638)
XLA Ops:
  0.9 10.4 %all_to_all.47 = bf16[2,96,512]{2,1,0:T(8,128)(2,1)S(1)} all-to-all(bf16[2,96,512]{2,1,0:T(8,128)(2,1)S(1)} %bitcast.18), channel_id=1, replica_groups=mesh['zh'=4,'y'=4,'c'=2,'zl'=4,'x'=4] {'c'}, dimensions={0} | all-to-all | bytes 393216 | tf_op jit(solution)/shard_map/all_to_all | solution.py:213
  11.3 3.3 %all-to-all-start = ((bf16[4,24,512]{2,1,0:T(8,128)(2,1)}), bf16[4,24,512]{2,1,0:T(8,128)(2,1)S(1)}, u32[]{:S(2)}, u32[]{:S(2)}) async-start(bf16[4,24,512]{2,1,0:T(8,128)(2,1)} %bitcast.19), calls=%async_computation | async-start | bytes 196608 | tf_op jit(solution)/shard_map/all_to_all | solution.py:216
  14.6 0.9 shard_map.114
  15.5 3.7 %all-to-all-done = bf16[4,24,512]{2,1,0:T(8,128)(2,1)S(1)} async-done(((bf16[4,24,512]{2,1,0:T(8,128)(2,1)}), bf16[4,24,512]{2,1,0:T(8,128)(2,1)S(1)}, u32[]{:S(2)}, u32[]{:S(2)}) %all-to-all-start) | async-done | bytes 98336 | tf_op jit(solution)/shard_map/all_to_all | solution.py:216
  19.2 3.5 %all-to-all-start.2 = ((bf16[4,192,512]{2,1,0:T(8,128)(2,1)}), bf16[4,192,512]{2,1,0:T(8,128)(2,1)S(1)}, u32[]{:S(2)}, u32[]{:S(2)}) async-start(bf16[4,192,512]{2,1,0:T(8,128)(2,1)} %shard_map.114), calls=%async_computation.2 | async-start | bytes 1572864 | tf_op jit(solution)/shard_map/all_to_all | solution.py:201
  22.9 1.9 copy-done
  24.8 1.3 shard_map.113.own_ref
  26.1 3.4 %collective-permute-start.6 = (bf16[16,256,256]{2,1,0:T(8,128)(2,1)S(1)}, bf16[16,256,256]{2,1,0:T(8,128)(2,1)}, u32[]{:S(2)}, u32[]{:S(2)}) collective-permute-start(bf16[16,256,256]{2,1,0:T(8,128)(2,1)S(1)} %shard_map.113.own_ref), channel_id=1, source_target_pairs={{0,16},{16,0},{1,17},{17,1},{2,18},{18,2},{3,19},{19,3},{4,20},{20... | collective-permute-start | bytes 6291464 | tf_op jit(solution)/shard_map/ppermute | solution.py:227
  29.5 9.1 %collective-permute-start.1 = (bf16[192,512]{1,0:T(8,128)(2,1)S(1)}, bf16[192,512]{1,0:T(8,128)(2,1)S(1)}, u32[]{:S(2)}, u32[]{:S(2)}) collective-permute-start(bf16[192,512]{1,0:T(8,128)(2,1)S(1)} %bitcast.14), channel_id=1, source_target_pairs={{0,128},{16,400},{128,0},{144,272},{256,384},{272,144},{384,256},{... | collective-permute-start | bytes 589832 | tf_op jit(solution)/shard_map/ppermute | solution.py:188
  38.6 6.5 %collective-permute-done.1.refs_1_.refs_0_ = bf16[192,512]{1,0:T(8,128)(2,1)S(1)} collective-permute-done((bf16[192,512]{1,0:T(8,128)(2,1)S(1)}, bf16[192,512]{1,0:T(8,128)(2,1)S(1)}, u32[]{:S(2)}, u32[]{:S(2)}) %collective-permute-start.1) | collective-permute-done | bytes 196640 | tf_op jit(solution)/shard_map/ppermute | solution.py:188
  45.1 0.9 shard_map.115
  46.1 4.5 %all-to-all-start.3 = ((bf16[4,192,512]{2,1,0:T(8,128)(2,1)}), bf16[4,192,512]{2,1,0:T(8,128)(2,1)}, u32[]{:S(2)}, u32[]{:S(2)}) async-start(bf16[4,192,512]{2,1,0:T(8,128)(2,1)} %shard_map.115), calls=%async_computation.3 | async-start | bytes 1572864 | tf_op jit(solution)/shard_map/all_to_all | solution.py:201
  50.6 8.1 %collective-permute-start.2 = (bf16[480,512]{1,0:T(8,128)(2,1)S(1)}, bf16[480,512]{1,0:T(8,128)(2,1)S(1)}, u32[]{:S(2)}, u32[]{:S(2)}) collective-permute-start(bf16[480,512]{1,0:T(8,128)(2,1)S(1)} %shard_map.109), channel_id=1, source_target_pairs={{0,384},{16,144},{128,256},{144,16},{256,128},{272,400},{384,0},{4... | collective-permute-start | bytes 1474568 | tf_op jit(solution)/shard_map/ppermute | solution.py:188
  58.7 20.8 %collective-permute-done.2.got_ref.refs_0_ = bf16[480,512]{1,0:T(8,128)(2,1)S(1)} collective-permute-done((bf16[480,512]{1,0:T(8,128)(2,1)S(1)}, bf16[480,512]{1,0:T(8,128)(2,1)S(1)}, u32[]{:S(2)}, u32[]{:S(2)}) %collective-permute-start.2) | collective-permute-done | bytes 491552 | tf_op jit(solution)/shard_map/ppermute | solution.py:188
  79.5 1.2 shard_map.117
  80.7 4.7 %all-to-all-start.4 = ((bf16[4,384,512]{2,1,0:T(8,128)(2,1)}), bf16[4,384,512]{2,1,0:T(8,128)(2,1)}, u32[]{:S(2)}, u32[]{:S(2)}) async-start(bf16[4,384,512]{2,1,0:T(8,128)(2,1)} %shard_map.117), calls=%async_computation.4 | async-start | bytes 3145728 | tf_op jit(solution)/shard_map/all_to_all | solution.py:201
  85.7 4.3 %shard_map.116 = (f32[512,512]{1,0:T(8,128)}, bf16[512,1536]{1,0:T(8,128)(2,1)}) custom-call(s32[33]{0:T(128)S(1)} %pad_add_fusion.ord_ref, bf16[16,256,256]{2,1,0:T(8,128)(2,1)S(1)} %shard_map.113.own_ref, bf16[16,256,256]{2,1,0:T(8,128)(2,1)} %collective-permute-done.6.mate_ref, bf16[768,512]{1,0:T(8,128)(2,1)S(1)} %bitcast.12, bf16[768,512]{1,0:T(8,128)(2,1)} %bitcast.8.b_ref), custom_call_target="tpu_custom_call" | custom-call | flops 805306368 | tf_op jit(solution)/shard_map/pallas_call | solution.py:249
  90.0 12.6 %all-to-all-done.4 = bf16[4,384,512]{2,1,0:T(8,128)(2,1)} async-done(((bf16[4,384,512]{2,1,0:T(8,128)(2,1)}), bf16[4,384,512]{2,1,0:T(8,128)(2,1)}, u32[]{:S(2)}, u32[]{:S(2)}) %all-to-all-start.4) | async-done | bytes 1572896 | tf_op jit(solution)/shard_map/all_to_all | solution.py:201
  102.7 5.0 %shard_map.118 = bf16[4,512,256]{2,1,0:T(8,128)(2,1)} custom-call(s32[33]{0:T(128)S(1)} %pad_add_fusion.ord_ref, bf16[512,1536]{1,0:T(8,128)(2,1)} %get-tuple-element.7.rows_ref, f32[512,512]{1,0:T(8,128)} %get-tuple-element.8.early_ref, bf16[1536,512]{1,0:T(8,128)(2,1)} %bitcast.9.c_ref), custom_call_target="tpu_custom_call" | custom-call | flops 805306368 | tf_op jit(solution)/shard_map/pallas_call | solution.py:258
  107.7 3.5 %all-to-all-start.5 = ((bf16[4,512,256]{2,1,0:T(8,128)(2,1)}), bf16[4,512,256]{2,1,0:T(8,128)(2,1)S(1)}, u32[]{:S(2)}, u32[]{:S(2)}) async-start(bf16[4,512,256]{2,1,0:T(8,128)(2,1)} %shard_map.118), calls=%async_computation.5 | async-start | bytes 2097152 | tf_op jit(solution)/shard_map/all_to_all | solution.py:272
  111.2 1.9 %collective-permute-start.3 = (bf16[48,2048]{1,0:T(8,128)(2,1)S(1)}, bf16[48,2048]{1,0:T(8,128)(2,1)S(1)}, u32[]{:S(2)}, u32[]{:S(2)}) collective-permute-start(bf16[48,2048]{1,0:T(8,128)(2,1)S(1)} %shard_map.110.refs_0_), channel_id=1, source_target_pairs={{0,128},{16,400},{128,0},{144,272},{256,384},{272,144},{384,256},{... | collective-permute-start | bytes 589832 | tf_op jit(solution)/shard_map/ppermute | solution.py:188
  113.1 8.5 %collective-permute-done.3.refs_1_ = bf16[48,2048]{1,0:T(8,128)(2,1)S(1)} collective-permute-done((bf16[48,2048]{1,0:T(8,128)(2,1)S(1)}, bf16[48,2048]{1,0:T(8,128)(2,1)S(1)}, u32[]{:S(2)}, u32[]{:S(2)}) %collective-permute-start.3) | collective-permute-done | bytes 196640 | tf_op jit(solution)/shard_map/ppermute | solution.py:188
  122.3 1.0 shard_map.111.refs_0_
  123.3 2.8 %collective-permute-start.4 = (bf16[96,2048]{1,0:T(8,128)(2,1)S(1)}, bf16[96,2048]{1,0:T(8,128)(2,1)}, u32[]{:S(2)}, u32[]{:S(2)}) collective-permute-start(bf16[96,2048]{1,0:T(8,128)(2,1)S(1)} %shard_map.111.refs_0_), channel_id=1, source_target_pairs={{0,32},{16,112},{32,0},{48,80},{64,96},{80,48},{96,64},{112,16},{1... | collective-permute-start | bytes 1179656 | tf_op jit(solution)/shard_map/ppermute | solution.py:188
  126.1 7.4 %collective-permute-start.7 = (bf16[4,512,256]{2,1,0:T(8,128)(2,1)S(1)}, bf16[4,512,256]{2,1,0:T(8,128)(2,1)S(1)}, u32[]{:S(2)}, u32[]{:S(2)}) collective-permute-start(bf16[4,512,256]{2,1,0:T(8,128)(2,1)S(1)} %all-to-all-done.5.hid_ref), channel_id=1, source_target_pairs={{0,16},{16,0},{1,17},{17,1},{2,18},{18,2},{3,19},{19,3},{4,20},{20... | collective-permute-start | bytes 3145736 | tf_op jit(solution)/shard_map/ppermute | solution.py:273
  133.5 1.0 shard_map.112.first_ref
  134.6 3.1 %collective-permute-start.5 = (bf16[192,2048]{1,0:T(8,128)(2,1)S(1)}, bf16[192,2048]{1,0:T(8,128)(2,1)S(1)}, u32[]{:S(2)}, u32[]{:S(2)}) collective-permute-start(bf16[192,2048]{1,0:T(8,128)(2,1)S(1)} %shard_map.112.first_ref), channel_id=1, source_target_pairs={{0,96},{16,48},{32,64},{48,16},{64,32},{80,112},{96,0},{112,80},{1... | collective-permute-start | bytes 2359304 | tf_op jit(solution)/shard_map/ppermute | solution.py:188
  137.6 9.8 %collective-permute-start = (s32[1,256]{1,0:T(1,128)S(1)}, s32[1,256]{1,0:T(1,128)S(1)}, u32[]{:S(2)}, u32[]{:S(2)}) collective-permute-start(s32[1,256]{1,0:T(1,128)S(1)} %copy-done.2), channel_id=1, source_target_pairs={{0,16},{16,0},{1,17},{17,1},{2,18},{18,2},{3,19},{19,3},{4,20},{20... | collective-permute-start | bytes 3080 | tf_op jit(solution)/shard_map/ppermute | solution.py:228
  148.2 3.0 %shard_map.119 = bf16[32,32,384]{2,1,0:T(8,128)(2,1)} custom-call(s32[33]{0:T(128)S(1)} %pad_add_fusion.ord_ref, s32[2,256]{1,0:T(2,128)S(1)} %add_select_fusion.idx_ref, bf16[192,2048]{1,0:T(8,128)(2,1)S(1)} %shard_map.112.first_ref, bf16[192,2048]{1,0:T(8,128)(2,1)S(1)} %collective-permute-done.5.second_ref, ...), custom_call_target="tpu_custom_call" | custom-call | flops 805306368 | tf_op jit(solution)/shard_map/pallas_call | solution.py:275
  151.3 16.4 %all-to-all-start.6 = ((bf16[32,32,384]{2,1,0:T(8,128)(2,1)}), bf16[32,32,384]{2,1,0:T(8,128)(2,1)S(1)}, u32[]{:S(2)}, u32[]{:S(2)}) async-start(bf16[32,32,384]{2,1,0:T(8,128)(2,1)} %shard_map.119), calls=%async_computation.6 | async-start | bytes 1572864 | tf_op jit(solution)/shard_map/all_to_all | solution.py:282
  168.6 20.9 %all-to-all-done.6.in_ref = bf16[32,32,384]{2,1,0:T(8,128)(2,1)S(1)} async-done(((bf16[32,32,384]{2,1,0:T(8,128)(2,1)}), bf16[32,32,384]{2,1,0:T(8,128)(2,1)S(1)}, u32[]{:S(2)}, u32[]{:S(2)}) %all-to-all-start.6) | async-done | bytes 786464 | tf_op jit(solution)/shard_map/all_to_all | solution.py:282
  189.5 1.6 shard_map.120
  (30 shorter events, 3.8 us)
Async XLA Ops:
  0.0 22.7 %copy-start.2 = (s32[1,256]{1,0:T(1,128)S(1)}, s32[1,256]{1,0:T(1,128)}, u32[]{:S(2)}) copy-start(s32[1,256]{1,0:T(1,128)} %param.14) | copy-start | bytes 3076
  11.3 7.9 %all-to-all-start = ((bf16[4,24,512]{2,1,0:T(8,128)(2,1)}), bf16[4,24,512]{2,1,0:T(8,128)(2,1)S(1)}, u32[]{:S(2)}, u32[]{:S(2)}) async-start(bf16[4,24,512]{2,1,0:T(8,128)(2,1)} %bitcast.19), calls=%async_computation | async-start | bytes 196608 | tf_op jit(solution)/shard_map/all_to_all | solution.py:216
  19.2 26.8 %all-to-all-start.2 = ((bf16[4,192,512]{2,1,0:T(8,128)(2,1)}), bf16[4,192,512]{2,1,0:T(8,128)(2,1)S(1)}, u32[]{:S(2)}, u32[]{:S(2)}) async-start(bf16[4,192,512]{2,1,0:T(8,128)(2,1)} %shard_map.114), calls=%async_computation.2 | async-start | bytes 1572864 | tf_op jit(solution)/shard_map/all_to_all | solution.py:201
  22.9 1.9 copy-start
  26.1 59.6 %collective-permute-start.6 = (bf16[16,256,256]{2,1,0:T(8,128)(2,1)S(1)}, bf16[16,256,256]{2,1,0:T(8,128)(2,1)}, u32[]{:S(2)}, u32[]{:S(2)}) collective-permute-start(bf16[16,256,256]{2,1,0:T(8,128)(2,1)S(1)} %shard_map.113.own_ref), channel_id=1, source_target_pairs={{0,16},{16,0},{1,17},{17,1},{2,18},{18,2},{3,19},{19,3},{4,20},{20... | collective-permute-start | bytes 6291464 | tf_op jit(solution)/shard_map/ppermute | solution.py:227
  29.5 15.6 %collective-permute-start.1 = (bf16[192,512]{1,0:T(8,128)(2,1)S(1)}, bf16[192,512]{1,0:T(8,128)(2,1)S(1)}, u32[]{:S(2)}, u32[]{:S(2)}) collective-permute-start(bf16[192,512]{1,0:T(8,128)(2,1)S(1)} %bitcast.14), channel_id=1, source_target_pairs={{0,128},{16,400},{128,0},{144,272},{256,384},{272,144},{384,256},{... | collective-permute-start | bytes 589832 | tf_op jit(solution)/shard_map/ppermute | solution.py:188
  46.1 34.6 %all-to-all-start.3 = ((bf16[4,192,512]{2,1,0:T(8,128)(2,1)}), bf16[4,192,512]{2,1,0:T(8,128)(2,1)}, u32[]{:S(2)}, u32[]{:S(2)}) async-start(bf16[4,192,512]{2,1,0:T(8,128)(2,1)} %shard_map.115), calls=%async_computation.3 | async-start | bytes 1572864 | tf_op jit(solution)/shard_map/all_to_all | solution.py:201
  50.6 28.8 %collective-permute-start.2 = (bf16[480,512]{1,0:T(8,128)(2,1)S(1)}, bf16[480,512]{1,0:T(8,128)(2,1)S(1)}, u32[]{:S(2)}, u32[]{:S(2)}) collective-permute-start(bf16[480,512]{1,0:T(8,128)(2,1)S(1)} %shard_map.109), channel_id=1, source_target_pairs={{0,384},{16,144},{128,256},{144,16},{256,128},{272,400},{384,0},{4... | collective-permute-start | bytes 1474568 | tf_op jit(solution)/shard_map/ppermute | solution.py:188
  80.7 4.7 %copy-start.3 = (s32[4]{0:T(128)S(1)}, s32[4]{0:T(128)}, u32[]{:S(2)}) copy-start(s32[4]{0:T(128)} %constant.38.clone) | copy-start | bytes 52
  80.7 4.7 %copy-start.4 = (s32[4]{0:T(128)S(1)}, s32[4]{0:T(128)}, u32[]{:S(2)}) copy-start(s32[4]{0:T(128)} %constant.39.clone) | copy-start | bytes 52
  80.7 21.9 %all-to-all-start.4 = ((bf16[4,384,512]{2,1,0:T(8,128)(2,1)}), bf16[4,384,512]{2,1,0:T(8,128)(2,1)}, u32[]{:S(2)}, u32[]{:S(2)}) async-start(bf16[4,384,512]{2,1,0:T(8,128)(2,1)} %shard_map.117), calls=%async_computation.4 | async-start | bytes 3145728 | tf_op jit(solution)/shard_map/all_to_all | solution.py:201
  107.7 18.5 %all-to-all-start.5 = ((bf16[4,512,256]{2,1,0:T(8,128)(2,1)}), bf16[4,512,256]{2,1,0:T(8,128)(2,1)S(1)}, u32[]{:S(2)}, u32[]{:S(2)}) async-start(bf16[4,512,256]{2,1,0:T(8,128)(2,1)} %shard_map.118), calls=%async_computation.5 | async-start | bytes 2097152 | tf_op jit(solution)/shard_map/all_to_all | solution.py:272
  111.2 10.4 %collective-permute-start.3 = (bf16[48,2048]{1,0:T(8,128)(2,1)S(1)}, bf16[48,2048]{1,0:T(8,128)(2,1)S(1)}, u32[]{:S(2)}, u32[]{:S(2)}) collective-permute-start(bf16[48,2048]{1,0:T(8,128)(2,1)S(1)} %shard_map.110.refs_0_), channel_id=1, source_target_pairs={{0,128},{16,400},{128,0},{144,272},{256,384},{272,144},{384,256},{... | collective-permute-start | bytes 589832 | tf_op jit(solution)/shard_map/ppermute | solution.py:188
  121.6 0.7 copy-start.1
  123.3 10.2 %collective-permute-start.4 = (bf16[96,2048]{1,0:T(8,128)(2,1)S(1)}, bf16[96,2048]{1,0:T(8,128)(2,1)}, u32[]{:S(2)}, u32[]{:S(2)}) collective-permute-start(bf16[96,2048]{1,0:T(8,128)(2,1)S(1)} %shard_map.111.refs_0_), channel_id=1, source_target_pairs={{0,32},{16,112},{32,0},{48,80},{64,96},{80,48},{96,64},{112,16},{1... | collective-permute-start | bytes 1179656 | tf_op jit(solution)/shard_map/ppermute | solution.py:188
  126.1 22.1 %collective-permute-start.7 = (bf16[4,512,256]{2,1,0:T(8,128)(2,1)S(1)}, bf16[4,512,256]{2,1,0:T(8,128)(2,1)S(1)}, u32[]{:S(2)}, u32[]{:S(2)}) collective-permute-start(bf16[4,512,256]{2,1,0:T(8,128)(2,1)S(1)} %all-to-all-done.5.hid_ref), channel_id=1, source_target_pairs={{0,16},{16,0},{1,17},{17,1},{2,18},{18,2},{3,19},{19,3},{4,20},{20... | collective-permute-start | bytes 3145736 | tf_op jit(solution)/shard_map/ppermute | solution.py:273
  134.6 13.7 %collective-permute-start.5 = (bf16[192,2048]{1,0:T(8,128)(2,1)S(1)}, bf16[192,2048]{1,0:T(8,128)(2,1)S(1)}, u32[]{:S(2)}, u32[]{:S(2)}) collective-permute-start(bf16[192,2048]{1,0:T(8,128)(2,1)S(1)} %shard_map.112.first_ref), channel_id=1, source_target_pairs={{0,96},{16,48},{32,64},{48,16},{64,32},{80,112},{96,0},{112,80},{1... | collective-permute-start | bytes 2359304 | tf_op jit(solution)/shard_map/ppermute | solution.py:188
  137.6 10.6 %collective-permute-start = (s32[1,256]{1,0:T(1,128)S(1)}, s32[1,256]{1,0:T(1,128)S(1)}, u32[]{:S(2)}, u32[]{:S(2)}) collective-permute-start(s32[1,256]{1,0:T(1,128)S(1)} %copy-done.2), channel_id=1, source_target_pairs={{0,16},{16,0},{1,17},{17,1},{2,18},{18,2},{3,19},{19,3},{4,20},{20... | collective-permute-start | bytes 3080 | tf_op jit(solution)/shard_map/ppermute | solution.py:228
  151.3 38.2 %all-to-all-start.6 = ((bf16[32,32,384]{2,1,0:T(8,128)(2,1)}), bf16[32,32,384]{2,1,0:T(8,128)(2,1)S(1)}, u32[]{:S(2)}, u32[]{:S(2)}) async-start(bf16[32,32,384]{2,1,0:T(8,128)(2,1)} %shard_map.119), calls=%async_computation.6 | async-start | bytes 1572864 | tf_op jit(solution)/shard_map/all_to_all | solution.py:282

commit v5 on v4

--- a/solution.py
+++ b/solution.py
@@ -59,23 +59,28 @@
         out_ref[caps:, i * width : (i + 1) * width] = mate_ref[ord_ref[k], :, :width]
 
 
-def early_body(ord_ref, own_ref, mate_ref, a_ref, b_ref, out_ref, late_ref, now_ref, then_ref, sum_ref, sems):
+def early_body(ord_ref, own_ref, mate_ref, *rest):
+    piece_refs, (out_ref, late_ref, now_ref, then_ref, sum_ref, sems) = rest[:4], rest[4:]
     lay(ord_ref, own_ref, mate_ref, then_ref, [4 * q + n for q in range(4) for n in (2, 3)])
     copy = pltpu.make_async_copy(then_ref, late_ref, sems.at[0])
     copy.start()
-    lay(ord_ref, own_ref, mate_ref, now_ref, [4 * q + n for n in (0, 1) for q in range(4)])
-    half = a_ref.shape[0]
-    sum_ref[...] = dot_nn(now_ref[:, :half], a_ref[...]) + dot_nn(now_ref[:, half:], b_ref[...])
+    lay(ord_ref, own_ref, mate_ref, now_ref, [4 * q + n for q in range(4) for n in (0, 1)])
+    acc = None
+    for q, piece in enumerate(piece_refs):
+        part = dot_nn(now_ref[:, 384 * q : 384 * (q + 1)], piece[...])
+        acc = part if acc is None else acc + part
+    sum_ref[...] = acc
     store = pltpu.make_async_copy(sum_ref, out_ref, sems.at[1])
     store.start()
     copy.wait()
     store.wait()
 
 
-def hidden_body(ord_ref, rows_ref, early_ref, c_ref, out_ref, res_ref, rows_vmem, sum_ref, sems, out_sems):
+def hidden_body(ord_ref, rows_ref, early_ref, *rest):
+    piece_refs, (out_ref, res_ref, rows_vmem, sum_ref, sems, out_sems) = rest[:4], rest[4:]
     caps = rows_ref.shape[0] // 2
     half = rows_ref.shape[1] // 2
-    core = ord_ref[32]
+    core = ord_ref[16]
     copies = [
         pltpu.make_async_copy(rows_ref.at[:, pl.ds(n * half, half)], rows_vmem.at[:, pl.ds(n * half, half)], sems.at[n])
         for n in range(2)
@@ -85,8 +90,9 @@
     acc = None
     for n in range(2):
         copies[n].wait()
-        part = dot_nn(rows_vmem[:, n * half : (n + 1) * half], c_ref[n * half : (n + 1) * half, :])
-        acc = part if acc is None else acc + part
+        for q in (2 * n, 2 * n + 1):
+            part = dot_nn(rows_vmem[:, 384 * q : 384 * (q + 1)], piece_refs[q][...])
+            acc = part if acc is None else acc + part
     copies[2].wait()
     acc = acc + sum_ref[...]
     cols = []
@@ -104,23 +110,24 @@
         copy.wait()
 
 
-def down_body(ord_ref, idx_ref, first_ref, second_ref, hid_ref, mate_ref, out_ref, scr, w_ref, sems):
+def down_body(ord_ref, idx_ref, *rest):
+    piece_refs, (hid_ref, mate_ref, out_ref, scr, w_ref, sems) = rest[:4], rest[4:]
     caps = idx_ref.shape[1]
     rows, unit, acc = 512, 24, None
     copies = [
-        pltpu.make_async_copy(r, w_ref.at[pl.ds(192 * n, 192)], sems.at[n]) for n, r in enumerate((first_ref, second_ref))
+        pltpu.make_async_copy(r, w_ref.at[pl.ds(96 * n, 96)], sems.at[n]) for n, r in enumerate(piece_refs)
     ]
     for copy in copies:
         copy.start()
     for copy in copies:
         copy.wait()
-    for core, h_ref in ((ord_ref[32], hid_ref), (1 - ord_ref[32], mate_ref)):
+    for core, h_ref in ((ord_ref[16], hid_ref), (1 - ord_ref[16], mate_ref)):
         for x in range(4):
             lo = pl.multiple_of(512 * x + 256 * core, 256)
             part = dot_nt(w_ref[:, pl.ds(lo, 256)], h_ref[x])
             acc = part if acc is None else acc + part
     for k in range(16):
-        at = pl.multiple_of(ord_ref[16 + k] * unit, 8)
+        at = pl.multiple_of(ord_ref[k] * unit, 8)
         scr[pl.ds(at, unit), :] = acc[k * unit : (k + 1) * unit, :]
     for b in range(2):
         hot = (lax.broadcasted_iota(jnp.int32, (rows, caps), 0) == idx_ref[b : b + 1, :]).astype(BF)
@@ -129,27 +136,9 @@
             out_ref[16 * b + n] = dense[32 * n : 32 * n + 32, :]
 
 
-def spread_body(*refs):
-    out_ref, sems = refs[-2], refs[-1]
-    lo, copies = 0, []
-    for n, r in enumerate(refs[:-2]):
-        rows = min(r.shape[0], out_ref.shape[1] - lo)
-        for q in range(out_ref.shape[0]):
-            copies.append(
-                pltpu.make_async_copy(r.at[pl.ds(0, rows)], out_ref.at[q, pl.ds(lo, rows)], sems.at[n, q])
-            )
-        lo += rows
-    for copy in copies:
-        copy.start()
-    for copy in copies:
-        copy.wait()
-
-
-def quarter_body(own_ref, got_ref, out_ref):
-    lo = got_ref.shape[0] - 96
+def quarter_body(in_ref, out_ref):
     for x in range(4):
-        out_ref[:24, 512 * x : 512 * (x + 1)] = own_ref[24 * x : 24 * (x + 1), :]
-        out_ref[24:, 512 * x : 512 * (x + 1)] = got_ref[lo + 24 * x : lo + 24 * (x + 1), :]
+        out_ref[:, 512 * x : 512 * (x + 1)] = in_ref[24 * x : 24 * (x + 1), :]
 
 
 def place_body(in_ref, scale_ref, out_ref, scr):
@@ -188,17 +177,10 @@
     return lax.ppermute(value, (axis, "c"), pairs(step))
 
 
-def over_y(parts, rows):
-    cols = parts[0].shape[1]
-    wide = call(
-        spread_body,
-        pltpu.HBM((4, rows, cols), BF),
-        [vm()] * len(parts),
-        scratch=[pltpu.SemaphoreType.DMA((len(parts), 4))],
-        mib=4,
-        to=hb,
-    )(*parts)
-    return lax.all_to_all(wide, "y", 0, 0, tiled=True)
+def over_y(value):
+    near = meet(value, "y", 0)
+    other = meet(value, "y", 1)
+    return value, near, other, meet(near, "y", 1)
 
 
 def shards(tokens, expert_ids, route_weight, index_list, gate_weight, up_weight, down_weight):
@@ -214,11 +196,11 @@
 
     turned = down_weight.T
     quarter = lax.all_to_all(turned, "x", 0, 0, tiled=True)
+    quarter = call(quarter_body, jax.ShapeDtypeStruct((24, 2048), BF), [vm()], mib=4)(quarter)
+
     flip = jnp.where(c == 0, jnp.array([0, 1, 3, 2]), jnp.array([0, 3, 1, 2])).astype(jnp.int32)
-    order = ((zh ^ flip)[None, :] * 4 + jnp.arange(4, dtype=jnp.int32)[:, None]).reshape(16)
-    turned_flip = jnp.where(c == 0, jnp.array([0, 3, 1, 2]), jnp.array([0, 1, 3, 2])).astype(jnp.int32)
-    order_down = ((zh ^ turned_flip)[None, :] * 4 + (y ^ flip)[:, None]).reshape(16)
-    order = jnp.concatenate([order, order_down, c.reshape(1)]).astype(jnp.int32)
+    order = ((zh ^ flip)[None, :] * 4 + (y ^ flip)[:, None]).reshape(16)
+    order = jnp.concatenate([order, c.reshape(1)]).astype(jnp.int32)
 
     rows = call(
         pick_body, jax.ShapeDtypeStruct((16, caps, 256), BF), [vm(), vm()], flops=2 * 256 * 512 * 3072
@@ -233,32 +215,29 @@
     )
 
     near = meet(both_rows, "zh", 0)
-    ya = over_y((both_rows,), 192)
-    yb = over_y((near,), 192)
-    far = meet(join((both_rows, near, quarter)), "zh", 1)
-    yc = over_y((far,), 384)
-    ya, yb, yc = ya.reshape(768, 512), yb.reshape(768, 512), yc.reshape(1536, 512)
-
-    two = call(quarter_body, jax.ShapeDtypeStruct((48, 2048), BF), [vm()] * 2, mib=4)(quarter, far)
-    far = pltpu.with_memory_space_constraint(meet(two, "zh", 0), pltpu.HBM)
-    four = join((two, far))
-    near = pltpu.with_memory_space_constraint(meet(four, "y", 0), pltpu.HBM)
-    down_first = join((four, near))
-    down_second = meet(down_first, "y", 1)
+    both = join((both_rows, near))
+    far = meet(both, "zh", 1)
+    soon = over_y(both)
+    later = over_y(far)
+
+    near = pltpu.with_memory_space_constraint(meet(quarter, "zh", 0), pltpu.HBM)
+    two = join((quarter, near))
+    far = pltpu.with_memory_space_constraint(meet(two, "zh", 1), pltpu.HBM)
+    downs = over_y(join((two, far)))
 
     early, rows_late = call(
         early_body,
         [pltpu.HBM((512, 512), F32), pltpu.HBM((512, 1536), BF)],
-        [sm()] + [vm()] * 4,
+        [sm()] + [vm()] * 6,
         scratch=[pltpu.VMEM((512, 1536), BF)] * 2 + [pltpu.VMEM((512, 512), F32), pltpu.SemaphoreType.DMA((2,))],
         flops=512 * 3072 * 512,
         to=hb,
-    )(order, rows, rows_mate, ya, yb)
+    )(order, rows, rows_mate, *soon)
     early, rows_late = (pltpu.with_memory_space_constraint(v, pltpu.HBM) for v in (early, rows_late))
     wide = call(
         hidden_body,
         pltpu.HBM((4, 512, 256), BF),
-        [sm(), hb(), hb(), vm()],
+        [sm(), hb(), hb()] + [vm()] * 4,
         scratch=[
             pltpu.VMEM((512, 256), BF),
             pltpu.VMEM((512, 1536), BF),
@@ -268,17 +247,17 @@
         ],
         flops=512 * 3072 * 512,
         to=hb,
-    )(order, rows_late, early, yc)
+    )(order, rows_late, early, *later)
     hid = lax.all_to_all(wide, "x", 0, 0, tiled=True)
     hid_mate = lax.ppermute(hid, "c", swap)
 
     parts = call(
         down_body,
         jax.ShapeDtypeStruct((32, 32, 384), BF),
-        [sm(), vm(), hb(), hb(), vm(), vm()],
-        scratch=[pltpu.VMEM((384, 512), F32), pltpu.VMEM((384, 2048), BF), pltpu.SemaphoreType.DMA((2,))],
+        [sm(), vm()] + [hb()] * 4 + [vm()] * 2,
+        scratch=[pltpu.VMEM((384, 512), F32), pltpu.VMEM((384, 2048), BF), pltpu.SemaphoreType.DMA((4,))],
         flops=2 * 512 * 384 * 2048,
-    )(order, index_both, down_first, down_second, hid, hid_mate)
+    )(order, index_both, *downs, hid, hid_mate)
     owned = lax.all_to_all(parts, ("c", "zl", "x"), 0, 0, tiled=True)
 
     start = (zl * 4 + x) * 32

time: 192 us -> 189 us (0.984)
  starting transfers between devices: 81.5 us -> 88.4 us
  blocking collectives: 10.4 us -> 3.8 us
  Pallas kernels: 20.4 us -> 18.1 us
    ppermute x5 -> x13, starting transfers between devices: 25 us -> 53.6 us  [meet(): return lax.ppermute(value, (axis, 'c'), pairs(step))]
    all_to_all x3 -> x0, starting transfers between devices: 12.7 us -> none  [over_y(): return lax.all_to_all(wide, 'y', 0, 0, tiled=True)]
    all_to_all x3 -> x0, waiting for transfers between devices: 12.6 us -> none  [over_y(): return lax.all_to_all(wide, 'y', 0, 0, tiled=True)]
    all_to_all x1, waiting for transfers between devices: 0.01 us -> 10.1 us  [shards(): hid = lax.all_to_all(wide, 'x', 0, 0, tiled=True)]
    ppermute x1, starting transfers between devices: 9.8 us -> 3.03 us  [shards(): index_mate = lax.ppermute(index_list, 'c', swap)]
    all_to_all x1, blocking collectives: 10.4 us -> 3.8 us  [shards(): lax.all_to_all(jnp.concatenate(mine, axis=0), 'c', 0, 0, tiled=True)]
    ppermute x1, starting transfers between devices: 3.42 us -> 8.75 us  [shards(): rows_mate = lax.ppermute(rows, 'c', swap)]
    ppermute x1, starting transfers between devices: 7.38 us -> 2.58 us  [shards(): hid_mate = lax.ppermute(hid, 'c', swap)]
  transfers between devices with their start and end apart: 14 -> 19, of which waited for: 7 -> 10; matrix products, arithmetic and copies ran while one was open for 1% -> 1% of each run, Pallas kernels for 6% -> 6%
where the time goes in v5:
time: 189 us; the launch traced here: 188 us
  starting transfers between devices  88.4 us (47%)
  waiting for transfers between devices  71.9 us (38%)
  Pallas kernels  18.1 us (10%)
  local copies, waits for them, and re-layouts  4.24 us (2%)
  blocking collectives  3.8 us (2%)
    ppermute x13, starting transfers between devices, meet(): return lax.ppermute(value, (axis, 'c'), pairs(step))  53.6 us
    ppermute x13, waiting for transfers between devices, meet(): return lax.ppermute(value, (axis, 'c'), pairs(step))  40.1 us
    all_to_all x1, waiting for transfers between devices, shards(): owned = lax.all_to_all(parts, ('c', 'zl', 'x'), 0, 0, tiled=True)  20.9 us
    all_to_all x1, starting transfers between devices, shards(): owned = lax.all_to_all(parts, ('c', 'zl', 'x'), 0, 0, tiled=True)  12.2 us
    all_to_all x1, waiting for transfers between devices, shards(): hid = lax.all_to_all(wide, 'x', 0, 0, tiled=True)  10.1 us
    ppermute x1, starting transfers between devices, shards(): rows_mate = lax.ppermute(rows, 'c', swap)  8.75 us
    pallas_call x1, Pallas kernels, shards(): call(hidden_body, pltpu.HBM((4, 512, 256), BF), [sm(), hb(), hb()] + [vm(...  5.01 us
    pallas_call x1, Pallas kernels, shards(): call(early_body, [pltpu.HBM((512, 512), F32), pltpu.HBM((512, 1536), BF)]...  4.5 us
  transfers between devices with their start and end apart: 19, of which 10 were waited for; matrix products, arithmetic and copies ran while one was open for 1% of the time, Pallas kernels for 6%

profile of v5, /device:TPU:1, one launch (start us, length us, event | category | flops | bytes accessed | tf_op | source)
XLA Modules:
  0.0 187.8 jit_solution(18079588038972717178)
XLA Ops:
  4.1 8.7 %collective-permute-start.6 = (bf16[16,256,256]{2,1,0:T(8,128)(2,1)S(1)}, bf16[16,256,256]{2,1,0:T(8,128)(2,1)}, u32[]{:S(2)}, u32[]{:S(2)}) collective-permute-start(bf16[16,256,256]{2,1,0:T(8,128)(2,1)S(1)} %shard_map.94.own_ref), channel_id=1, source_target_pairs={{0,16},{16,0},{1,17},{17,1},{2,18},{18,2},{3,19},{19,3},{4,20},{20... | collective-permute-start | bytes 6291464 | tf_op jit(solution)/shard_map/ppermute | solution.py:209
  12.9 3.8 %all_to_all.32 = bf16[2,96,512]{2,1,0:T(8,128)(2,1)S(1)} all-to-all(bf16[2,96,512]{2,1,0:T(8,128)(2,1)S(1)} %bitcast.12), channel_id=1, replica_groups=mesh['zh'=4,'y'=4,'c'=2,'zl'=4,'x'=4] {'c'}, dimensions={0} | all-to-all | bytes 393216 | tf_op jit(solution)/shard_map/all_to_all | solution.py:195
  16.7 7.1 %collective-permute-start.7 = (bf16[192,512]{1,0:T(8,128)(2,1)S(1)}, bf16[192,512]{1,0:T(8,128)(2,1)S(1)}, u32[]{:S(2)}, u32[]{:S(2)}) collective-permute-start(bf16[192,512]{1,0:T(8,128)(2,1)S(1)} %bitcast.9), channel_id=1, source_target_pairs={{0,128},{16,400},{128,0},{144,272},{256,384},{272,144},{384,256},{... | collective-permute-start | bytes 589832 | tf_op jit(solution)/shard_map/ppermute | solution.py:177
  23.8 6.7 %collective-permute-done.7.refs_1_ = bf16[192,512]{1,0:T(8,128)(2,1)S(1)} collective-permute-done((bf16[192,512]{1,0:T(8,128)(2,1)S(1)}, bf16[192,512]{1,0:T(8,128)(2,1)S(1)}, u32[]{:S(2)}, u32[]{:S(2)}) %collective-permute-start.7) | collective-permute-done | bytes 196640 | tf_op jit(solution)/shard_map/ppermute | solution.py:177
  30.6 7.8 %collective-permute-start.11 = (bf16[384,512]{1,0:T(8,128)(2,1)S(1)}, bf16[384,512]{1,0:T(8,128)(2,1)}, u32[]{:S(2)}, u32[]{:S(2)}) collective-permute-start(bf16[384,512]{1,0:T(8,128)(2,1)S(1)} %shard_map.95.rest_0_), channel_id=1, source_target_pairs={{0,384},{16,144},{128,256},{144,16},{256,128},{272,400},{384,0},{4... | collective-permute-start | bytes 1179656 | tf_op jit(solution)/shard_map/ppermute | solution.py:177
  38.4 4.6 %collective-permute-start.8 = (bf16[384,512]{1,0:T(8,128)(2,1)S(1)}, bf16[384,512]{1,0:T(8,128)(2,1)S(1)}, u32[]{:S(2)}, u32[]{:S(2)}) collective-permute-start(bf16[384,512]{1,0:T(8,128)(2,1)S(1)} %shard_map.95.rest_0_), channel_id=1, source_target_pairs={{0,32},{16,112},{32,0},{48,80},{64,96},{80,48},{96,64},{112,16},{1... | collective-permute-start | bytes 1179656 | tf_op jit(solution)/shard_map/ppermute | solution.py:177
  43.1 8.8 %collective-permute-done.11.rest_0_ = bf16[384,512]{1,0:T(8,128)(2,1)} collective-permute-done((bf16[384,512]{1,0:T(8,128)(2,1)S(1)}, bf16[384,512]{1,0:T(8,128)(2,1)}, u32[]{:S(2)}, u32[]{:S(2)}) %collective-permute-start.11) | collective-permute-done | bytes 393248 | tf_op jit(solution)/shard_map/ppermute | solution.py:177
  51.9 8.3 %collective-permute-start.12 = (bf16[384,512]{1,0:T(8,128)(2,1)}, bf16[384,512]{1,0:T(8,128)(2,1)}, u32[]{:S(2)}, u32[]{:S(2)}) collective-permute-start(bf16[384,512]{1,0:T(8,128)(2,1)} %collective-permute-done.11.rest_0_), channel_id=1, source_target_pairs={{0,32},{16,112},{32,0},{48,80},{64,96},{80,48},{96,64},{112,16},{1... | collective-permute-start | bytes 1179656 | tf_op jit(solution)/shard_map/ppermute | solution.py:177
  60.2 4.0 %all-to-all-start = ((bf16[4,24,512]{2,1,0:T(8,128)(2,1)}), bf16[4,24,512]{2,1,0:T(8,128)(2,1)S(1)}, u32[]{:S(2)}, u32[]{:S(2)}) async-start(bf16[4,24,512]{2,1,0:T(8,128)(2,1)} %bitcast.2), calls=%async_computation | async-start | bytes 196608 | tf_op jit(solution)/shard_map/all_to_all | solution.py:198
  64.2 1.9 %collective-permute-start.9 = (bf16[384,512]{1,0:T(8,128)(2,1)S(1)}, bf16[384,512]{1,0:T(8,128)(2,1)S(1)}, u32[]{:S(2)}, u32[]{:S(2)}) collective-permute-start(bf16[384,512]{1,0:T(8,128)(2,1)S(1)} %shard_map.95.rest_0_), channel_id=1, source_target_pairs={{0,96},{16,48},{32,64},{48,16},{64,32},{80,112},{96,0},{112,80},{1... | collective-permute-start | bytes 1179656 | tf_op jit(solution)/shard_map/ppermute | solution.py:177
  66.2 3.4 %collective-permute-start.10 = (bf16[384,512]{1,0:T(8,128)(2,1)S(1)}, bf16[384,512]{1,0:T(8,128)(2,1)}, u32[]{:S(2)}, u32[]{:S(2)}) collective-permute-start(bf16[384,512]{1,0:T(8,128)(2,1)S(1)} %collective-permute-done.8.rest_1_), channel_id=1, source_target_pairs={{0,96},{16,48},{32,64},{48,16},{64,32},{80,112},{96,0},{112,80},{1... | collective-permute-start | bytes 1179656 | tf_op jit(solution)/shard_map/ppermute | solution.py:177
  69.6 1.9 %collective-permute-start.13 = (bf16[384,512]{1,0:T(8,128)(2,1)}, bf16[384,512]{1,0:T(8,128)(2,1)}, u32[]{:S(2)}, u32[]{:S(2)}) collective-permute-start(bf16[384,512]{1,0:T(8,128)(2,1)} %collective-permute-done.11.rest_0_), channel_id=1, source_target_pairs={{0,96},{16,48},{32,64},{48,16},{64,32},{80,112},{96,0},{112,80},{1... | collective-permute-start | bytes 1179656 | tf_op jit(solution)/shard_map/ppermute | solution.py:177
  71.5 3.4 %collective-permute-start.14 = (bf16[384,512]{1,0:T(8,128)(2,1)}, bf16[384,512]{1,0:T(8,128)(2,1)}, u32[]{:S(2)}, u32[]{:S(2)}) collective-permute-start(bf16[384,512]{1,0:T(8,128)(2,1)} %collective-permute-done.12.rest_1_), channel_id=1, source_target_pairs={{0,96},{16,48},{32,64},{48,16},{64,32},{80,112},{96,0},{112,80},{1... | collective-permute-start | bytes 1179656 | tf_op jit(solution)/shard_map/ppermute | solution.py:177
  75.1 2.2 %collective-permute-done.10.rest_3_ = bf16[384,512]{1,0:T(8,128)(2,1)} collective-permute-done((bf16[384,512]{1,0:T(8,128)(2,1)S(1)}, bf16[384,512]{1,0:T(8,128)(2,1)}, u32[]{:S(2)}, u32[]{:S(2)}) %collective-permute-start.10) | collective-permute-done | bytes 393248 | tf_op jit(solution)/shard_map/ppermute | solution.py:177
  77.3 4.5 %shard_map.96 = (f32[512,512]{1,0:T(8,128)}, bf16[512,1536]{1,0:T(8,128)(2,1)}) custom-call(s32[17]{0:T(128)S(1)} %pad_add_fusion.ord_ref, bf16[16,256,256]{2,1,0:T(8,128)(2,1)S(1)} %shard_map.94.own_ref, bf16[16,256,256]{2,1,0:T(8,128)(2,1)} %collective-permute-done.6.mate_ref, bf16[384,512]{1,0:T(8,128)(2,1)S(1)} %shard_map.95.rest_0_, ...), custom_call_target="tpu_custom_call" | custom-call | flops 805306368 | tf_op jit(solution)/shard_map/pallas_call | solution.py:228
  81.9 3.6 %collective-permute-done.14.rest_3_ = bf16[384,512]{1,0:T(8,128)(2,1)} collective-permute-done((bf16[384,512]{1,0:T(8,128)(2,1)}, bf16[384,512]{1,0:T(8,128)(2,1)}, u32[]{:S(2)}, u32[]{:S(2)}) %collective-permute-start.14) | collective-permute-done | bytes 393248 | tf_op jit(solution)/shard_map/ppermute | solution.py:177
  85.5 5.0 %shard_map.97 = bf16[4,512,256]{2,1,0:T(8,128)(2,1)} custom-call(s32[17]{0:T(128)S(1)} %pad_add_fusion.ord_ref, bf16[512,1536]{1,0:T(8,128)(2,1)} %get-tuple-element.7.rows_ref, f32[512,512]{1,0:T(8,128)} %get-tuple-element.8.early_ref, bf16[384,512]{1,0:T(8,128)(2,1)} %collective-permute-done.11.rest_0_, bf16[384,512]{1,0:T(8,128)(2,1)} %collective-permute-done.12.rest_1_, ...), custom_call_target="tpu_custom_call" | custom-call | flops 805306368 | tf_op jit(solution)/shard_map/pallas_call | solution.py:237
  90.5 4.2 %all-to-all-start.2 = ((bf16[4,512,256]{2,1,0:T(8,128)(2,1)}), bf16[4,512,256]{2,1,0:T(8,128)(2,1)S(1)}, u32[]{:S(2)}, u32[]{:S(2)}) async-start(bf16[4,512,256]{2,1,0:T(8,128)(2,1)} %shard_map.97), calls=%async_computation.2 | async-start | bytes 2097152 | tf_op jit(solution)/shard_map/all_to_all | solution.py:251
  94.8 5.2 %collective-permute-start.1 = (bf16[24,2048]{1,0:T(8,128)(2,1)S(1)}, bf16[24,2048]{1,0:T(8,128)(2,1)S(1)}, u32[]{:S(2)}, u32[]{:S(2)}) collective-permute-start(bf16[24,2048]{1,0:T(8,128)(2,1)S(1)} %shard_map.91.refs_0_), channel_id=1, source_target_pairs={{0,128},{16,400},{128,0},{144,272},{256,384},{272,144},{384,256},{... | collective-permute-start | bytes 294920 | tf_op jit(solution)/shard_map/ppermute | solution.py:177
  100.0 10.1 %all-to-all-done.2.rest_4_ = bf16[4,512,256]{2,1,0:T(8,128)(2,1)S(1)} async-done(((bf16[4,512,256]{2,1,0:T(8,128)(2,1)}), bf16[4,512,256]{2,1,0:T(8,128)(2,1)S(1)}, u32[]{:S(2)}, u32[]{:S(2)}) %all-to-all-start.2) | async-done | bytes 1048608 | tf_op jit(solution)/shard_map/all_to_all | solution.py:251
  110.1 2.6 %collective-permute-start.15 = (bf16[4,512,256]{2,1,0:T(8,128)(2,1)S(1)}, bf16[4,512,256]{2,1,0:T(8,128)(2,1)S(1)}, u32[]{:S(2)}, u32[]{:S(2)}) collective-permute-start(bf16[4,512,256]{2,1,0:T(8,128)(2,1)S(1)} %all-to-all-done.2.rest_4_), channel_id=1, source_target_pairs={{0,16},{16,0},{1,17},{17,1},{2,18},{18,2},{3,19},{19,3},{4,20},{20... | collective-permute-start | bytes 3145736 | tf_op jit(solution)/shard_map/ppermute | solution.py:252
  114.3 3.1 %collective-permute-start.2 = (bf16[48,2048]{1,0:T(8,128)(2,1)S(1)}, bf16[48,2048]{1,0:T(8,128)(2,1)S(1)}, u32[]{:S(2)}, u32[]{:S(2)}) collective-permute-start(bf16[48,2048]{1,0:T(8,128)(2,1)S(1)} %shard_map.92.refs_0_), channel_id=1, source_target_pairs={{0,384},{16,144},{128,256},{144,16},{256,128},{272,400},{384,0},{4... | collective-permute-start | bytes 589832 | tf_op jit(solution)/shard_map/ppermute | solution.py:177
  117.4 9.3 %collective-permute-done.2.refs_1_ = bf16[48,2048]{1,0:T(8,128)(2,1)S(1)} collective-permute-done((bf16[48,2048]{1,0:T(8,128)(2,1)S(1)}, bf16[48,2048]{1,0:T(8,128)(2,1)S(1)}, u32[]{:S(2)}, u32[]{:S(2)}) %collective-permute-start.2) | collective-permute-done | bytes 196640 | tf_op jit(solution)/shard_map/ppermute | solution.py:177
  128.4 3.0 %collective-permute-start.3 = (bf16[96,2048]{1,0:T(8,128)(2,1)S(1)}, bf16[96,2048]{1,0:T(8,128)(2,1)S(1)}, u32[]{:S(2)}, u32[]{:S(2)}) collective-permute-start(bf16[96,2048]{1,0:T(8,128)(2,1)S(1)} %shard_map.93.rest_0_), channel_id=1, source_target_pairs={{0,32},{16,112},{32,0},{48,80},{64,96},{80,48},{96,64},{112,16},{1... | collective-permute-start | bytes 1179656 | tf_op jit(solution)/shard_map/ppermute | solution.py:177
  131.4 1.9 %collective-permute-start.4 = (bf16[96,2048]{1,0:T(8,128)(2,1)S(1)}, bf16[96,2048]{1,0:T(8,128)(2,1)S(1)}, u32[]{:S(2)}, u32[]{:S(2)}) collective-permute-start(bf16[96,2048]{1,0:T(8,128)(2,1)S(1)} %shard_map.93.rest_0_), channel_id=1, source_target_pairs={{0,96},{16,48},{32,64},{48,16},{64,32},{80,112},{96,0},{112,80},{1... | collective-permute-start | bytes 1179656 | tf_op jit(solution)/shard_map/ppermute | solution.py:177
  133.4 6.3 %collective-permute-done.3.rest_1_ = bf16[96,2048]{1,0:T(8,128)(2,1)S(1)} collective-permute-done((bf16[96,2048]{1,0:T(8,128)(2,1)S(1)}, bf16[96,2048]{1,0:T(8,128)(2,1)S(1)}, u32[]{:S(2)}, u32[]{:S(2)}) %collective-permute-start.3) | collective-permute-done | bytes 393248 | tf_op jit(solution)/shard_map/ppermute | solution.py:177
  139.7 1.9 %collective-permute-start.5 = (bf16[96,2048]{1,0:T(8,128)(2,1)S(1)}, bf16[96,2048]{1,0:T(8,128)(2,1)S(1)}, u32[]{:S(2)}, u32[]{:S(2)}) collective-permute-start(bf16[96,2048]{1,0:T(8,128)(2,1)S(1)} %collective-permute-done.3.rest_1_), channel_id=1, source_target_pairs={{0,96},{16,48},{32,64},{48,16},{64,32},{80,112},{96,0},{112,80},{1... | collective-permute-start | bytes 1179656 | tf_op jit(solution)/shard_map/ppermute | solution.py:177
  141.6 3.0 %collective-permute-start = (s32[1,256]{1,0:T(1,128)S(1)}, s32[1,256]{1,0:T(1,128)S(1)}, u32[]{:S(2)}, u32[]{:S(2)}) collective-permute-start(s32[1,256]{1,0:T(1,128)S(1)} %copy-done.5), channel_id=1, source_target_pairs={{0,16},{16,0},{1,17},{17,1},{2,18},{18,2},{3,19},{19,3},{4,20},{20... | collective-permute-start | bytes 3080 | tf_op jit(solution)/shard_map/ppermute | solution.py:210
  145.4 3.0 %collective-permute-done.5.rest_3_ = bf16[96,2048]{1,0:T(8,128)(2,1)S(1)} collective-permute-done((bf16[96,2048]{1,0:T(8,128)(2,1)S(1)}, bf16[96,2048]{1,0:T(8,128)(2,1)S(1)}, u32[]{:S(2)}, u32[]{:S(2)}) %collective-permute-start.5) | collective-permute-done | bytes 393248 | tf_op jit(solution)/shard_map/ppermute | solution.py:177
  148.5 3.7 %shard_map.98 = bf16[32,32,384]{2,1,0:T(8,128)(2,1)} custom-call(s32[17]{0:T(128)S(1)} %pad_add_fusion.ord_ref, s32[2,256]{1,0:T(2,128)S(1)} %add_select_fusion.idx_ref, bf16[96,2048]{1,0:T(8,128)(2,1)S(1)} %shard_map.93.rest_0_, bf16[96,2048]{1,0:T(8,128)(2,1)S(1)} %collective-permute-done.3.rest_1_, bf16[96,2048]{1,0:T(8,128)(2,1)S(1)} %collective-permute-done.4.rest_2_, ...), custom_call_target="tpu_custom_call" | custom-call | flops 805306368 | tf_op jit(solution)/shard_map/pallas_call | solution.py:254
  152.2 12.2 %all-to-all-start.3 = ((bf16[32,32,384]{2,1,0:T(8,128)(2,1)}), bf16[32,32,384]{2,1,0:T(8,128)(2,1)S(1)}, u32[]{:S(2)}, u32[]{:S(2)}) async-start(bf16[32,32,384]{2,1,0:T(8,128)(2,1)} %shard_map.98), calls=%async_computation.3 | async-start | bytes 1572864 | tf_op jit(solution)/shard_map/all_to_all | solution.py:261
  165.3 20.9 %all-to-all-done.3.in_ref = bf16[32,32,384]{2,1,0:T(8,128)(2,1)S(1)} async-done(((bf16[32,32,384]{2,1,0:T(8,128)(2,1)}), bf16[32,32,384]{2,1,0:T(8,128)(2,1)S(1)}, u32[]{:S(2)}, u32[]{:S(2)}) %all-to-all-start.3) | async-done | bytes 786464 | tf_op jit(solution)/shard_map/all_to_all | solution.py:261
  (42 shorter events, 10.9 us)
Async XLA Ops:
  0.8 1.9 %copy-start = (bf16[512,3072]{1,0:T(8,128)(2,1)S(1)}, bf16[512,3072]{1,0:T(8,128)(2,1)}, u32[]{:S(2)}) copy-start(bf16[512,3072]{1,0:T(8,128)(2,1)} %tok_ref.1) | copy-start | bytes 9437188
  2.7 10.1 %copy-start.2 = (bf16[96,512]{1,0:T(8,128)(2,1)S(1)}, bf16[96,512]{1,0:T(8,128)(2,1)}, u32[]{:S(2)}) copy-start(bf16[96,512]{1,0:T(8,128)(2,1)} %param.13) | copy-start | bytes 294916
  2.7 10.1 %copy-start.3 = (bf16[96,512]{1,0:T(8,128)(2,1)S(1)}, bf16[96,512]{1,0:T(8,128)(2,1)}, u32[]{:S(2)}) copy-start(bf16[96,512]{1,0:T(8,128)(2,1)} %param.14) | copy-start | bytes 294916
  4.1 65.5 %copy-start.6 = (s32[4]{0:T(128)S(1)}, s32[4]{0:T(128)}, u32[]{:S(2)}) copy-start(s32[4]{0:T(128)} %constant.38.clone) | copy-start | bytes 52
  4.1 65.5 %copy-start.7 = (s32[4]{0:T(128)S(1)}, s32[4]{0:T(128)}, u32[]{:S(2)}) copy-start(s32[4]{0:T(128)} %constant.39.clone) | copy-start | bytes 52
  4.1 73.3 %collective-permute-start.6 = (bf16[16,256,256]{2,1,0:T(8,128)(2,1)S(1)}, bf16[16,256,256]{2,1,0:T(8,128)(2,1)}, u32[]{:S(2)}, u32[]{:S(2)}) collective-permute-start(bf16[16,256,256]{2,1,0:T(8,128)(2,1)S(1)} %shard_map.94.own_ref), channel_id=1, source_target_pairs={{0,16},{16,0},{1,17},{17,1},{2,18},{18,2},{3,19},{19,3},{4,20},{20... | collective-permute-start | bytes 6291464 | tf_op jit(solution)/shard_map/ppermute | solution.py:209
  16.7 13.8 %collective-permute-start.7 = (bf16[192,512]{1,0:T(8,128)(2,1)S(1)}, bf16[192,512]{1,0:T(8,128)(2,1)S(1)}, u32[]{:S(2)}, u32[]{:S(2)}) collective-permute-start(bf16[192,512]{1,0:T(8,128)(2,1)S(1)} %bitcast.9), channel_id=1, source_target_pairs={{0,128},{16,400},{128,0},{144,272},{256,384},{272,144},{384,256},{... | collective-permute-start | bytes 589832 | tf_op jit(solution)/shard_map/ppermute | solution.py:177
  30.6 21.3 %collective-permute-start.11 = (bf16[384,512]{1,0:T(8,128)(2,1)S(1)}, bf16[384,512]{1,0:T(8,128)(2,1)}, u32[]{:S(2)}, u32[]{:S(2)}) collective-permute-start(bf16[384,512]{1,0:T(8,128)(2,1)S(1)} %shard_map.95.rest_0_), channel_id=1, source_target_pairs={{0,384},{16,144},{128,256},{144,16},{256,128},{272,400},{384,0},{4... | collective-permute-start | bytes 1179656 | tf_op jit(solution)/shard_map/ppermute | solution.py:177
  38.4 27.7 %collective-permute-start.8 = (bf16[384,512]{1,0:T(8,128)(2,1)S(1)}, bf16[384,512]{1,0:T(8,128)(2,1)S(1)}, u32[]{:S(2)}, u32[]{:S(2)}) collective-permute-start(bf16[384,512]{1,0:T(8,128)(2,1)S(1)} %shard_map.95.rest_0_), channel_id=1, source_target_pairs={{0,32},{16,112},{32,0},{48,80},{64,96},{80,48},{96,64},{112,16},{1... | collective-permute-start | bytes 1179656 | tf_op jit(solution)/shard_map/ppermute | solution.py:177
  51.9 19.6 %collective-permute-start.12 = (bf16[384,512]{1,0:T(8,128)(2,1)}, bf16[384,512]{1,0:T(8,128)(2,1)}, u32[]{:S(2)}, u32[]{:S(2)}) collective-permute-start(bf16[384,512]{1,0:T(8,128)(2,1)} %collective-permute-done.11.rest_0_), channel_id=1, source_target_pairs={{0,32},{16,112},{32,0},{48,80},{64,96},{80,48},{96,64},{112,16},{1... | collective-permute-start | bytes 1179656 | tf_op jit(solution)/shard_map/ppermute | solution.py:177
  60.2 30.3 %all-to-all-start = ((bf16[4,24,512]{2,1,0:T(8,128)(2,1)}), bf16[4,24,512]{2,1,0:T(8,128)(2,1)S(1)}, u32[]{:S(2)}, u32[]{:S(2)}) async-start(bf16[4,24,512]{2,1,0:T(8,128)(2,1)} %bitcast.2), calls=%async_computation | async-start | bytes 196608 | tf_op jit(solution)/shard_map/all_to_all | solution.py:198
  64.2 10.9 %collective-permute-start.9 = (bf16[384,512]{1,0:T(8,128)(2,1)S(1)}, bf16[384,512]{1,0:T(8,128)(2,1)S(1)}, u32[]{:S(2)}, u32[]{:S(2)}) collective-permute-start(bf16[384,512]{1,0:T(8,128)(2,1)S(1)} %shard_map.95.rest_0_), channel_id=1, source_target_pairs={{0,96},{16,48},{32,64},{48,16},{64,32},{80,112},{96,0},{112,80},{1... | collective-permute-start | bytes 1179656 | tf_op jit(solution)/shard_map/ppermute | solution.py:177
  66.2 11.2 %collective-permute-start.10 = (bf16[384,512]{1,0:T(8,128)(2,1)S(1)}, bf16[384,512]{1,0:T(8,128)(2,1)}, u32[]{:S(2)}, u32[]{:S(2)}) collective-permute-start(bf16[384,512]{1,0:T(8,128)(2,1)S(1)} %collective-permute-done.8.rest_1_), channel_id=1, source_target_pairs={{0,96},{16,48},{32,64},{48,16},{64,32},{80,112},{96,0},{112,80},{1... | collective-permute-start | bytes 1179656 | tf_op jit(solution)/shard_map/ppermute | solution.py:177
  69.6 12.3 %collective-permute-start.13 = (bf16[384,512]{1,0:T(8,128)(2,1)}, bf16[384,512]{1,0:T(8,128)(2,1)}, u32[]{:S(2)}, u32[]{:S(2)}) collective-permute-start(bf16[384,512]{1,0:T(8,128)(2,1)} %collective-permute-done.11.rest_0_), channel_id=1, source_target_pairs={{0,96},{16,48},{32,64},{48,16},{64,32},{80,112},{96,0},{112,80},{1... | collective-permute-start | bytes 1179656 | tf_op jit(solution)/shard_map/ppermute | solution.py:177
  71.5 14.0 %collective-permute-start.14 = (bf16[384,512]{1,0:T(8,128)(2,1)}, bf16[384,512]{1,0:T(8,128)(2,1)}, u32[]{:S(2)}, u32[]{:S(2)}) collective-permute-start(bf16[384,512]{1,0:T(8,128)(2,1)} %collective-permute-done.12.rest_1_), channel_id=1, source_target_pairs={{0,96},{16,48},{32,64},{48,16},{64,32},{80,112},{96,0},{112,80},{1... | collective-permute-start | bytes 1179656 | tf_op jit(solution)/shard_map/ppermute | solution.py:177
  90.5 51.1 %copy-start.5 = (s32[1,256]{1,0:T(1,128)S(1)}, s32[1,256]{1,0:T(1,128)}, u32[]{:S(2)}) copy-start(s32[1,256]{1,0:T(1,128)} %param.12) | copy-start | bytes 3076
  90.5 19.6 %all-to-all-start.2 = ((bf16[4,512,256]{2,1,0:T(8,128)(2,1)}), bf16[4,512,256]{2,1,0:T(8,128)(2,1)S(1)}, u32[]{:S(2)}, u32[]{:S(2)}) async-start(bf16[4,512,256]{2,1,0:T(8,128)(2,1)} %shard_map.97), calls=%async_computation.2 | async-start | bytes 2097152 | tf_op jit(solution)/shard_map/all_to_all | solution.py:251
  94.8 17.9 %collective-permute-start.1 = (bf16[24,2048]{1,0:T(8,128)(2,1)S(1)}, bf16[24,2048]{1,0:T(8,128)(2,1)S(1)}, u32[]{:S(2)}, u32[]{:S(2)}) collective-permute-start(bf16[24,2048]{1,0:T(8,128)(2,1)S(1)} %shard_map.91.refs_0_), channel_id=1, source_target_pairs={{0,128},{16,400},{128,0},{144,272},{256,384},{272,144},{384,256},{... | collective-permute-start | bytes 294920 | tf_op jit(solution)/shard_map/ppermute | solution.py:177
  110.1 38.3 %collective-permute-start.15 = (bf16[4,512,256]{2,1,0:T(8,128)(2,1)S(1)}, bf16[4,512,256]{2,1,0:T(8,128)(2,1)S(1)}, u32[]{:S(2)}, u32[]{:S(2)}) collective-permute-start(bf16[4,512,256]{2,1,0:T(8,128)(2,1)S(1)} %all-to-all-done.2.rest_4_), channel_id=1, source_target_pairs={{0,16},{16,0},{1,17},{17,1},{2,18},{18,2},{3,19},{19,3},{4,20},{20... | collective-permute-start | bytes 3145736 | tf_op jit(solution)/shard_map/ppermute | solution.py:252
  112.7 0.6 copy-start.4
  114.3 12.5 %collective-permute-start.2 = (bf16[48,2048]{1,0:T(8,128)(2,1)S(1)}, bf16[48,2048]{1,0:T(8,128)(2,1)S(1)}, u32[]{:S(2)}, u32[]{:S(2)}) collective-permute-start(bf16[48,2048]{1,0:T(8,128)(2,1)S(1)} %shard_map.92.refs_0_), channel_id=1, source_target_pairs={{0,384},{16,144},{128,256},{144,16},{256,128},{272,400},{384,0},{4... | collective-permute-start | bytes 589832 | tf_op jit(solution)/shard_map/ppermute | solution.py:177
  126.7 0.7 copy-start.1
  128.4 11.3 %collective-permute-start.3 = (bf16[96,2048]{1,0:T(8,128)(2,1)S(1)}, bf16[96,2048]{1,0:T(8,128)(2,1)S(1)}, u32[]{:S(2)}, u32[]{:S(2)}) collective-permute-start(bf16[96,2048]{1,0:T(8,128)(2,1)S(1)} %shard_map.93.rest_0_), channel_id=1, source_target_pairs={{0,32},{16,112},{32,0},{48,80},{64,96},{80,48},{96,64},{112,16},{1... | collective-permute-start | bytes 1179656 | tf_op jit(solution)/shard_map/ppermute | solution.py:177
  131.4 14.0 %collective-permute-start.4 = (bf16[96,2048]{1,0:T(8,128)(2,1)S(1)}, bf16[96,2048]{1,0:T(8,128)(2,1)S(1)}, u32[]{:S(2)}, u32[]{:S(2)}) collective-permute-start(bf16[96,2048]{1,0:T(8,128)(2,1)S(1)} %shard_map.93.rest_0_), channel_id=1, source_target_pairs={{0,96},{16,48},{32,64},{48,16},{64,32},{80,112},{96,0},{112,80},{1... | collective-permute-start | bytes 1179656 | tf_op jit(solution)/shard_map/ppermute | solution.py:177
  139.7 8.8 %collective-permute-start.5 = (bf16[96,2048]{1,0:T(8,128)(2,1)S(1)}, bf16[96,2048]{1,0:T(8,128)(2,1)S(1)}, u32[]{:S(2)}, u32[]{:S(2)}) collective-permute-start(bf16[96,2048]{1,0:T(8,128)(2,1)S(1)} %collective-permute-done.3.rest_1_), channel_id=1, source_target_pairs={{0,96},{16,48},{32,64},{48,16},{64,32},{80,112},{96,0},{112,80},{1... | collective-permute-start | bytes 1179656 | tf_op jit(solution)/shard_map/ppermute | solution.py:177
  141.6 3.8 %collective-permute-start = (s32[1,256]{1,0:T(1,128)S(1)}, s32[1,256]{1,0:T(1,128)S(1)}, u32[]{:S(2)}, u32[]{:S(2)}) collective-permute-start(s32[1,256]{1,0:T(1,128)S(1)} %copy-done.5), channel_id=1, source_target_pairs={{0,16},{16,0},{1,17},{17,1},{2,18},{18,2},{3,19},{19,3},{4,20},{20... | collective-permute-start | bytes 3080 | tf_op jit(solution)/shard_map/ppermute | solution.py:210
  152.2 34.0 %all-to-all-start.3 = ((bf16[32,32,384]{2,1,0:T(8,128)(2,1)}), bf16[32,32,384]{2,1,0:T(8,128)(2,1)S(1)}, u32[]{:S(2)}, u32[]{:S(2)}) async-start(bf16[32,32,384]{2,1,0:T(8,128)(2,1)} %shard_map.98), calls=%async_computation.3 | async-start | bytes 1572864 | tf_op jit(solution)/shard_map/all_to_all | solution.py:261

commit v6 on v4

--- a/solution.py
+++ b/solution.py
@@ -52,20 +52,20 @@
         out_ref[m, :, width:] = pad
 
 
-def lay(ord_ref, own_ref, mate_ref, out_ref, places):
+def lay(ord_ref, own_ref, mate_ref, out_ref, first):
     caps, width = own_ref.shape[1], 192
+    places = [4 * q + n for q in range(4) for n in (first, first + 1)]
     for i, k in enumerate(places):
         out_ref[:caps, i * width : (i + 1) * width] = own_ref[ord_ref[k], :, :width]
         out_ref[caps:, i * width : (i + 1) * width] = mate_ref[ord_ref[k], :, :width]
 
 
-def early_body(ord_ref, own_ref, mate_ref, a_ref, b_ref, out_ref, late_ref, now_ref, then_ref, sum_ref, sems):
-    lay(ord_ref, own_ref, mate_ref, then_ref, [4 * q + n for q in range(4) for n in (2, 3)])
+def early_body(ord_ref, own_ref, mate_ref, ab_ref, out_ref, late_ref, now_ref, then_ref, sum_ref, sems):
+    lay(ord_ref, own_ref, mate_ref, then_ref, 2)
     copy = pltpu.make_async_copy(then_ref, late_ref, sems.at[0])
     copy.start()
-    lay(ord_ref, own_ref, mate_ref, now_ref, [4 * q + n for n in (0, 1) for q in range(4)])
-    half = a_ref.shape[0]
-    sum_ref[...] = dot_nn(now_ref[:, :half], a_ref[...]) + dot_nn(now_ref[:, half:], b_ref[...])
+    lay(ord_ref, own_ref, mate_ref, now_ref, 0)
+    sum_ref[...] = dot_nn(now_ref[...], ab_ref[...])
     store = pltpu.make_async_copy(sum_ref, out_ref, sems.at[1])
     store.start()
     copy.wait()
@@ -133,23 +133,18 @@
     out_ref, sems = refs[-2], refs[-1]
     lo, copies = 0, []
     for n, r in enumerate(refs[:-2]):
-        rows = min(r.shape[0], out_ref.shape[1] - lo)
         for q in range(out_ref.shape[0]):
-            copies.append(
-                pltpu.make_async_copy(r.at[pl.ds(0, rows)], out_ref.at[q, pl.ds(lo, rows)], sems.at[n, q])
-            )
-        lo += rows
+            copies.append(pltpu.make_async_copy(r, out_ref.at[q, pl.ds(lo, r.shape[0])], sems.at[n, q]))
+        lo += r.shape[0]
     for copy in copies:
         copy.start()
     for copy in copies:
         copy.wait()
 
 
-def quarter_body(own_ref, got_ref, out_ref):
-    lo = got_ref.shape[0] - 96
+def quarter_body(in_ref, out_ref):
     for x in range(4):
-        out_ref[:24, 512 * x : 512 * (x + 1)] = own_ref[24 * x : 24 * (x + 1), :]
-        out_ref[24:, 512 * x : 512 * (x + 1)] = got_ref[lo + 24 * x : lo + 24 * (x + 1), :]
+        out_ref[:, 512 * x : 512 * (x + 1)] = in_ref[24 * x : 24 * (x + 1), :]
 
 
 def place_body(in_ref, scale_ref, out_ref, scr):
@@ -172,24 +167,23 @@
     return [(2 * i + c, 2 * (i ^ flips[c][step]) + c) for i in range(4) for c in range(2)]
 
 
-def join_body(*refs):
-    lo = 0
-    for r in refs[:-1]:
-        refs[-1][lo : lo + r.shape[0], :] = r[...]
-        lo += r.shape[0]
-
-
-def join(parts):
-    out = jax.ShapeDtypeStruct((sum(p.shape[0] for p in parts), parts[0].shape[1]), BF)
-    return call(join_body, out, [vm()] * len(parts), mib=4)(*parts)
+def join_body(a_ref, b_ref, out_ref):
+    rows = a_ref.shape[0]
+    out_ref[:rows, :] = a_ref[...]
+    out_ref[rows:, :] = b_ref[...]
+
+
+def join(a, b):
+    out = jax.ShapeDtypeStruct((a.shape[0] + b.shape[0], a.shape[1]), BF)
+    return call(join_body, out, [vm(), vm()], mib=4)(a, b)
 
 
 def meet(value, axis, step):
     return lax.ppermute(value, (axis, "c"), pairs(step))
 
 
-def over_y(parts, rows):
-    cols = parts[0].shape[1]
+def over_y(parts):
+    rows, cols = sum(p.shape[0] for p in parts), parts[0].shape[1]
     wide = call(
         spread_body,
         pltpu.HBM((4, rows, cols), BF),
@@ -214,10 +208,11 @@
 
     turned = down_weight.T
     quarter = lax.all_to_all(turned, "x", 0, 0, tiled=True)
+    quarter = call(quarter_body, jax.ShapeDtypeStruct((24, 2048), BF), [vm()], mib=4)(quarter)
+
     flip = jnp.where(c == 0, jnp.array([0, 1, 3, 2]), jnp.array([0, 3, 1, 2])).astype(jnp.int32)
     order = ((zh ^ flip)[None, :] * 4 + jnp.arange(4, dtype=jnp.int32)[:, None]).reshape(16)
-    turned_flip = jnp.where(c == 0, jnp.array([0, 3, 1, 2]), jnp.array([0, 1, 3, 2])).astype(jnp.int32)
-    order_down = ((zh ^ turned_flip)[None, :] * 4 + (y ^ flip)[:, None]).reshape(16)
+    order_down = ((zh ^ flip)[None, :] * 4 + (y ^ flip)[:, None]).reshape(16)
     order = jnp.concatenate([order, order_down, c.reshape(1)]).astype(jnp.int32)
 
     rows = call(
@@ -233,27 +228,28 @@
     )
 
     near = meet(both_rows, "zh", 0)
-    ya = over_y((both_rows,), 192)
-    yb = over_y((near,), 192)
-    far = meet(join((both_rows, near, quarter)), "zh", 1)
-    yc = over_y((far,), 384)
-    ya, yb, yc = ya.reshape(768, 512), yb.reshape(768, 512), yc.reshape(1536, 512)
-
-    two = call(quarter_body, jax.ShapeDtypeStruct((48, 2048), BF), [vm()] * 2, mib=4)(quarter, far)
-    far = pltpu.with_memory_space_constraint(meet(two, "zh", 0), pltpu.HBM)
-    four = join((two, far))
+    both = join(both_rows, near)
+    far = meet(both, "zh", 1)
+    yab = over_y((both,))
+    yc = over_y((far,))
+
+    near = meet(quarter, "zh", 0)
+    two = join(quarter, near)
+    far = pltpu.with_memory_space_constraint(meet(two, "zh", 1), pltpu.HBM)
+    four = join(two, far)
     near = pltpu.with_memory_space_constraint(meet(four, "y", 0), pltpu.HBM)
-    down_first = join((four, near))
+    down_first = join(four, near)
     down_second = meet(down_first, "y", 1)
 
+    yab, yc = yab.reshape(1536, 512), yc.reshape(1536, 512)
     early, rows_late = call(
         early_body,
         [pltpu.HBM((512, 512), F32), pltpu.HBM((512, 1536), BF)],
-        [sm()] + [vm()] * 4,
+        [sm()] + [vm()] * 3,
         scratch=[pltpu.VMEM((512, 1536), BF)] * 2 + [pltpu.VMEM((512, 512), F32), pltpu.SemaphoreType.DMA((2,))],
         flops=512 * 3072 * 512,
         to=hb,
-    )(order, rows, rows_mate, ya, yb)
+    )(order, rows, rows_mate, yab)
     early, rows_late = (pltpu.with_memory_space_constraint(v, pltpu.HBM) for v in (early, rows_late))
     wide = call(
         hidden_body,

time: 192 us -> 195 us (1.016)
  waiting for transfers between devices: 73.8 us -> 78.1 us
  starting transfers between devices: 81.5 us -> 78.9 us
    ppermute x5 -> x6, waiting for transfers between devices: 35.8 us -> 41.4 us  [meet(): return lax.ppermute(value, (axis, 'c'), pairs(step))]
    all_to_all x1, waiting for transfers between devices: 3.68 us -> 0.01 us  [shards(): quarter = lax.all_to_all(turned, 'x', 0, 0, tiled=True)]
    ppermute x1, starting transfers between devices: 9.8 us -> 7.18 us  [shards(): index_mate = lax.ppermute(index_list, 'c', swap)]
    all_to_all x3 -> x2, waiting for transfers between devices: 12.6 us -> 15 us  [over_y(): return lax.all_to_all(wide, 'y', 0, 0, tiled=True)]
    all_to_all x1, starting transfers between devices: 16.4 us -> 18.7 us  [shards(): owned = lax.all_to_all(parts, ('c', 'zl', 'x'), 0, 0, tiled=True)]
    all_to_all x3 -> x2, starting transfers between devices: 12.7 us -> 10.7 us  [over_y(): return lax.all_to_all(wide, 'y', 0, 0, tiled=True)]
    ppermute x5 -> x6, starting transfers between devices: 25 us -> 25.4 us  [meet(): return lax.ppermute(value, (axis, 'c'), pairs(step))]
  transfers between devices with their start and end apart: 14 -> 14, of which waited for: 7 -> 9; matrix products, arithmetic and copies ran while one was open for 1% -> 1% of each run, Pallas kernels for 6% -> 7%
where the time goes in v6:
time: 195 us; the launch traced here: 194 us
  starting transfers between devices  78.9 us (40%)
  waiting for transfers between devices  78.1 us (40%)
  Pallas kernels  20.3 us (10%)
  blocking collectives  10.4 us (5%)
  local copies, waits for them, and re-layouts  4.6 us (2%)
    ppermute x6, waiting for transfers between devices, meet(): return lax.ppermute(value, (axis, 'c'), pairs(step))  41.4 us
    ppermute x6, starting transfers between devices, meet(): return lax.ppermute(value, (axis, 'c'), pairs(step))  25.4 us
    all_to_all x1, waiting for transfers between devices, shards(): owned = lax.all_to_all(parts, ('c', 'zl', 'x'), 0, 0, tiled=True)  20.9 us
    all_to_all x1, starting transfers between devices, shards(): owned = lax.all_to_all(parts, ('c', 'zl', 'x'), 0, 0, tiled=True)  18.7 us
    all_to_all x2, waiting for transfers between devices, over_y(): return lax.all_to_all(wide, 'y', 0, 0, tiled=True)  15 us
    all_to_all x2, starting transfers between devices, over_y(): return lax.all_to_all(wide, 'y', 0, 0, tiled=True)  10.7 us
    all_to_all x1, blocking collectives, shards(): lax.all_to_all(jnp.concatenate(mine, axis=0), 'c', 0, 0, tiled=True)  10.4 us
    ppermute x1, starting transfers between devices, shards(): index_mate = lax.ppermute(index_list, 'c', swap)  7.18 us
  transfers between devices with their start and end apart: 14, of which 9 were waited for; matrix products, arithmetic and copies ran while one was open for 1% of the time, Pallas kernels for 7%

profile of v6, /device:TPU:1, one launch (start us, length us, event | category | flops | bytes accessed | tf_op | source)
XLA Modules:
  0.0 193.5 jit_solution(3092056585388184155)
XLA Ops:
  0.9 10.4 %all_to_all.42 = bf16[2,96,512]{2,1,0:T(8,128)(2,1)S(1)} all-to-all(bf16[2,96,512]{2,1,0:T(8,128)(2,1)S(1)} %bitcast.14), channel_id=1, replica_groups=mesh['zh'=4,'y'=4,'c'=2,'zl'=4,'x'=4] {'c'}, dimensions={0} | all-to-all | bytes 393216 | tf_op jit(solution)/shard_map/all_to_all | solution.py:207
  11.3 7.1 %collective-permute-start.6 = (bf16[192,512]{1,0:T(8,128)(2,1)S(1)}, bf16[192,512]{1,0:T(8,128)(2,1)S(1)}, u32[]{:S(2)}, u32[]{:S(2)}) collective-permute-start(bf16[192,512]{1,0:T(8,128)(2,1)S(1)} %bitcast.11), channel_id=1, source_target_pairs={{0,128},{16,400},{128,0},{144,272},{256,384},{272,144},{384,256},{... | collective-permute-start | bytes 589832 | tf_op jit(solution)/shard_map/ppermute | solution.py:182
  18.4 6.7 %collective-permute-done.6.b_ref = bf16[192,512]{1,0:T(8,128)(2,1)S(1)} collective-permute-done((bf16[192,512]{1,0:T(8,128)(2,1)S(1)}, bf16[192,512]{1,0:T(8,128)(2,1)S(1)}, u32[]{:S(2)}, u32[]{:S(2)}) %collective-permute-start.6) | collective-permute-done | bytes 196640 | tf_op jit(solution)/shard_map/ppermute | solution.py:182
  25.1 1.2 shard_map.97
  26.4 6.4 %all-to-all-start.2 = ((bf16[4,384,512]{2,1,0:T(8,128)(2,1)}), bf16[4,384,512]{2,1,0:T(8,128)(2,1)}, u32[]{:S(2)}, u32[]{:S(2)}) async-start(bf16[4,384,512]{2,1,0:T(8,128)(2,1)} %shard_map.97), calls=%async_computation.2 | async-start | bytes 3145728 | tf_op jit(solution)/shard_map/all_to_all | solution.py:195
  32.9 1.9 copy-done
  34.8 1.3 shard_map.95.own_ref
  36.1 1.9 collective-permute-start.5
  38.1 5.8 %collective-permute-start.7 = (bf16[384,512]{1,0:T(8,128)(2,1)S(1)}, bf16[384,512]{1,0:T(8,128)(2,1)S(1)}, u32[]{:S(2)}, u32[]{:S(2)}) collective-permute-start(bf16[384,512]{1,0:T(8,128)(2,1)S(1)} %shard_map.96.refs_0_), channel_id=1, source_target_pairs={{0,384},{16,144},{128,256},{144,16},{256,128},{272,400},{384,0},{4... | collective-permute-start | bytes 1179656 | tf_op jit(solution)/shard_map/ppermute | solution.py:182
  43.9 19.3 %collective-permute-done.7.refs_0_ = bf16[384,512]{1,0:T(8,128)(2,1)S(1)} collective-permute-done((bf16[384,512]{1,0:T(8,128)(2,1)S(1)}, bf16[384,512]{1,0:T(8,128)(2,1)S(1)}, u32[]{:S(2)}, u32[]{:S(2)}) %collective-permute-start.7) | collective-permute-done | bytes 393248 | tf_op jit(solution)/shard_map/ppermute | solution.py:182
  63.1 1.3 shard_map.99
  64.5 4.3 %all-to-all-start.3 = ((bf16[4,384,512]{2,1,0:T(8,128)(2,1)}), bf16[4,384,512]{2,1,0:T(8,128)(2,1)}, u32[]{:S(2)}, u32[]{:S(2)}) async-start(bf16[4,384,512]{2,1,0:T(8,128)(2,1)} %shard_map.99), calls=%async_computation.3 | async-start | bytes 3145728 | tf_op jit(solution)/shard_map/all_to_all | solution.py:195
  69.2 4.8 %shard_map.98 = (f32[512,512]{1,0:T(8,128)}, bf16[512,1536]{1,0:T(8,128)(2,1)}) custom-call(s32[33]{0:T(128)S(1)} %pad_add_fusion.ord_ref, bf16[16,256,256]{2,1,0:T(8,128)(2,1)S(1)} %shard_map.95.own_ref, bf16[16,256,256]{2,1,0:T(8,128)(2,1)} %collective-permute-done.5.mate_ref, bf16[1536,512]{1,0:T(8,128)(2,1)} %bitcast.7.ab_ref), custom_call_target="tpu_custom_call" | custom-call | flops 805306368 | tf_op jit(solution)/shard_map/pallas_call | solution.py:245
  73.9 15.0 %all-to-all-done.3 = bf16[4,384,512]{2,1,0:T(8,128)(2,1)} async-done(((bf16[4,384,512]{2,1,0:T(8,128)(2,1)}), bf16[4,384,512]{2,1,0:T(8,128)(2,1)}, u32[]{:S(2)}, u32[]{:S(2)}) %all-to-all-start.3) | async-done | bytes 1572896 | tf_op jit(solution)/shard_map/all_to_all | solution.py:195
  89.0 4.1 %all-to-all-start = ((bf16[4,24,512]{2,1,0:T(8,128)(2,1)}), bf16[4,24,512]{2,1,0:T(8,128)(2,1)S(1)}, u32[]{:S(2)}, u32[]{:S(2)}) async-start(bf16[4,24,512]{2,1,0:T(8,128)(2,1)} %bitcast.2), calls=%async_computation | async-start | bytes 196608 | tf_op jit(solution)/shard_map/all_to_all | solution.py:210
  93.0 5.0 %shard_map.100 = bf16[4,512,256]{2,1,0:T(8,128)(2,1)} custom-call(s32[33]{0:T(128)S(1)} %pad_add_fusion.ord_ref, bf16[512,1536]{1,0:T(8,128)(2,1)} %get-tuple-element.7.rows_ref, f32[512,512]{1,0:T(8,128)} %get-tuple-element.8.early_ref, bf16[1536,512]{1,0:T(8,128)(2,1)} %bitcast.8.c_ref), custom_call_target="tpu_custom_call" | custom-call | flops 805306368 | tf_op jit(solution)/shard_map/pallas_call | solution.py:254
  98.0 4.2 %all-to-all-start.4 = ((bf16[4,512,256]{2,1,0:T(8,128)(2,1)}), bf16[4,512,256]{2,1,0:T(8,128)(2,1)S(1)}, u32[]{:S(2)}, u32[]{:S(2)}) async-start(bf16[4,512,256]{2,1,0:T(8,128)(2,1)} %shard_map.100), calls=%async_computation.4 | async-start | bytes 2097152 | tf_op jit(solution)/shard_map/all_to_all | solution.py:268
  102.3 2.7 %collective-permute-start.1 = (bf16[24,2048]{1,0:T(8,128)(2,1)S(1)}, bf16[24,2048]{1,0:T(8,128)(2,1)S(1)}, u32[]{:S(2)}, u32[]{:S(2)}) collective-permute-start(bf16[24,2048]{1,0:T(8,128)(2,1)S(1)} %shard_map.91.a_ref), channel_id=1, source_target_pairs={{0,128},{16,400},{128,0},{144,272},{256,384},{272,144},{384,256},{... | collective-permute-start | bytes 294920 | tf_op jit(solution)/shard_map/ppermute | solution.py:182
  105.0 6.6 %collective-permute-done.1.b_ref = bf16[24,2048]{1,0:T(8,128)(2,1)S(1)} collective-permute-done((bf16[24,2048]{1,0:T(8,128)(2,1)S(1)}, bf16[24,2048]{1,0:T(8,128)(2,1)S(1)}, u32[]{:S(2)}, u32[]{:S(2)}) %collective-permute-start.1) | collective-permute-done | bytes 98336 | tf_op jit(solution)/shard_map/ppermute | solution.py:182
  111.6 4.0 %collective-permute-start.2 = (bf16[48,2048]{1,0:T(8,128)(2,1)S(1)}, bf16[48,2048]{1,0:T(8,128)(2,1)S(1)}, u32[]{:S(2)}, u32[]{:S(2)}) collective-permute-start(bf16[48,2048]{1,0:T(8,128)(2,1)S(1)} %shard_map.92.a_ref), channel_id=1, source_target_pairs={{0,384},{16,144},{128,256},{144,16},{256,128},{272,400},{384,0},{4... | collective-permute-start | bytes 589832 | tf_op jit(solution)/shard_map/ppermute | solution.py:182
  115.6 6.5 %collective-permute-done.2.b_ref = bf16[48,2048]{1,0:T(8,128)(2,1)S(1)} collective-permute-done((bf16[48,2048]{1,0:T(8,128)(2,1)S(1)}, bf16[48,2048]{1,0:T(8,128)(2,1)S(1)}, u32[]{:S(2)}, u32[]{:S(2)}) %collective-permute-start.2) | collective-permute-done | bytes 196640 | tf_op jit(solution)/shard_map/ppermute | solution.py:182
  122.8 1.0 shard_map.93.a_ref
  123.7 2.8 %collective-permute-start.3 = (bf16[96,2048]{1,0:T(8,128)(2,1)S(1)}, bf16[96,2048]{1,0:T(8,128)(2,1)S(1)}, u32[]{:S(2)}, u32[]{:S(2)}) collective-permute-start(bf16[96,2048]{1,0:T(8,128)(2,1)S(1)} %shard_map.93.a_ref), channel_id=1, source_target_pairs={{0,32},{16,112},{32,0},{48,80},{64,96},{80,48},{96,64},{112,16},{1... | collective-permute-start | bytes 1179656 | tf_op jit(solution)/shard_map/ppermute | solution.py:182
  126.6 6.6 %collective-permute-start.8 = (bf16[4,512,256]{2,1,0:T(8,128)(2,1)S(1)}, bf16[4,512,256]{2,1,0:T(8,128)(2,1)S(1)}, u32[]{:S(2)}, u32[]{:S(2)}) collective-permute-start(bf16[4,512,256]{2,1,0:T(8,128)(2,1)S(1)} %all-to-all-done.4.hid_ref), channel_id=1, source_target_pairs={{0,16},{16,0},{1,17},{17,1},{2,18},{18,2},{3,19},{19,3},{4,20},{20... | collective-permute-start | bytes 3145736 | tf_op jit(solution)/shard_map/ppermute | solution.py:269
  134.2 1.0 shard_map.94.first_ref
  135.3 2.9 %collective-permute-start.4 = (bf16[192,2048]{1,0:T(8,128)(2,1)S(1)}, bf16[192,2048]{1,0:T(8,128)(2,1)S(1)}, u32[]{:S(2)}, u32[]{:S(2)}) collective-permute-start(bf16[192,2048]{1,0:T(8,128)(2,1)S(1)} %shard_map.94.first_ref), channel_id=1, source_target_pairs={{0,96},{16,48},{32,64},{48,16},{64,32},{80,112},{96,0},{112,80},{1... | collective-permute-start | bytes 2359304 | tf_op jit(solution)/shard_map/ppermute | solution.py:182
  138.2 7.2 %collective-permute-start = (s32[1,256]{1,0:T(1,128)S(1)}, s32[1,256]{1,0:T(1,128)S(1)}, u32[]{:S(2)}, u32[]{:S(2)}) collective-permute-start(s32[1,256]{1,0:T(1,128)S(1)} %copy-done.3), channel_id=1, source_target_pairs={{0,16},{16,0},{1,17},{17,1},{2,18},{18,2},{3,19},{19,3},{4,20},{20... | collective-permute-start | bytes 3080 | tf_op jit(solution)/shard_map/ppermute | solution.py:223
  146.2 2.1 %collective-permute-done.4.second_ref = bf16[192,2048]{1,0:T(8,128)(2,1)S(1)} collective-permute-done((bf16[192,2048]{1,0:T(8,128)(2,1)S(1)}, bf16[192,2048]{1,0:T(8,128)(2,1)S(1)}, u32[]{:S(2)}, u32[]{:S(2)}) %collective-permute-start.4) | collective-permute-done | bytes 786464 | tf_op jit(solution)/shard_map/ppermute | solution.py:182
  148.3 3.0 %shard_map.101 = bf16[32,32,384]{2,1,0:T(8,128)(2,1)} custom-call(s32[33]{0:T(128)S(1)} %pad_add_fusion.ord_ref, s32[2,256]{1,0:T(2,128)S(1)} %add_select_fusion.idx_ref, bf16[192,2048]{1,0:T(8,128)(2,1)S(1)} %shard_map.94.first_ref, bf16[192,2048]{1,0:T(8,128)(2,1)S(1)} %collective-permute-done.4.second_ref, ...), custom_call_target="tpu_custom_call" | custom-call | flops 805306368 | tf_op jit(solution)/shard_map/pallas_call | solution.py:271
  151.3 18.7 %all-to-all-start.5 = ((bf16[32,32,384]{2,1,0:T(8,128)(2,1)}), bf16[32,32,384]{2,1,0:T(8,128)(2,1)S(1)}, u32[]{:S(2)}, u32[]{:S(2)}) async-start(bf16[32,32,384]{2,1,0:T(8,128)(2,1)} %shard_map.101), calls=%async_computation.5 | async-start | bytes 1572864 | tf_op jit(solution)/shard_map/all_to_all | solution.py:278
  171.0 20.9 %all-to-all-done.5.in_ref = bf16[32,32,384]{2,1,0:T(8,128)(2,1)S(1)} async-done(((bf16[32,32,384]{2,1,0:T(8,128)(2,1)}), bf16[32,32,384]{2,1,0:T(8,128)(2,1)S(1)}, u32[]{:S(2)}, u32[]{:S(2)}) %all-to-all-start.5) | async-done | bytes 786464 | tf_op jit(solution)/shard_map/all_to_all | solution.py:278
  191.9 1.6 shard_map.102
  (32 shorter events, 4.8 us)
Async XLA Ops:
  11.3 13.8 %collective-permute-start.6 = (bf16[192,512]{1,0:T(8,128)(2,1)S(1)}, bf16[192,512]{1,0:T(8,128)(2,1)S(1)}, u32[]{:S(2)}, u32[]{:S(2)}) collective-permute-start(bf16[192,512]{1,0:T(8,128)(2,1)S(1)} %bitcast.11), channel_id=1, source_target_pairs={{0,128},{16,400},{128,0},{144,272},{256,384},{272,144},{384,256},{... | collective-permute-start | bytes 589832 | tf_op jit(solution)/shard_map/ppermute | solution.py:182
  26.4 6.4 %copy-start.3 = (s32[1,256]{1,0:T(1,128)S(1)}, s32[1,256]{1,0:T(1,128)}, u32[]{:S(2)}) copy-start(s32[1,256]{1,0:T(1,128)} %param.12) | copy-start | bytes 3076
  26.4 38.1 %all-to-all-start.2 = ((bf16[4,384,512]{2,1,0:T(8,128)(2,1)}), bf16[4,384,512]{2,1,0:T(8,128)(2,1)}, u32[]{:S(2)}, u32[]{:S(2)}) async-start(bf16[4,384,512]{2,1,0:T(8,128)(2,1)} %shard_map.97), calls=%async_computation.2 | async-start | bytes 3145728 | tf_op jit(solution)/shard_map/all_to_all | solution.py:195
  32.9 1.9 copy-start
  36.1 33.0 %collective-permute-start.5 = (bf16[16,256,256]{2,1,0:T(8,128)(2,1)S(1)}, bf16[16,256,256]{2,1,0:T(8,128)(2,1)}, u32[]{:S(2)}, u32[]{:S(2)}) collective-permute-start(bf16[16,256,256]{2,1,0:T(8,128)(2,1)S(1)} %shard_map.95.own_ref), channel_id=1, source_target_pairs={{0,16},{16,0},{1,17},{17,1},{2,18},{18,2},{3,19},{19,3},{4,20},{20... | collective-permute-start | bytes 6291464 | tf_op jit(solution)/shard_map/ppermute | solution.py:222
  38.1 25.1 %collective-permute-start.7 = (bf16[384,512]{1,0:T(8,128)(2,1)S(1)}, bf16[384,512]{1,0:T(8,128)(2,1)S(1)}, u32[]{:S(2)}, u32[]{:S(2)}) collective-permute-start(bf16[384,512]{1,0:T(8,128)(2,1)S(1)} %shard_map.96.refs_0_), channel_id=1, source_target_pairs={{0,384},{16,144},{128,256},{144,16},{256,128},{272,400},{384,0},{4... | collective-permute-start | bytes 1179656 | tf_op jit(solution)/shard_map/ppermute | solution.py:182
  64.4 4.4 %copy-start.4 = (s32[4]{0:T(128)S(1)}, s32[4]{0:T(128)}, u32[]{:S(2)}) copy-start(s32[4]{0:T(128)} %constant.38.clone) | copy-start | bytes 52
  64.4 4.4 %copy-start.5 = (s32[4]{0:T(128)S(1)}, s32[4]{0:T(128)}, u32[]{:S(2)}) copy-start(s32[4]{0:T(128)} %constant.39.clone) | copy-start | bytes 52
  64.5 24.5 %all-to-all-start.3 = ((bf16[4,384,512]{2,1,0:T(8,128)(2,1)}), bf16[4,384,512]{2,1,0:T(8,128)(2,1)}, u32[]{:S(2)}, u32[]{:S(2)}) async-start(bf16[4,384,512]{2,1,0:T(8,128)(2,1)} %shard_map.99), calls=%async_computation.3 | async-start | bytes 3145728 | tf_op jit(solution)/shard_map/all_to_all | solution.py:195
  89.0 9.1 %all-to-all-start = ((bf16[4,24,512]{2,1,0:T(8,128)(2,1)}), bf16[4,24,512]{2,1,0:T(8,128)(2,1)S(1)}, u32[]{:S(2)}, u32[]{:S(2)}) async-start(bf16[4,24,512]{2,1,0:T(8,128)(2,1)} %bitcast.2), calls=%async_computation | async-start | bytes 196608 | tf_op jit(solution)/shard_map/all_to_all | solution.py:210
  98.0 28.5 %all-to-all-start.4 = ((bf16[4,512,256]{2,1,0:T(8,128)(2,1)}), bf16[4,512,256]{2,1,0:T(8,128)(2,1)S(1)}, u32[]{:S(2)}, u32[]{:S(2)}) async-start(bf16[4,512,256]{2,1,0:T(8,128)(2,1)} %shard_map.100), calls=%async_computation.4 | async-start | bytes 2097152 | tf_op jit(solution)/shard_map/all_to_all | solution.py:268
  102.3 9.3 %collective-permute-start.1 = (bf16[24,2048]{1,0:T(8,128)(2,1)S(1)}, bf16[24,2048]{1,0:T(8,128)(2,1)S(1)}, u32[]{:S(2)}, u32[]{:S(2)}) collective-permute-start(bf16[24,2048]{1,0:T(8,128)(2,1)S(1)} %shard_map.91.a_ref), channel_id=1, source_target_pairs={{0,128},{16,400},{128,0},{144,272},{256,384},{272,144},{384,256},{... | collective-permute-start | bytes 294920 | tf_op jit(solution)/shard_map/ppermute | solution.py:182
  111.6 10.5 %collective-permute-start.2 = (bf16[48,2048]{1,0:T(8,128)(2,1)S(1)}, bf16[48,2048]{1,0:T(8,128)(2,1)S(1)}, u32[]{:S(2)}, u32[]{:S(2)}) collective-permute-start(bf16[48,2048]{1,0:T(8,128)(2,1)S(1)} %shard_map.92.a_ref), channel_id=1, source_target_pairs={{0,384},{16,144},{128,256},{144,16},{256,128},{272,400},{384,0},{4... | collective-permute-start | bytes 589832 | tf_op jit(solution)/shard_map/ppermute | solution.py:182
  122.1 0.7 copy-start.2
  123.7 9.7 %collective-permute-start.3 = (bf16[96,2048]{1,0:T(8,128)(2,1)S(1)}, bf16[96,2048]{1,0:T(8,128)(2,1)S(1)}, u32[]{:S(2)}, u32[]{:S(2)}) collective-permute-start(bf16[96,2048]{1,0:T(8,128)(2,1)S(1)} %shard_map.93.a_ref), channel_id=1, source_target_pairs={{0,32},{16,112},{32,0},{48,80},{64,96},{80,48},{96,64},{112,16},{1... | collective-permute-start | bytes 1179656 | tf_op jit(solution)/shard_map/ppermute | solution.py:182
  126.6 21.7 %collective-permute-start.8 = (bf16[4,512,256]{2,1,0:T(8,128)(2,1)S(1)}, bf16[4,512,256]{2,1,0:T(8,128)(2,1)S(1)}, u32[]{:S(2)}, u32[]{:S(2)}) collective-permute-start(bf16[4,512,256]{2,1,0:T(8,128)(2,1)S(1)} %all-to-all-done.4.hid_ref), channel_id=1, source_target_pairs={{0,16},{16,0},{1,17},{17,1},{2,18},{18,2},{3,19},{19,3},{4,20},{20... | collective-permute-start | bytes 3145736 | tf_op jit(solution)/shard_map/ppermute | solution.py:269
  133.5 0.7 copy-start.1
  135.3 13.0 %collective-permute-start.4 = (bf16[192,2048]{1,0:T(8,128)(2,1)S(1)}, bf16[192,2048]{1,0:T(8,128)(2,1)S(1)}, u32[]{:S(2)}, u32[]{:S(2)}) collective-permute-start(bf16[192,2048]{1,0:T(8,128)(2,1)S(1)} %shard_map.94.first_ref), channel_id=1, source_target_pairs={{0,96},{16,48},{32,64},{48,16},{64,32},{80,112},{96,0},{112,80},{1... | collective-permute-start | bytes 2359304 | tf_op jit(solution)/shard_map/ppermute | solution.py:182
  138.2 8.0 %collective-permute-start = (s32[1,256]{1,0:T(1,128)S(1)}, s32[1,256]{1,0:T(1,128)S(1)}, u32[]{:S(2)}, u32[]{:S(2)}) collective-permute-start(s32[1,256]{1,0:T(1,128)S(1)} %copy-done.3), channel_id=1, source_target_pairs={{0,16},{16,0},{1,17},{17,1},{2,18},{18,2},{3,19},{19,3},{4,20},{20... | collective-permute-start | bytes 3080 | tf_op jit(solution)/shard_map/ppermute | solution.py:223
  151.3 40.5 %all-to-all-start.5 = ((bf16[32,32,384]{2,1,0:T(8,128)(2,1)}), bf16[32,32,384]{2,1,0:T(8,128)(2,1)S(1)}, u32[]{:S(2)}, u32[]{:S(2)}) async-start(bf16[32,32,384]{2,1,0:T(8,128)(2,1)} %shard_map.101), calls=%async_computation.5 | async-start | bytes 1572864 | tf_op jit(solution)/shard_map/all_to_all | solution.py:278

commit v7 on v6

--- a/solution.py
+++ b/solution.py
@@ -52,42 +52,49 @@
         out_ref[m, :, width:] = pad
 
 
-def lay(ord_ref, own_ref, mate_ref, out_ref, first):
+def lay(ord_ref, own_ref, mate_ref, out_ref, places):
     caps, width = own_ref.shape[1], 192
-    places = [4 * q + n for q in range(4) for n in (first, first + 1)]
     for i, k in enumerate(places):
         out_ref[:caps, i * width : (i + 1) * width] = own_ref[ord_ref[k], :, :width]
         out_ref[caps:, i * width : (i + 1) * width] = mate_ref[ord_ref[k], :, :width]
 
 
-def early_body(ord_ref, own_ref, mate_ref, ab_ref, out_ref, late_ref, now_ref, then_ref, sum_ref, sems):
-    lay(ord_ref, own_ref, mate_ref, then_ref, 2)
+def early_body(ord_ref, own_ref, mate_ref, *rest):
+    piece_refs, (out_ref, late_ref, now_ref, then_ref, sum_ref, sems) = rest[:4], rest[4:]
+    lay(ord_ref, own_ref, mate_ref, then_ref, [4 * q + n for q in range(4) for n in (2, 3)])
     copy = pltpu.make_async_copy(then_ref, late_ref, sems.at[0])
     copy.start()
-    lay(ord_ref, own_ref, mate_ref, now_ref, 0)
-    sum_ref[...] = dot_nn(now_ref[...], ab_ref[...])
+    lay(ord_ref, own_ref, mate_ref, now_ref, [16 + 4 * q + n for q in range(4) for n in (0, 1)])
+    acc = None
+    for q, piece in enumerate(piece_refs):
+        part = dot_nn(now_ref[:, 384 * q : 384 * (q + 1)], piece[...])
+        acc = part if acc is None else acc + part
+    sum_ref[...] = acc
     store = pltpu.make_async_copy(sum_ref, out_ref, sems.at[1])
     store.start()
     copy.wait()
     store.wait()
 
 
-def hidden_body(ord_ref, rows_ref, early_ref, c_ref, out_ref, res_ref, rows_vmem, sum_ref, sems, out_sems):
+def hidden_body(ord_ref, rows_ref, early_ref, c_ref, out_ref, res_ref, rows_vmem, c_vmem, sum_ref, sems, out_sems):
     caps = rows_ref.shape[0] // 2
     half = rows_ref.shape[1] // 2
     core = ord_ref[32]
-    copies = [
-        pltpu.make_async_copy(rows_ref.at[:, pl.ds(n * half, half)], rows_vmem.at[:, pl.ds(n * half, half)], sems.at[n])
-        for n in range(2)
-    ] + [pltpu.make_async_copy(early_ref, sum_ref, sems.at[2])]
+    copies = []
+    for n in range(2):
+        cut = pl.ds(n * half, half)
+        copies.append(pltpu.make_async_copy(rows_ref.at[:, cut], rows_vmem.at[:, cut], sems.at[2 * n]))
+        copies.append(pltpu.make_async_copy(c_ref.at[cut], c_vmem.at[cut], sems.at[2 * n + 1]))
+    copies.append(pltpu.make_async_copy(early_ref, sum_ref, sems.at[4]))
     for copy in copies:
         copy.start()
     acc = None
     for n in range(2):
-        copies[n].wait()
-        part = dot_nn(rows_vmem[:, n * half : (n + 1) * half], c_ref[n * half : (n + 1) * half, :])
+        copies[2 * n].wait()
+        copies[2 * n + 1].wait()
+        part = dot_nn(rows_vmem[:, n * half : (n + 1) * half], c_vmem[n * half : (n + 1) * half, :])
         acc = part if acc is None else acc + part
-    copies[2].wait()
+    copies[4].wait()
     acc = acc + sum_ref[...]
     cols = []
     for s in range(2):
@@ -195,6 +202,12 @@
     return lax.all_to_all(wide, "y", 0, 0, tiled=True)
 
 
+def near_y(value):
+    near = meet(value, "y", 0)
+    other = meet(value, "y", 1)
+    return value, near, other, meet(near, "y", 1)
+
+
 def shards(tokens, expert_ids, route_weight, index_list, gate_weight, up_weight, down_weight):
     zh, y, c, zl, x = (lax.axis_index(n) for n in ("zh", "y", "c", "zl", "x"))
     caps = index_list.shape[1]
@@ -230,7 +243,7 @@
     near = meet(both_rows, "zh", 0)
     both = join(both_rows, near)
     far = meet(both, "zh", 1)
-    yab = over_y((both,))
+    soon = near_y(both)
     yc = over_y((far,))
 
     near = meet(quarter, "zh", 0)
@@ -241,25 +254,26 @@
     down_first = join(four, near)
     down_second = meet(down_first, "y", 1)
 
-    yab, yc = yab.reshape(1536, 512), yc.reshape(1536, 512)
+    yc = yc.reshape(1536, 512)
     early, rows_late = call(
         early_body,
         [pltpu.HBM((512, 512), F32), pltpu.HBM((512, 1536), BF)],
-        [sm()] + [vm()] * 3,
+        [sm()] + [vm()] * 6,
         scratch=[pltpu.VMEM((512, 1536), BF)] * 2 + [pltpu.VMEM((512, 512), F32), pltpu.SemaphoreType.DMA((2,))],
         flops=512 * 3072 * 512,
         to=hb,
-    )(order, rows, rows_mate, yab)
+    )(order, rows, rows_mate, *soon)
     early, rows_late = (pltpu.with_memory_space_constraint(v, pltpu.HBM) for v in (early, rows_late))
     wide = call(
         hidden_body,
         pltpu.HBM((4, 512, 256), BF),
-        [sm(), hb(), hb(), vm()],
+        [sm(), hb(), hb(), hb()],
         scratch=[
             pltpu.VMEM((512, 256), BF),
             pltpu.VMEM((512, 1536), BF),
+            pltpu.VMEM((1536, 512), BF),
             pltpu.VMEM((512, 512), F32),
-            pltpu.SemaphoreType.DMA((3,)),
+            pltpu.SemaphoreType.DMA((5,)),
             pltpu.SemaphoreType.DMA((4,)),
         ],
         flops=512 * 3072 * 512,

time: 195 us -> 214 us (1.097)
  waiting for transfers between devices: 78.1 us -> 96.8 us
  starting transfers between devices: 78.9 us -> 88.8 us
  blocking collectives: 10.4 us -> 3.8 us
    ppermute x6 -> x9, waiting for transfers between devices: 41.4 us -> 75 us  [meet(): return lax.ppermute(value, (axis, 'c'), pairs(step))]
    all_to_all x2 -> x1, waiting for transfers between devices: 15 us -> 0.01 us  [over_y(): return lax.all_to_all(wide, 'y', 0, 0, tiled=True)]
    ppermute x6 -> x9, starting transfers between devices: 25.4 us -> 35 us  [meet(): return lax.ppermute(value, (axis, 'c'), pairs(step))]
    ppermute x1, starting transfers between devices: 1.92 us -> 8.75 us  [shards(): rows_mate = lax.ppermute(rows, 'c', swap)]
    all_to_all x1, blocking collectives: 10.4 us -> 3.8 us  [shards(): lax.all_to_all(jnp.concatenate(mine, axis=0), 'c', 0, 0, tiled=True)]
    ppermute x1, starting transfers between devices: 6.63 us -> 1.92 us  [shards(): hid_mate = lax.ppermute(hid, 'c', swap)]
    all_to_all x2 -> x1, starting transfers between devices: 10.7 us -> 7.86 us  [over_y(): return lax.all_to_all(wide, 'y', 0, 0, tiled=True)]
  transfers between devices with their start and end apart: 14 -> 16, of which waited for: 9 -> 10; matrix products, arithmetic and copies ran while one was open for 1% -> 1% of each run, Pallas kernels for 7% -> 6%
where the time goes in v7:
time: 214 us; the launch traced here: 213 us
  waiting for transfers between devices  96.8 us (45%)
  starting transfers between devices  88.8 us (41%)
  Pallas kernels  18.3 us (9%)
  local copies, waits for them, and re-layouts  4.44 us (2%)
  blocking collectives  3.8 us (2%)
    ppermute x9, waiting for transfers between devices, meet(): return lax.ppermute(value, (axis, 'c'), pairs(step))  75 us
    ppermute x9, starting transfers between devices, meet(): return lax.ppermute(value, (axis, 'c'), pairs(step))  35 us
    all_to_all x1, waiting for transfers between devices, shards(): owned = lax.all_to_all(parts, ('c', 'zl', 'x'), 0, 0, tiled=True)  20.9 us
    all_to_all x1, starting transfers between devices, shards(): owned = lax.all_to_all(parts, ('c', 'zl', 'x'), 0, 0, tiled=True)  19 us
    ppermute x1, starting transfers between devices, shards(): rows_mate = lax.ppermute(rows, 'c', swap)  8.75 us
    ppermute x1, starting transfers between devices, shards(): index_mate = lax.ppermute(index_list, 'c', swap)  8.04 us
    all_to_all x1, starting transfers between devices, over_y(): return lax.all_to_all(wide, 'y', 0, 0, tiled=True)  7.86 us
    pallas_call x1, Pallas kernels, shards(): call(hidden_body, pltpu.HBM((4, 512, 256), BF), [sm(), hb(), hb(), hb()],...  4.59 us
  transfers between devices with their start and end apart: 16, of which 10 were waited for; matrix products, arithmetic and copies ran while one was open for 1% of the time, Pallas kernels for 6%

profile of v7, /device:TPU:1, one launch (start us, length us, event | category | flops | bytes accessed | tf_op | source)
XLA Modules:
  0.0 213.4 jit_solution(2582411348868280757)
XLA Ops:
  0.8 1.9 copy-done
  2.7 1.3 shard_map.95.own_ref
  4.1 8.7 %collective-permute-start.5 = (bf16[16,256,256]{2,1,0:T(8,128)(2,1)S(1)}, bf16[16,256,256]{2,1,0:T(8,128)(2,1)}, u32[]{:S(2)}, u32[]{:S(2)}) collective-permute-start(bf16[16,256,256]{2,1,0:T(8,128)(2,1)S(1)} %shard_map.95.own_ref), channel_id=1, source_target_pairs={{0,16},{16,0},{1,17},{17,1},{2,18},{18,2},{3,19},{19,3},{4,20},{20... | collective-permute-start | bytes 6291464 | tf_op jit(solution)/shard_map/ppermute | solution.py:235
  12.9 3.8 %all_to_all.37 = bf16[2,96,512]{2,1,0:T(8,128)(2,1)S(1)} all-to-all(bf16[2,96,512]{2,1,0:T(8,128)(2,1)S(1)} %bitcast.13), channel_id=1, replica_groups=mesh['zh'=4,'y'=4,'c'=2,'zl'=4,'x'=4] {'c'}, dimensions={0} | all-to-all | bytes 393216 | tf_op jit(solution)/shard_map/all_to_all | solution.py:220
  16.7 7.1 %collective-permute-start.6 = (bf16[192,512]{1,0:T(8,128)(2,1)S(1)}, bf16[192,512]{1,0:T(8,128)(2,1)S(1)}, u32[]{:S(2)}, u32[]{:S(2)}) collective-permute-start(bf16[192,512]{1,0:T(8,128)(2,1)S(1)} %bitcast.10), channel_id=1, source_target_pairs={{0,128},{16,400},{128,0},{144,272},{256,384},{272,144},{384,256},{... | collective-permute-start | bytes 589832 | tf_op jit(solution)/shard_map/ppermute | solution.py:189
  23.8 6.7 %collective-permute-done.6.b_ref = bf16[192,512]{1,0:T(8,128)(2,1)S(1)} collective-permute-done((bf16[192,512]{1,0:T(8,128)(2,1)S(1)}, bf16[192,512]{1,0:T(8,128)(2,1)S(1)}, u32[]{:S(2)}, u32[]{:S(2)}) %collective-permute-start.6) | collective-permute-done | bytes 196640 | tf_op jit(solution)/shard_map/ppermute | solution.py:189
  30.6 7.8 %collective-permute-start.10 = (bf16[384,512]{1,0:T(8,128)(2,1)S(1)}, bf16[384,512]{1,0:T(8,128)(2,1)S(1)}, u32[]{:S(2)}, u32[]{:S(2)}) collective-permute-start(bf16[384,512]{1,0:T(8,128)(2,1)S(1)} %shard_map.96.rest_0_), channel_id=1, source_target_pairs={{0,384},{16,144},{128,256},{144,16},{256,128},{272,400},{384,0},{4... | collective-permute-start | bytes 1179656 | tf_op jit(solution)/shard_map/ppermute | solution.py:189
  38.4 13.4 %collective-permute-done.10.refs_0_ = bf16[384,512]{1,0:T(8,128)(2,1)S(1)} collective-permute-done((bf16[384,512]{1,0:T(8,128)(2,1)S(1)}, bf16[384,512]{1,0:T(8,128)(2,1)S(1)}, u32[]{:S(2)}, u32[]{:S(2)}) %collective-permute-start.10) | collective-permute-done | bytes 393248 | tf_op jit(solution)/shard_map/ppermute | solution.py:189
  53.0 7.9 %all-to-all-start.2 = ((bf16[4,384,512]{2,1,0:T(8,128)(2,1)}), bf16[4,384,512]{2,1,0:T(8,128)(2,1)}, u32[]{:S(2)}, u32[]{:S(2)}) async-start(bf16[4,384,512]{2,1,0:T(8,128)(2,1)} %shard_map.98), calls=%async_computation.2 | async-start | bytes 3145728 | tf_op jit(solution)/shard_map/all_to_all | solution.py:202
  60.9 4.8 %collective-permute-start.7 = (bf16[384,512]{1,0:T(8,128)(2,1)S(1)}, bf16[384,512]{1,0:T(8,128)(2,1)S(1)}, u32[]{:S(2)}, u32[]{:S(2)}) collective-permute-start(bf16[384,512]{1,0:T(8,128)(2,1)S(1)} %shard_map.96.rest_0_), channel_id=1, source_target_pairs={{0,32},{16,112},{32,0},{48,80},{64,96},{80,48},{96,64},{112,16},{1... | collective-permute-start | bytes 1179656 | tf_op jit(solution)/shard_map/ppermute | solution.py:189
  65.7 1.9 collective-permute-start.8
  67.6 21.0 %collective-permute-done.7.rest_1_ = bf16[384,512]{1,0:T(8,128)(2,1)S(1)} collective-permute-done((bf16[384,512]{1,0:T(8,128)(2,1)S(1)}, bf16[384,512]{1,0:T(8,128)(2,1)S(1)}, u32[]{:S(2)}, u32[]{:S(2)}) %collective-permute-start.7) | collective-permute-done | bytes 393248 | tf_op jit(solution)/shard_map/ppermute | solution.py:189
  88.6 1.9 collective-permute-start.9
  90.9 6.5 %collective-permute-done.9.rest_3_ = bf16[384,512]{1,0:T(8,128)(2,1)} collective-permute-done((bf16[384,512]{1,0:T(8,128)(2,1)S(1)}, bf16[384,512]{1,0:T(8,128)(2,1)}, u32[]{:S(2)}, u32[]{:S(2)}) %collective-permute-start.9) | collective-permute-done | bytes 393248 | tf_op jit(solution)/shard_map/ppermute | solution.py:189
  97.4 4.5 %shard_map.97 = (f32[512,512]{1,0:T(8,128)}, bf16[512,1536]{1,0:T(8,128)(2,1)}) custom-call(s32[33]{0:T(128)S(1)} %pad_add_fusion.ord_ref, bf16[16,256,256]{2,1,0:T(8,128)(2,1)S(1)} %shard_map.95.own_ref, bf16[16,256,256]{2,1,0:T(8,128)(2,1)} %collective-permute-done.5.mate_ref, bf16[384,512]{1,0:T(8,128)(2,1)S(1)} %shard_map.96.rest_0_, ...), custom_call_target="tpu_custom_call" | custom-call | flops 805306368 | tf_op jit(solution)/shard_map/pallas_call | solution.py:258
  101.9 4.0 %all-to-all-start = ((bf16[4,24,512]{2,1,0:T(8,128)(2,1)}), bf16[4,24,512]{2,1,0:T(8,128)(2,1)S(1)}, u32[]{:S(2)}, u32[]{:S(2)}) async-start(bf16[4,24,512]{2,1,0:T(8,128)(2,1)} %bitcast.2), calls=%async_computation | async-start | bytes 196608 | tf_op jit(solution)/shard_map/all_to_all | solution.py:223
  105.9 4.6 %shard_map.99 = bf16[4,512,256]{2,1,0:T(8,128)(2,1)} custom-call(s32[33]{0:T(128)S(1)} %pad_add_fusion.ord_ref, bf16[512,1536]{1,0:T(8,128)(2,1)} %get-tuple-element.7.rows_ref, f32[512,512]{1,0:T(8,128)} %get-tuple-element.8.early_ref, bf16[1536,512]{1,0:T(8,128)(2,1)} %bitcast.7.c_ref), custom_call_target="tpu_custom_call" | custom-call | flops 805306368 | tf_op jit(solution)/shard_map/pallas_call | solution.py:267
  110.5 4.2 %all-to-all-start.3 = ((bf16[4,512,256]{2,1,0:T(8,128)(2,1)}), bf16[4,512,256]{2,1,0:T(8,128)(2,1)S(1)}, u32[]{:S(2)}, u32[]{:S(2)}) async-start(bf16[4,512,256]{2,1,0:T(8,128)(2,1)} %shard_map.99), calls=%async_computation.3 | async-start | bytes 2097152 | tf_op jit(solution)/shard_map/all_to_all | solution.py:282
  114.8 5.5 %collective-permute-start.1 = (bf16[24,2048]{1,0:T(8,128)(2,1)S(1)}, bf16[24,2048]{1,0:T(8,128)(2,1)S(1)}, u32[]{:S(2)}, u32[]{:S(2)}) collective-permute-start(bf16[24,2048]{1,0:T(8,128)(2,1)S(1)} %shard_map.91.a_ref), channel_id=1, source_target_pairs={{0,128},{16,400},{128,0},{144,272},{256,384},{272,144},{384,256},{... | collective-permute-start | bytes 294920 | tf_op jit(solution)/shard_map/ppermute | solution.py:189
  120.3 3.8 %collective-permute-done.1.b_ref = bf16[24,2048]{1,0:T(8,128)(2,1)S(1)} collective-permute-done((bf16[24,2048]{1,0:T(8,128)(2,1)S(1)}, bf16[24,2048]{1,0:T(8,128)(2,1)S(1)}, u32[]{:S(2)}, u32[]{:S(2)}) %collective-permute-start.1) | collective-permute-done | bytes 98336 | tf_op jit(solution)/shard_map/ppermute | solution.py:189
  124.2 1.9 collective-permute-start.2
  126.1 15.6 %collective-permute-done.2.b_ref = bf16[48,2048]{1,0:T(8,128)(2,1)S(1)} collective-permute-done((bf16[48,2048]{1,0:T(8,128)(2,1)S(1)}, bf16[48,2048]{1,0:T(8,128)(2,1)S(1)}, u32[]{:S(2)}, u32[]{:S(2)}) %collective-permute-start.2) | collective-permute-done | bytes 196640 | tf_op jit(solution)/shard_map/ppermute | solution.py:189
  143.4 2.1 collective-permute-start.3
  145.4 1.9 collective-permute-start.11
  147.4 5.7 %collective-permute-done.3.b_ref = bf16[96,2048]{1,0:T(8,128)(2,1)S(1)} collective-permute-done((bf16[96,2048]{1,0:T(8,128)(2,1)S(1)}, bf16[96,2048]{1,0:T(8,128)(2,1)S(1)}, u32[]{:S(2)}, u32[]{:S(2)}) %collective-permute-start.3) | collective-permute-done | bytes 393248 | tf_op jit(solution)/shard_map/ppermute | solution.py:189
  154.9 1.9 collective-permute-start.4
  156.8 8.0 %collective-permute-start = (s32[1,256]{1,0:T(1,128)S(1)}, s32[1,256]{1,0:T(1,128)S(1)}, u32[]{:S(2)}, u32[]{:S(2)}) collective-permute-start(s32[1,256]{1,0:T(1,128)S(1)} %copy-done.5), channel_id=1, source_target_pairs={{0,16},{16,0},{1,17},{17,1},{2,18},{18,2},{3,19},{19,3},{4,20},{20... | collective-permute-start | bytes 3080 | tf_op jit(solution)/shard_map/ppermute | solution.py:236
  165.7 2.2 %collective-permute-done.4.second_ref = bf16[192,2048]{1,0:T(8,128)(2,1)S(1)} collective-permute-done((bf16[192,2048]{1,0:T(8,128)(2,1)S(1)}, bf16[192,2048]{1,0:T(8,128)(2,1)S(1)}, u32[]{:S(2)}, u32[]{:S(2)}) %collective-permute-start.4) | collective-permute-done | bytes 786464 | tf_op jit(solution)/shard_map/ppermute | solution.py:189
  167.9 3.0 %shard_map.100 = bf16[32,32,384]{2,1,0:T(8,128)(2,1)} custom-call(s32[33]{0:T(128)S(1)} %pad_add_fusion.ord_ref, s32[2,256]{1,0:T(2,128)S(1)} %add_select_fusion.idx_ref, bf16[192,2048]{1,0:T(8,128)(2,1)S(1)} %shard_map.94.first_ref, bf16[192,2048]{1,0:T(8,128)(2,1)S(1)} %collective-permute-done.4.second_ref, ...), custom_call_target="tpu_custom_call" | custom-call | flops 805306368 | tf_op jit(solution)/shard_map/pallas_call | solution.py:285
  171.0 19.0 %all-to-all-start.4 = ((bf16[32,32,384]{2,1,0:T(8,128)(2,1)}), bf16[32,32,384]{2,1,0:T(8,128)(2,1)S(1)}, u32[]{:S(2)}, u32[]{:S(2)}) async-start(bf16[32,32,384]{2,1,0:T(8,128)(2,1)} %shard_map.100), calls=%async_computation.4 | async-start | bytes 1572864 | tf_op jit(solution)/shard_map/all_to_all | solution.py:292
  190.8 20.9 %all-to-all-done.4.in_ref = bf16[32,32,384]{2,1,0:T(8,128)(2,1)S(1)} async-done(((bf16[32,32,384]{2,1,0:T(8,128)(2,1)}), bf16[32,32,384]{2,1,0:T(8,128)(2,1)S(1)}, u32[]{:S(2)}, u32[]{:S(2)}) %all-to-all-start.4) | async-done | bytes 786464 | tf_op jit(solution)/shard_map/all_to_all | solution.py:292
  211.8 1.6 shard_map.101
  (39 shorter events, 7.7 us)
Async XLA Ops:
  0.8 1.9 copy-start
  2.7 10.1 %copy-start.3 = (bf16[96,512]{1,0:T(8,128)(2,1)S(1)}, bf16[96,512]{1,0:T(8,128)(2,1)}, u32[]{:S(2)}) copy-start(bf16[96,512]{1,0:T(8,128)(2,1)} %param.13) | copy-start | bytes 294916
  2.7 10.1 %copy-start.4 = (bf16[96,512]{1,0:T(8,128)(2,1)S(1)}, bf16[96,512]{1,0:T(8,128)(2,1)}, u32[]{:S(2)}) copy-start(bf16[96,512]{1,0:T(8,128)(2,1)} %param.14) | copy-start | bytes 294916
  4.1 93.3 %collective-permute-start.5 = (bf16[16,256,256]{2,1,0:T(8,128)(2,1)S(1)}, bf16[16,256,256]{2,1,0:T(8,128)(2,1)}, u32[]{:S(2)}, u32[]{:S(2)}) collective-permute-start(bf16[16,256,256]{2,1,0:T(8,128)(2,1)S(1)} %shard_map.95.own_ref), channel_id=1, source_target_pairs={{0,16},{16,0},{1,17},{17,1},{2,18},{18,2},{3,19},{19,3},{4,20},{20... | collective-permute-start | bytes 6291464 | tf_op jit(solution)/shard_map/ppermute | solution.py:235
  16.7 13.8 %collective-permute-start.6 = (bf16[192,512]{1,0:T(8,128)(2,1)S(1)}, bf16[192,512]{1,0:T(8,128)(2,1)S(1)}, u32[]{:S(2)}, u32[]{:S(2)}) collective-permute-start(bf16[192,512]{1,0:T(8,128)(2,1)S(1)} %bitcast.10), channel_id=1, source_target_pairs={{0,128},{16,400},{128,0},{144,272},{256,384},{272,144},{384,256},{... | collective-permute-start | bytes 589832 | tf_op jit(solution)/shard_map/ppermute | solution.py:189
  30.6 60.0 %copy-start.6 = (s32[4]{0:T(128)S(1)}, s32[4]{0:T(128)}, u32[]{:S(2)}) copy-start(s32[4]{0:T(128)} %constant.38.clone) | copy-start | bytes 52
  30.6 60.0 %copy-start.7 = (s32[4]{0:T(128)S(1)}, s32[4]{0:T(128)}, u32[]{:S(2)}) copy-start(s32[4]{0:T(128)} %constant.39.clone) | copy-start | bytes 52
  30.6 21.2 %collective-permute-start.10 = (bf16[384,512]{1,0:T(8,128)(2,1)S(1)}, bf16[384,512]{1,0:T(8,128)(2,1)S(1)}, u32[]{:S(2)}, u32[]{:S(2)}) collective-permute-start(bf16[384,512]{1,0:T(8,128)(2,1)S(1)} %shard_map.96.rest_0_), channel_id=1, source_target_pairs={{0,384},{16,144},{128,256},{144,16},{256,128},{272,400},{384,0},{4... | collective-permute-start | bytes 1179656 | tf_op jit(solution)/shard_map/ppermute | solution.py:189
  53.0 48.9 %all-to-all-start.2 = ((bf16[4,384,512]{2,1,0:T(8,128)(2,1)}), bf16[4,384,512]{2,1,0:T(8,128)(2,1)}, u32[]{:S(2)}, u32[]{:S(2)}) async-start(bf16[4,384,512]{2,1,0:T(8,128)(2,1)} %shard_map.98), calls=%async_computation.2 | async-start | bytes 3145728 | tf_op jit(solution)/shard_map/all_to_all | solution.py:202
  60.9 27.8 %collective-permute-start.7 = (bf16[384,512]{1,0:T(8,128)(2,1)S(1)}, bf16[384,512]{1,0:T(8,128)(2,1)S(1)}, u32[]{:S(2)}, u32[]{:S(2)}) collective-permute-start(bf16[384,512]{1,0:T(8,128)(2,1)S(1)} %shard_map.96.rest_0_), channel_id=1, source_target_pairs={{0,32},{16,112},{32,0},{48,80},{64,96},{80,48},{96,64},{112,16},{1... | collective-permute-start | bytes 1179656 | tf_op jit(solution)/shard_map/ppermute | solution.py:189
  65.7 25.2 %collective-permute-start.8 = (bf16[384,512]{1,0:T(8,128)(2,1)S(1)}, bf16[384,512]{1,0:T(8,128)(2,1)S(1)}, u32[]{:S(2)}, u32[]{:S(2)}) collective-permute-start(bf16[384,512]{1,0:T(8,128)(2,1)S(1)} %shard_map.96.rest_0_), channel_id=1, source_target_pairs={{0,96},{16,48},{32,64},{48,16},{64,32},{80,112},{96,0},{112,80},{1... | collective-permute-start | bytes 1179656 | tf_op jit(solution)/shard_map/ppermute | solution.py:189
  88.6 8.8 %collective-permute-start.9 = (bf16[384,512]{1,0:T(8,128)(2,1)S(1)}, bf16[384,512]{1,0:T(8,128)(2,1)}, u32[]{:S(2)}, u32[]{:S(2)}) collective-permute-start(bf16[384,512]{1,0:T(8,128)(2,1)S(1)} %collective-permute-done.7.rest_1_), channel_id=1, source_target_pairs={{0,96},{16,48},{32,64},{48,16},{64,32},{80,112},{96,0},{112,80},{1... | collective-permute-start | bytes 1179656 | tf_op jit(solution)/shard_map/ppermute | solution.py:189
  101.9 8.6 %all-to-all-start = ((bf16[4,24,512]{2,1,0:T(8,128)(2,1)}), bf16[4,24,512]{2,1,0:T(8,128)(2,1)S(1)}, u32[]{:S(2)}, u32[]{:S(2)}) async-start(bf16[4,24,512]{2,1,0:T(8,128)(2,1)} %bitcast.2), calls=%async_computation | async-start | bytes 196608 | tf_op jit(solution)/shard_map/all_to_all | solution.py:223
  110.5 46.3 %copy-start.5 = (s32[1,256]{1,0:T(1,128)S(1)}, s32[1,256]{1,0:T(1,128)}, u32[]{:S(2)}) copy-start(s32[1,256]{1,0:T(1,128)} %param.12) | copy-start | bytes 3076
  110.5 34.9 %all-to-all-start.3 = ((bf16[4,512,256]{2,1,0:T(8,128)(2,1)}), bf16[4,512,256]{2,1,0:T(8,128)(2,1)S(1)}, u32[]{:S(2)}, u32[]{:S(2)}) async-start(bf16[4,512,256]{2,1,0:T(8,128)(2,1)} %shard_map.99), calls=%async_computation.3 | async-start | bytes 2097152 | tf_op jit(solution)/shard_map/all_to_all | solution.py:282
  114.8 9.4 %collective-permute-start.1 = (bf16[24,2048]{1,0:T(8,128)(2,1)S(1)}, bf16[24,2048]{1,0:T(8,128)(2,1)S(1)}, u32[]{:S(2)}, u32[]{:S(2)}) collective-permute-start(bf16[24,2048]{1,0:T(8,128)(2,1)S(1)} %shard_map.91.a_ref), channel_id=1, source_target_pairs={{0,128},{16,400},{128,0},{144,272},{256,384},{272,144},{384,256},{... | collective-permute-start | bytes 294920 | tf_op jit(solution)/shard_map/ppermute | solution.py:189
  124.2 17.5 %collective-permute-start.2 = (bf16[48,2048]{1,0:T(8,128)(2,1)S(1)}, bf16[48,2048]{1,0:T(8,128)(2,1)S(1)}, u32[]{:S(2)}, u32[]{:S(2)}) collective-permute-start(bf16[48,2048]{1,0:T(8,128)(2,1)S(1)} %shard_map.92.a_ref), channel_id=1, source_target_pairs={{0,384},{16,144},{128,256},{144,16},{256,128},{272,400},{384,0},{4... | collective-permute-start | bytes 589832 | tf_op jit(solution)/shard_map/ppermute | solution.py:189
  141.7 0.7 copy-start.2
  143.4 9.7 %collective-permute-start.3 = (bf16[96,2048]{1,0:T(8,128)(2,1)S(1)}, bf16[96,2048]{1,0:T(8,128)(2,1)S(1)}, u32[]{:S(2)}, u32[]{:S(2)}) collective-permute-start(bf16[96,2048]{1,0:T(8,128)(2,1)S(1)} %shard_map.93.a_ref), channel_id=1, source_target_pairs={{0,32},{16,112},{32,0},{48,80},{64,96},{80,48},{96,64},{112,16},{1... | collective-permute-start | bytes 1179656 | tf_op jit(solution)/shard_map/ppermute | solution.py:189
  145.4 22.5 %collective-permute-start.11 = (bf16[4,512,256]{2,1,0:T(8,128)(2,1)S(1)}, bf16[4,512,256]{2,1,0:T(8,128)(2,1)S(1)}, u32[]{:S(2)}, u32[]{:S(2)}) collective-permute-start(bf16[4,512,256]{2,1,0:T(8,128)(2,1)S(1)} %all-to-all-done.3.hid_ref), channel_id=1, source_target_pairs={{0,16},{16,0},{1,17},{17,1},{2,18},{18,2},{3,19},{19,3},{4,20},{20... | collective-permute-start | bytes 3145736 | tf_op jit(solution)/shard_map/ppermute | solution.py:283
  153.1 0.8 copy-start.1
  154.9 13.0 %collective-permute-start.4 = (bf16[192,2048]{1,0:T(8,128)(2,1)S(1)}, bf16[192,2048]{1,0:T(8,128)(2,1)S(1)}, u32[]{:S(2)}, u32[]{:S(2)}) collective-permute-start(bf16[192,2048]{1,0:T(8,128)(2,1)S(1)} %shard_map.94.first_ref), channel_id=1, source_target_pairs={{0,96},{16,48},{32,64},{48,16},{64,32},{80,112},{96,0},{112,80},{1... | collective-permute-start | bytes 2359304 | tf_op jit(solution)/shard_map/ppermute | solution.py:189
  156.8 8.8 %collective-permute-start = (s32[1,256]{1,0:T(1,128)S(1)}, s32[1,256]{1,0:T(1,128)S(1)}, u32[]{:S(2)}, u32[]{:S(2)}) collective-permute-start(s32[1,256]{1,0:T(1,128)S(1)} %copy-done.5), channel_id=1, source_target_pairs={{0,16},{16,0},{1,17},{17,1},{2,18},{18,2},{3,19},{19,3},{4,20},{20... | collective-permute-start | bytes 3080 | tf_op jit(solution)/shard_map/ppermute | solution.py:236
  171.0 40.8 %all-to-all-start.4 = ((bf16[32,32,384]{2,1,0:T(8,128)(2,1)}), bf16[32,32,384]{2,1,0:T(8,128)(2,1)S(1)}, u32[]{:S(2)}, u32[]{:S(2)}) async-start(bf16[32,32,384]{2,1,0:T(8,128)(2,1)} %shard_map.100), calls=%async_computation.4 | async-start | bytes 1572864 | tf_op jit(solution)/shard_map/all_to_all | solution.py:292
